TPU v7x, 8 devices: a whole 2x2x1 slice. The times are simulated.
8 devices in a mesh: dp: 2 (over z, y), tp: 4 (over x, core).
Axes of the slice: x: 2, y: 2, z: 1, core: 2. Of those that a mesh axis runs over, the one named last changes fastest.
Arguments:
- x_in: float32 [8, 128, 2048], P('dp', 'tp'), parts along dimension 0
- d_out: bfloat16 [8, 128, 2048], P('dp', 'tp'), parts along dimension 0
- lengths: int32 [8], P('dp'), parts along dimension 0
- w_qkv: bfloat16 [4, 2048, 3, 32, 64], P(None, None, None, 'tp')
- w_out: bfloat16 [4, 32, 64, 2048], P(None, 'tp')
- w_up: bfloat16 [4, 2048, 8192], P(None, None, 'tp')
- b_up: float32 [4, 8192], P(None, 'tp')
- w_down: bfloat16 [4, 8192, 2048], P(None, 'tp')
- vec_par: float32 [4, 6, 2048], replicated
Outputs:
- output 1: float32 [8, 128, 2048], P('dp', 'tp'), parts along dimension 0
- output 2: float32 [8, 128, 2048], P('dp', 'tp'), parts along dimension 0
- output 3: bfloat16 [8, 2048, 3, 32, 64], P('dp', None, None, 'tp'), parts along dimension 0
- output 4: bfloat16 [8, 32, 64, 2048], P('dp', 'tp'), parts along dimension 0
- output 5: bfloat16 [8, 2048, 8192], P('dp', None, 'tp'), parts along dimension 0
- output 6: float32 [8, 8192], P('dp', 'tp'), parts along dimension 0
- output 7: bfloat16 [8, 8192, 2048], P('dp', 'tp'), parts along dimension 0
- output 8: float32 [8, 6, 2048], P('dp'), parts along dimension 0
There are 2 independent parts. A program takes and returns all parts, laid end to end along the dimension named above; an argument that names none is the same for every part.
All inputs are finite; a program needn't handle non-finite values.
Results may differ from a plain program's by a relative error of at most 0.02.
Values are sent between devices in bfloat16 or wider.
A program may use at most 1 GiB of HBM per device.

v0:
```python
import jax
import jax.numpy as jnp
from jax import lax
from jax.sharding import PartitionSpec as P

TENSOR_AXIS = 'tp'
PARTS_AXIS = 'dp'


def layer_norm(x_val, gain_vec, shift_vec):
    row_mean = jnp.mean(x_val, axis=-1, keepdims=True)
    centered = x_val - row_mean
    row_var = jnp.mean(centered * centered, axis=-1, keepdims=True)
    return centered * lax.rsqrt(row_var + 1e-5) * gain_vec + shift_vec


def gelu_tanh(pre_act):
    return jax.nn.gelu(pre_act, approximate=True)


def visible_mask(lengths, seq_len):
    positions = jnp.arange(seq_len)
    causal = positions[None, :] <= positions[:, None]
    return causal[None, None] & (positions[None, None, None, :] < lengths[:, None, None, None])


def attention_fwd(q_all, k_all, v_all, lengths):
    score_scale = q_all.shape[3] ** -0.5
    scores = jnp.einsum('bhqe,bhke->bhqk', q_all, k_all, preferred_element_type=jnp.float32) * score_scale
    attn_prob = jax.nn.softmax(jnp.where(visible_mask(lengths, q_all.shape[2]), scores, -1e30), axis=-1)
    context = jnp.einsum('bhqk,bhke->bhqe', attn_prob.astype(jnp.bfloat16), v_all, preferred_element_type=jnp.float32)
    return context.astype(jnp.bfloat16), attn_prob


def attention_bwd(d_ctx, q_all, k_all, v_all, attn_prob):
    score_scale = q_all.shape[3] ** -0.5
    d_prob = jnp.einsum('bhqe,bhke->bhqk', d_ctx, v_all, preferred_element_type=jnp.float32).astype(jnp.bfloat16).astype(jnp.float32)
    d_v = jnp.einsum('bhqk,bhqe->bhke', attn_prob.astype(jnp.bfloat16), d_ctx, preferred_element_type=jnp.float32).astype(jnp.bfloat16)
    d_score = attn_prob * (d_prob - jnp.sum(d_prob * attn_prob, axis=-1, keepdims=True))
    d_score = (d_score * score_scale).astype(jnp.bfloat16)
    d_q = jnp.einsum('bhqk,bhke->bhqe', d_score, k_all, preferred_element_type=jnp.float32).astype(jnp.bfloat16)
    d_k = jnp.einsum('bhqk,bhqe->bhke', d_score, q_all, preferred_element_type=jnp.float32).astype(jnp.bfloat16)
    return jnp.stack([d_q, d_k, d_v])


def layer_fwd(x_cur, lengths, weights, vec_layer):
    w_qkv, w_out, w_up, b_up, w_down = weights
    a_shard = layer_norm(x_cur, vec_layer[0], vec_layer[1]).astype(jnp.bfloat16)
    a_full = lax.all_gather(a_shard, TENSOR_AXIS, axis=1, tiled=True)
    qkv_all = jnp.einsum('bsd,dthe->tbhse', a_full, w_qkv, preferred_element_type=jnp.float32).astype(jnp.bfloat16)
    context, attn_prob = attention_fwd(qkv_all[0], qkv_all[1], qkv_all[2], lengths)
    attn_part = jnp.einsum('bhse,hed->bsd', context, w_out, preferred_element_type=jnp.float32).astype(jnp.bfloat16)
    attn_shard = lax.psum_scatter(attn_part, TENSOR_AXIS, scatter_dimension=1, tiled=True)
    hidden = x_cur + attn_shard.astype(jnp.float32) + vec_layer[4]
    m_shard = layer_norm(hidden, vec_layer[2], vec_layer[3]).astype(jnp.bfloat16)
    m_full = lax.all_gather(m_shard, TENSOR_AXIS, axis=1, tiled=True)
    pre_act = jnp.einsum('bsd,df->bsf', m_full, w_up, preferred_element_type=jnp.float32) + b_up
    act_bf = gelu_tanh(pre_act).astype(jnp.bfloat16)
    mlp_part = jnp.einsum('bsf,fd->bsd', act_bf, w_down, preferred_element_type=jnp.float32).astype(jnp.bfloat16)
    mlp_shard = lax.psum_scatter(mlp_part, TENSOR_AXIS, scatter_dimension=1, tiled=True)
    x_next = hidden + mlp_shard.astype(jnp.float32) + vec_layer[5]
    return x_next, (x_cur, a_full, qkv_all, context, attn_prob, hidden, m_full, pre_act, act_bf)


def layer_bwd(d_cur, residues, weights, vec_layer):
    w_qkv, w_out, w_up, w_down = weights[0], weights[1], weights[2], weights[4]
    x_prev, a_full, qkv_all, context, attn_prob, hidden, m_full, pre_act, act_bf = residues
    d_mlp = lax.all_gather(d_cur.astype(jnp.bfloat16), TENSOR_AXIS, axis=1, tiled=True)
    d_act = jnp.einsum('bsd,fd->bsf', d_mlp, w_down, preferred_element_type=jnp.float32).astype(jnp.bfloat16)
    g_down = jnp.einsum('bsf,bsd->fd', act_bf, d_mlp, preferred_element_type=jnp.float32).astype(jnp.bfloat16)
    d_pre = jax.vjp(gelu_tanh, pre_act)[1](d_act.astype(jnp.float32))[0]
    d_pre_bf = d_pre.astype(jnp.bfloat16)
    g_up = jnp.einsum('bsd,bsf->df', m_full, d_pre_bf, preferred_element_type=jnp.float32).astype(jnp.bfloat16)
    g_bup = jnp.sum(d_pre, axis=(0, 1))
    d_mid_part = jnp.einsum('bsf,df->bsd', d_pre_bf, w_up, preferred_element_type=jnp.float32).astype(jnp.bfloat16)
    d_mid = lax.psum_scatter(d_mid_part, TENSOR_AXIS, scatter_dimension=1, tiled=True)
    d_hid_ln, d_gain2, d_shift2 = jax.vjp(layer_norm, hidden, vec_layer[2], vec_layer[3])[1](d_mid.astype(jnp.float32))
    d_hid = d_cur + d_hid_ln
    d_attn = lax.all_gather(d_hid.astype(jnp.bfloat16), TENSOR_AXIS, axis=1, tiled=True)
    d_ctx = jnp.einsum('bsd,hed->bhse', d_attn, w_out, preferred_element_type=jnp.float32).astype(jnp.bfloat16)
    g_out = jnp.einsum('bhse,bsd->hed', context, d_attn, preferred_element_type=jnp.float32).astype(jnp.bfloat16)
    d_qkv = attention_bwd(d_ctx, qkv_all[0], qkv_all[1], qkv_all[2], attn_prob)
    g_qkv = jnp.einsum('bsd,tbhse->dthe', a_full, d_qkv, preferred_element_type=jnp.float32).astype(jnp.bfloat16)
    d_in_part = jnp.einsum('tbhse,dthe->bsd', d_qkv, w_qkv, preferred_element_type=jnp.float32).astype(jnp.bfloat16)
    d_in = lax.psum_scatter(d_in_part, TENSOR_AXIS, scatter_dimension=1, tiled=True)
    d_x_ln, d_gain1, d_shift1 = jax.vjp(layer_norm, x_prev, vec_layer[0], vec_layer[1])[1](d_in.astype(jnp.float32))
    g_vec = jnp.stack([d_gain1, d_shift1, d_gain2, d_shift2, jnp.sum(d_hid, axis=(0, 1)), jnp.sum(d_cur, axis=(0, 1))])
    return d_hid + d_x_ln, (g_qkv, g_out, g_up, g_bup, g_down, g_vec)


def group_body(x_loc, dy_loc, len_loc, wqkv_loc, wout_loc, wup_loc, bup_loc, wdown_loc, vec_loc):
    n_layers = wqkv_loc.shape[0]
    saved_acts = []
    x_cur = x_loc
    for layer_idx in range(n_layers):
        weights = (wqkv_loc[layer_idx], wout_loc[layer_idx], wup_loc[layer_idx], bup_loc[layer_idx], wdown_loc[layer_idx])
        x_cur, residues = layer_fwd(x_cur, len_loc, weights, vec_loc[layer_idx])
        saved_acts.append(residues)
    d_cur = dy_loc.astype(jnp.float32)
    layer_grads = [None] * n_layers
    for layer_idx in reversed(range(n_layers)):
        weights = (wqkv_loc[layer_idx], wout_loc[layer_idx], wup_loc[layer_idx], bup_loc[layer_idx], wdown_loc[layer_idx])
        d_cur, grad_set = layer_bwd(d_cur, saved_acts[layer_idx], weights, vec_loc[layer_idx])
        layer_grads[layer_idx] = grad_set
    stacked = [jnp.stack([grad_set[grad_pos] for grad_set in layer_grads]) for grad_pos in range(6)]
    g_vec = lax.psum(stacked[5], TENSOR_AXIS)
    return x_cur, d_cur, stacked[0], stacked[1], stacked[2], stacked[3], stacked[4], g_vec


def solution(mesh):
    act_spec = P(PARTS_AXIS, TENSOR_AXIS, None)
    in_specs = (act_spec, act_spec, P(PARTS_AXIS), P(None, None, None, TENSOR_AXIS, None), P(None, TENSOR_AXIS, None, None), P(None, None, TENSOR_AXIS), P(None, TENSOR_AXIS), P(None, TENSOR_AXIS, None), P())
    out_specs = (act_spec, act_spec, P(PARTS_AXIS, None, None, TENSOR_AXIS, None), P(PARTS_AXIS, TENSOR_AXIS, None, None), P(PARTS_AXIS, None, TENSOR_AXIS), P(PARTS_AXIS, TENSOR_AXIS), P(PARTS_AXIS, TENSOR_AXIS, None), P(PARTS_AXIS, None, None))
    return jax.shard_map(group_body, mesh=mesh, in_specs=in_specs, out_specs=out_specs, check_vma=False)
```

profile of v0, /device:TPU:0, one launch (start us, length us, event | category | flops | bytes accessed | tf_op | source)
XLA Modules:
  0.0 1194.0 jit_solution(10042829640024848201)
XLA Ops:
  12.5 22.2 %all-gather.17.cloned.1.call-done = bf16[4,128,2048]{2,1,0:T(8,128)(2,1)} async-done(((bf16[4,32,2048]{2,1,0:T(8,128)(2,1)}), bf16[4,128,2048]{2,1,0:T(8,128)(2,1)}) %all-gather.17.cloned.1.call-update) | async-done | bytes 2097168 | tf_op jit(solution)/shard_map/all_gather | solution.py:49
  54.1 24.1 %reduce-scatter.17.cloned.1.call-done = bf16[4,32,2048]{2,1,0:T(8,128)(2,1)} async-done(((bf16[4,128,2048]{2,1,0:T(8,128)(2,1)}), bf16[4,32,2048]{2,1,0:T(8,128)(2,1)}) %reduce-scatter.17.cloned.1.call-update) | async-done | bytes 524304 | tf_op jit(solution)/shard_map/reduce_scatter | solution.py:53
  80.9 19.6 %all-gather.19.cloned.1.call-done = bf16[4,128,2048]{2,1,0:T(8,128)(2,1)} async-done(((bf16[4,32,2048]{2,1,0:T(8,128)(2,1)}), bf16[4,128,2048]{2,1,0:T(8,128)(2,1)}) %all-gather.19.cloned.1.call-update) | async-done | bytes 2097168 | tf_op jit(solution)/shard_map/all_gather | solution.py:56
  119.8 25.6 %reduce-scatter.19.cloned.1.call-done = bf16[4,32,2048]{2,1,0:T(8,128)(2,1)} async-done(((bf16[4,128,2048]{2,1,0:T(8,128)(2,1)}), bf16[4,32,2048]{2,1,0:T(8,128)(2,1)}) %reduce-scatter.19.cloned.1.call-update) | async-done | bytes 524304 | tf_op jit(solution)/shard_map/reduce_scatter | solution.py:60
  148.6 19.2 %all-gather.21.cloned.1.call-done = bf16[4,128,2048]{2,1,0:T(8,128)(2,1)} async-done(((bf16[4,32,2048]{2,1,0:T(8,128)(2,1)}), bf16[4,128,2048]{2,1,0:T(8,128)(2,1)}) %all-gather.21.cloned.1.call-update) | async-done | bytes 2097168 | tf_op jit(solution)/shard_map/all_gather | solution.py:49
  185.6 25.6 %reduce-scatter.21.cloned.1.call-done = bf16[4,32,2048]{2,1,0:T(8,128)(2,1)} async-done(((bf16[4,128,2048]{2,1,0:T(8,128)(2,1)}), bf16[4,32,2048]{2,1,0:T(8,128)(2,1)}) %reduce-scatter.21.cloned.1.call-update) | async-done | bytes 524304 | tf_op jit(solution)/shard_map/reduce_scatter | solution.py:53
  213.9 19.6 %all-gather.23.cloned.1.call-done = bf16[4,128,2048]{2,1,0:T(8,128)(2,1)} async-done(((bf16[4,32,2048]{2,1,0:T(8,128)(2,1)}), bf16[4,128,2048]{2,1,0:T(8,128)(2,1)}) %all-gather.23.cloned.1.call-update) | async-done | bytes 2097168 | tf_op jit(solution)/shard_map/all_gather | solution.py:56
  253.0 25.6 %reduce-scatter.23.cloned.1.call-done = bf16[4,32,2048]{2,1,0:T(8,128)(2,1)} async-done(((bf16[4,128,2048]{2,1,0:T(8,128)(2,1)}), bf16[4,32,2048]{2,1,0:T(8,128)(2,1)}) %reduce-scatter.23.cloned.1.call-update) | async-done | bytes 524304 | tf_op jit(solution)/shard_map/reduce_scatter | solution.py:60
  281.5 19.5 %all-gather.25.cloned.1.call-done = bf16[4,128,2048]{2,1,0:T(8,128)(2,1)} async-done(((bf16[4,32,2048]{2,1,0:T(8,128)(2,1)}), bf16[4,128,2048]{2,1,0:T(8,128)(2,1)}) %all-gather.25.cloned.1.call-update) | async-done | bytes 2097168 | tf_op jit(solution)/shard_map/all_gather | solution.py:49
  316.6 25.6 %reduce-scatter.25.cloned.1.call-done = bf16[4,32,2048]{2,1,0:T(8,128)(2,1)} async-done(((bf16[4,128,2048]{2,1,0:T(8,128)(2,1)}), bf16[4,32,2048]{2,1,0:T(8,128)(2,1)}) %reduce-scatter.25.cloned.1.call-update) | async-done | bytes 524304 | tf_op jit(solution)/shard_map/reduce_scatter | solution.py:53
  344.8 19.6 %all-gather.27.cloned.1.call-done = bf16[4,128,2048]{2,1,0:T(8,128)(2,1)} async-done(((bf16[4,32,2048]{2,1,0:T(8,128)(2,1)}), bf16[4,128,2048]{2,1,0:T(8,128)(2,1)}) %all-gather.27.cloned.1.call-update) | async-done | bytes 2097168 | tf_op jit(solution)/shard_map/all_gather | solution.py:56
  383.8 25.6 %reduce-scatter.27.cloned.1.call-done = bf16[4,32,2048]{2,1,0:T(8,128)(2,1)} async-done(((bf16[4,128,2048]{2,1,0:T(8,128)(2,1)}), bf16[4,32,2048]{2,1,0:T(8,128)(2,1)}) %reduce-scatter.27.cloned.1.call-update) | async-done | bytes 524304 | tf_op jit(solution)/shard_map/reduce_scatter | solution.py:60
  412.1 19.6 %all-gather.29.cloned.1.call-done = bf16[4,128,2048]{2,1,0:T(8,128)(2,1)} async-done(((bf16[4,32,2048]{2,1,0:T(8,128)(2,1)}), bf16[4,128,2048]{2,1,0:T(8,128)(2,1)}) %all-gather.29.cloned.1.call-update) | async-done | bytes 2097168 | tf_op jit(solution)/shard_map/all_gather | solution.py:49
  449.7 25.6 %reduce-scatter.29.cloned.1.call-done = bf16[4,32,2048]{2,1,0:T(8,128)(2,1)} async-done(((bf16[4,128,2048]{2,1,0:T(8,128)(2,1)}), bf16[4,32,2048]{2,1,0:T(8,128)(2,1)}) %reduce-scatter.29.cloned.1.call-update) | async-done | bytes 524304 | tf_op jit(solution)/shard_map/reduce_scatter | solution.py:53
  479.4 18.9 %all-gather.31.cloned.1.call-done = bf16[4,128,2048]{2,1,0:T(8,128)(2,1)} async-done(((bf16[4,32,2048]{2,1,0:T(8,128)(2,1)}), bf16[4,128,2048]{2,1,0:T(8,128)(2,1)}) %all-gather.31.cloned.1.call-update) | async-done | bytes 2097168 | tf_op jit(solution)/shard_map/all_gather | solution.py:56
  519.2 11.2 fusion.489
  541.0 11.0 fusion.166
  552.4 14.1 %reduce-scatter.33.cloned.1.call-done = bf16[4,32,2048]{2,1,0:T(8,128)(2,1)} async-done(((bf16[4,128,2048]{2,1,0:T(8,128)(2,1)}), bf16[4,32,2048]{2,1,0:T(8,128)(2,1)}) %reduce-scatter.33.cloned.1.call-update) | async-done | bytes 524304 | tf_op jit(solution)/shard_map/reduce_scatter | solution.py:76
  571.2 23.2 %reduce-scatter.31.cloned.1.call-done = bf16[4,32,2048]{2,1,0:T(8,128)(2,1)} async-done(((bf16[4,128,2048]{2,1,0:T(8,128)(2,1)}), bf16[4,32,2048]{2,1,0:T(8,128)(2,1)}) %reduce-scatter.31.cloned.1.call-update) | async-done | bytes 524304 | tf_op jit(solution)/shard_map/reduce_scatter | solution.py:60
  600.3 19.6 %all-gather.35.cloned.1.call-done = bf16[4,128,2048]{2,1,0:T(8,128)(2,1)} async-done(((bf16[4,32,2048]{2,1,0:T(8,128)(2,1)}), bf16[4,128,2048]{2,1,0:T(8,128)(2,1)}) %all-gather.35.cloned.1.call-update) | async-done | bytes 2097168 | tf_op jit(solution)/shard_map/all_gather | solution.py:79
  647.2 25.6 %reduce-scatter.35.cloned.1.call-done = bf16[4,32,2048]{2,1,0:T(8,128)(2,1)} async-done(((bf16[4,128,2048]{2,1,0:T(8,128)(2,1)}), bf16[4,32,2048]{2,1,0:T(8,128)(2,1)}) %reduce-scatter.35.cloned.1.call-update) | async-done | bytes 524304 | tf_op jit(solution)/shard_map/reduce_scatter | solution.py:85
  680.3 19.5 %all-gather.37.cloned.1.call-done = bf16[4,128,2048]{2,1,0:T(8,128)(2,1)} async-done(((bf16[4,32,2048]{2,1,0:T(8,128)(2,1)}), bf16[4,128,2048]{2,1,0:T(8,128)(2,1)}) %all-gather.37.cloned.1.call-update) | async-done | bytes 2097168 | tf_op jit(solution)/shard_map/all_gather | solution.py:68
  699.8 11.2 fusion.490
  721.6 25.6 %reduce-scatter.37.cloned.1.call-done = bf16[4,32,2048]{2,1,0:T(8,128)(2,1)} async-done(((bf16[4,128,2048]{2,1,0:T(8,128)(2,1)}), bf16[4,32,2048]{2,1,0:T(8,128)(2,1)}) %reduce-scatter.37.cloned.1.call-update) | async-done | bytes 524304 | tf_op jit(solution)/shard_map/reduce_scatter | solution.py:76
  754.7 19.6 %all-gather.39.cloned.1.call-done = bf16[4,128,2048]{2,1,0:T(8,128)(2,1)} async-done(((bf16[4,32,2048]{2,1,0:T(8,128)(2,1)}), bf16[4,128,2048]{2,1,0:T(8,128)(2,1)}) %all-gather.39.cloned.1.call-update) | async-done | bytes 2097168 | tf_op jit(solution)/shard_map/all_gather | solution.py:79
  799.5 25.4 %reduce-scatter.39.cloned.1.call-done = bf16[4,32,2048]{2,1,0:T(8,128)(2,1)} async-done(((bf16[4,128,2048]{2,1,0:T(8,128)(2,1)}), bf16[4,32,2048]{2,1,0:T(8,128)(2,1)}) %reduce-scatter.39.cloned.1.call-update) | async-done | bytes 524304 | tf_op jit(solution)/shard_map/reduce_scatter | solution.py:85
  831.2 19.6 %all-gather.41.cloned.1.call-done = bf16[4,128,2048]{2,1,0:T(8,128)(2,1)} async-done(((bf16[4,32,2048]{2,1,0:T(8,128)(2,1)}), bf16[4,128,2048]{2,1,0:T(8,128)(2,1)}) %all-gather.41.cloned.1.call-update) | async-done | bytes 2097168 | tf_op jit(solution)/shard_map/all_gather | solution.py:68
  850.8 11.2 fusion.491
  872.6 25.6 %reduce-scatter.41.cloned.1.call-done = bf16[4,32,2048]{2,1,0:T(8,128)(2,1)} async-done(((bf16[4,128,2048]{2,1,0:T(8,128)(2,1)}), bf16[4,32,2048]{2,1,0:T(8,128)(2,1)}) %reduce-scatter.41.cloned.1.call-update) | async-done | bytes 524304 | tf_op jit(solution)/shard_map/reduce_scatter | solution.py:76
  1006.5 10.6 fusion.492
  1061.3 43.5 %pad_maximum_fusion = (bf16[4,2048,2048]{2,1,0:T(8,128)(2,1)}, bf16[4,2048,2048]{2,1,0:T(8,128)(2,1)}) fusion(bf16[1,2048,2048]{2,1,0:T(8,128)(2,1)} %fusion.59, bf16[1,2048,2048]{2,1,0:T(8,128)(2,1)} %fusion.58, bf16[1,2048,2048]{2,1,0:T(8,128)(2,1)} %fusion.57, bf16[1,2048,2048]{2,1,0:T(8,128)(2,1)} %fusion.56, bf16[1,2048,2048]{2,1,0:T(8,128)(2,1)} %fusion.63, ...), kind=kLoop, calls=%fused_computation.8 | loop fusion | flops 100663296 | bytes 134217728 | tf_op jit(solution)/shard_map/stack | solution.py:105
  1159.9 25.4 %all-reduce.2.cloned.1.call-done = f32[4,6,2048]{2,1,0:T(8,128)} async-done(((f32[4,6,2048]{2,1,0:T(8,128)}), f32[4,6,2048]{2,1,0:T(8,128)}) %all-reduce.2.cloned.1.call-update) | async-done | bytes 196624 | tf_op jit(solution)/shard_map/psum | solution.py:106
  (573 shorter events, 499.5 us)
Async XLA Ops:
  12.2 65.9 %reduce-scatter.17.cloned.1.call-start = ((), (), s32[]{:S(2)}) async-start(), calls=%async_computation.17 | async-start | bytes 2621440 | tf_op jit(solution)/shard_map/reduce_scatter | solution.py:53
  52.4 48.0 %all-gather.19.cloned.1.call-start = ((), (), s32[]{:S(2)}) async-start(), calls=%async_computation.18 | async-start | bytes 2621440 | tf_op jit(solution)/shard_map/all_gather | solution.py:56
  80.8 64.7 %reduce-scatter.19.cloned.1.call-start = ((), (), s32[]{:S(2)}) async-start(), calls=%async_computation.19 | async-start | bytes 2621440 | tf_op jit(solution)/shard_map/reduce_scatter | solution.py:60
  119.7 48.0 %all-gather.21.cloned.1.call-start = ((), (), s32[]{:S(2)}) async-start(), calls=%async_computation.20 | async-start | bytes 2621440 | tf_op jit(solution)/shard_map/all_gather | solution.py:49
  148.1 63.2 %reduce-scatter.21.cloned.1.call-start = ((), (), s32[]{:S(2)}) async-start(), calls=%async_computation.21 | async-start | bytes 2621440 | tf_op jit(solution)/shard_map/reduce_scatter | solution.py:53
  185.6 48.0 %all-gather.23.cloned.1.call-start = ((), (), s32[]{:S(2)}) async-start(), calls=%async_computation.22 | async-start | bytes 2621440 | tf_op jit(solution)/shard_map/all_gather | solution.py:56
  213.9 64.7 %reduce-scatter.23.cloned.1.call-start = ((), (), s32[]{:S(2)}) async-start(), calls=%async_computation.23 | async-start | bytes 2621440 | tf_op jit(solution)/shard_map/reduce_scatter | solution.py:60
  252.9 48.0 %all-gather.25.cloned.1.call-start = ((), (), s32[]{:S(2)}) async-start(), calls=%async_computation.24 | async-start | bytes 2621440 | tf_op jit(solution)/shard_map/all_gather | solution.py:49
  281.2 60.9 %reduce-scatter.25.cloned.1.call-start = ((), (), s32[]{:S(2)}) async-start(), calls=%async_computation.25 | async-start | bytes 2621440 | tf_op jit(solution)/shard_map/reduce_scatter | solution.py:53
  316.5 48.0 %all-gather.27.cloned.1.call-start = ((), (), s32[]{:S(2)}) async-start(), calls=%async_computation.26 | async-start | bytes 2621440 | tf_op jit(solution)/shard_map/all_gather | solution.py:56
  344.8 64.7 %reduce-scatter.27.cloned.1.call-start = ((), (), s32[]{:S(2)}) async-start(), calls=%async_computation.27 | async-start | bytes 2621440 | tf_op jit(solution)/shard_map/reduce_scatter | solution.py:60
  383.8 48.0 %all-gather.29.cloned.1.call-start = ((), (), s32[]{:S(2)}) async-start(), calls=%async_computation.28 | async-start | bytes 2621440 | tf_op jit(solution)/shard_map/all_gather | solution.py:49
  412.1 63.2 %reduce-scatter.29.cloned.1.call-start = ((), (), s32[]{:S(2)}) async-start(), calls=%async_computation.29 | async-start | bytes 2621440 | tf_op jit(solution)/shard_map/reduce_scatter | solution.py:53
  449.6 48.7 %all-gather.31.cloned.1.call-start = ((), (), s32[]{:S(2)}) async-start(), calls=%async_computation.30 | async-start | bytes 2621440 | tf_op jit(solution)/shard_map/all_gather | solution.py:56
  478.6 40.6 %all-gather.33.cloned.1.call-start = ((), (), s32[]{:S(2)}) async-start(), calls=%async_computation.32 | async-start | bytes 2621440 | tf_op jit(solution)/shard_map/all_gather | solution.py:68
  479.2 87.4 %reduce-scatter.33.cloned.1.call-start = ((), (), s32[]{:S(2)}) async-start(), calls=%async_computation.33 | async-start | bytes 2621440 | tf_op jit(solution)/shard_map/reduce_scatter | solution.py:76
  540.9 53.5 %reduce-scatter.31.cloned.1.call-start = ((), (), s32[]{:S(2)}) async-start(), calls=%async_computation.31 | async-start | bytes 2621440 | tf_op jit(solution)/shard_map/reduce_scatter | solution.py:60
  552.0 68.0 %all-gather.35.cloned.1.call-start = ((), (), s32[]{:S(2)}) async-start(), calls=%async_computation.34 | async-start | bytes 2621440 | tf_op jit(solution)/shard_map/all_gather | solution.py:79
  600.3 72.5 %reduce-scatter.35.cloned.1.call-start = ((), (), s32[]{:S(2)}) async-start(), calls=%async_computation.35 | async-start | bytes 2621440 | tf_op jit(solution)/shard_map/reduce_scatter | solution.py:85
  647.1 52.7 %all-gather.37.cloned.1.call-start = ((), (), s32[]{:S(2)}) async-start(), calls=%async_computation.36 | async-start | bytes 2621440 | tf_op jit(solution)/shard_map/all_gather | solution.py:68
  680.1 67.1 %reduce-scatter.37.cloned.1.call-start = ((), (), s32[]{:S(2)}) async-start(), calls=%async_computation.37 | async-start | bytes 2621440 | tf_op jit(solution)/shard_map/reduce_scatter | solution.py:76
  721.6 52.8 %all-gather.39.cloned.1.call-start = ((), (), s32[]{:S(2)}) async-start(), calls=%async_computation.38 | async-start | bytes 2621440 | tf_op jit(solution)/shard_map/all_gather | solution.py:79
  754.7 70.2 %reduce-scatter.39.cloned.1.call-start = ((), (), s32[]{:S(2)}) async-start(), calls=%async_computation.39 | async-start | bytes 2621440 | tf_op jit(solution)/shard_map/reduce_scatter | solution.py:85
  799.2 51.6 %all-gather.41.cloned.1.call-start = ((), (), s32[]{:S(2)}) async-start(), calls=%async_computation.40 | async-start | bytes 2621440 | tf_op jit(solution)/shard_map/all_gather | solution.py:68
  831.1 67.1 %reduce-scatter.41.cloned.1.call-start = ((), (), s32[]{:S(2)}) async-start(), calls=%async_computation.41 | async-start | bytes 2621440 | tf_op jit(solution)/shard_map/reduce_scatter | solution.py:76
  872.5 55.0 %all-gather.43.cloned.1.call-start = ((), (), s32[]{:S(2)}) async-start(), calls=%async_computation.42 | async-start | bytes 2621440 | tf_op jit(solution)/shard_map/all_gather | solution.py:79
  905.4 72.7 %reduce-scatter.43.cloned.1.call-start = ((), (), s32[]{:S(2)}) async-start(), calls=%async_computation.43 | async-start | bytes 2621440 | tf_op jit(solution)/shard_map/reduce_scatter | solution.py:85
  950.6 55.8 %all-gather.45.cloned.1.call-start = ((), (), s32[]{:S(2)}) async-start(), calls=%async_computation.44 | async-start | bytes 2621440 | tf_op jit(solution)/shard_map/all_gather | solution.py:68
  983.3 73.5 %reduce-scatter.45.cloned.1.call-start = ((), (), s32[]{:S(2)}) async-start(), calls=%async_computation.45 | async-start | bytes 2621440 | tf_op jit(solution)/shard_map/reduce_scatter | solution.py:76
  1027.6 77.9 %all-gather.47.cloned.1.call-start = ((), (), s32[]{:S(2)}) async-start(), calls=%async_computation.46 | async-start | bytes 2621440 | tf_op jit(solution)/shard_map/all_gather | solution.py:79
  1061.2 93.2 %reduce-scatter.47.cloned.1.call-start = ((), (), s32[]{:S(2)}) async-start(), calls=%async_computation.47 | async-start | bytes 2621440 | tf_op jit(solution)/shard_map/reduce_scatter | solution.py:85
  1128.8 56.5 %all-reduce.2.cloned.1.call-start = ((), (), s32[]{:S(2)}) async-start(), calls=%async_computation.48 | async-start | bytes 524288 | tf_op jit(solution)/shard_map/psum | solution.py:106
  (165 other events, 2972.9 us)
Sparse Core Ops, SparseCore 0:
  12.3 22.3 all-gather.16
  52.6 25.5 reduce-scatter.16
  80.9 19.5 all-gather.18
  119.9 25.5 reduce-scatter.18
  148.2 19.5 all-gather.20
  185.7 25.5 reduce-scatter.20
  253.0 25.5 reduce-scatter.22
  281.4 19.5 all-gather.24
  316.6 25.4 reduce-scatter.24
  344.9 19.5 all-gather.26
  383.9 25.5 reduce-scatter.26
  412.2 19.5 all-gather.28
  449.7 25.5 reduce-scatter.28
  478.7 19.5 all-gather.30
  499.7 19.5 all-gather.32
  541.0 25.4 reduce-scatter.32
  568.9 25.4 reduce-scatter.30
  600.4 19.5 all-gather.34
  647.2 25.5 reduce-scatter.34
  680.2 19.5 all-gather.36
  721.7 25.4 reduce-scatter.36
  754.8 19.5 all-gather.38
  799.3 25.5 reduce-scatter.38
  831.2 19.5 all-gather.40
  872.7 25.5 reduce-scatter.40
  905.5 19.5 all-gather.42
  950.7 25.5 reduce-scatter.42
  983.3 19.5 all-gather.44
  1027.7 25.5 reduce-scatter.44
  1061.3 19.5 all-gather.46
  1128.9 25.5 reduce-scatter.46
  1158.6 26.6 all-reduce.1
  (1 shorter events, 19.5 us)
where the time goes:
time: 1200 us; the launch traced here: 1190 us
  waiting for transfers between devices  592 us (49%)
  matrix products  418 us (35%)
  other arithmetic  131 us (11%)
  local copies, waits for them, and re-layouts  33.2 us (3%)
  between operations  16.3 us (1%)
    reduce_scatter x4, waiting for transfers between devices, layer_fwd(): lax.psum_scatter(attn_part, TENSOR_AXIS, scatter_dimension=1, tiled=True)  101 us
    reduce_scatter x4, waiting for transfers between devices, layer_fwd(): lax.psum_scatter(mlp_part, TENSOR_AXIS, scatter_dimension=1, tiled=True)  100 us
    all_gather x4, waiting for transfers between devices, layer_fwd(): a_full = lax.all_gather(a_shard, TENSOR_AXIS, axis=1, tiled=True)  80.5 us
    all_gather x4, waiting for transfers between devices, layer_fwd(): m_full = lax.all_gather(m_shard, TENSOR_AXIS, axis=1, tiled=True)  77.7 us
    reduce_scatter x4, waiting for transfers between devices, layer_bwd(): lax.psum_scatter(d_mid_part, TENSOR_AXIS, scatter_dimension=1, tiled=True)  65.3 us
    another operation x5, other arithmetic, group_body(): jnp.stack([grad_set[grad_pos] for grad_set in layer_grads])  59.5 us
    reduce_scatter x4, waiting for transfers between devices, layer_bwd(): lax.psum_scatter(d_in_part, TENSOR_AXIS, scatter_dimension=1, tiled=True)  52.4 us
    all_gather x4, waiting for transfers between devices, layer_bwd(): lax.all_gather(d_cur.astype(jnp.bfloat16), TENSOR_AXIS, axis=1, tiled=True)  49.5 us
  transfers between devices with their start and end apart: 33, of which 28 were waited for; matrix products, arithmetic and copies ran while one was open for 16% of the time, Pallas kernels for 0%

commit v1 on v0

v1 whole, which is shorter than its diff:
```python
import functools
import jax
import jax.numpy as jnp
from jax import lax
from jax.experimental import pallas as pl
from jax.experimental.pallas import tpu as pltpu
from jax.sharding import PartitionSpec as P

TENSOR_AXIS = 'tp'
PARTS_AXIS = 'dp'
BF = jnp.bfloat16
F32 = jnp.float32
MESH = pl.DeviceIdType.MESH
VMEM_LIMIT = 67043328
NUM_CHUNKS = 2
RS_BLOCKS = 2
GELU_C = 0.7978845608028654


def dot_nn(a, b):
    return lax.dot_general(a, b, (((1,), (0,)), ((), ())), preferred_element_type=F32)


def dot_nt(a, b):
    return lax.dot_general(a, b, (((1,), (1,)), ((), ())), preferred_element_type=F32)


def dot_tn(a, b):
    return lax.dot_general(a, b, (((0,), (0,)), ((), ())), preferred_element_type=F32)


def seqs(c):
    return pl.ds(2 * c, 2)


def slab(r):
    return pl.ds(32 * r, 32)


def rows_of(ref, c):
    val = ref[seqs(c)]
    return val.reshape(256, val.shape[-1])


def normed(z):
    mean = jnp.mean(z, axis=-1, keepdims=True)
    centered = z - mean
    var = jnp.mean(centered * centered, axis=-1, keepdims=True)
    rstd = lax.rsqrt(var + 1e-5)
    return centered * rstd, rstd


class Exchange:
    def __init__(self, part, from_core, far_send, far_recv, sems):
        self.me = lax.axis_index(TENSOR_AXIS)
        self.part, self.from_core = part, from_core
        self.far_send, self.far_recv = far_send, far_recv
        self.gs, self.gr, self.cs, self.cr, self.xs, self.xr = sems

    def remote(self, src, dst, send, recv, flip):
        return pltpu.make_async_remote_copy(
            src_ref=src, dst_ref=dst, send_sem=send, recv_sem=recv,
            device_id={TENSOR_AXIS: lax.bitwise_xor(self.me, flip)}, device_id_type=MESH)

    def barrier(self):
        sem = pltpu.get_barrier_semaphore()
        for flip in (1, 2):
            pl.semaphore_signal(sem, inc=1, device_id={TENSOR_AXIS: lax.bitwise_xor(self.me, flip)}, device_id_type=MESH)
        pl.semaphore_wait(sem, 2)

    def gather_copy(self, buf, c, which):
        src, dst, flip = ((0, 2, 2), (0, 1, 1), (2, 3, 1))[which]
        return self.remote(buf.at[seqs(c), slab(src)], buf.at[seqs(c), slab(dst)], self.gs.at[c, which], self.gr.at[c, which], flip)

    def gather_start(self, buf, c):
        self.gather_copy(buf, c, 0).start()
        self.gather_copy(buf, c, 1).start()

    def gather_finish(self, buf, c):
        self.gather_copy(buf, c, 0).wait_recv()
        self.gather_copy(buf, c, 2).start()
        self.gather_copy(buf, c, 1).wait_recv()
        self.gather_copy(buf, c, 2).wait_recv()
        for which in range(3):
            self.gather_copy(buf, c, which).wait_send()

    def cols(self, b):
        width = self.part.shape[-1] // RS_BLOCKS
        return pl.ds(b * width, width)

    def core_copy(self, c, b, which):
        return self.remote(self.part.at[seqs(c), slab((1, 3)[which]), self.cols(b)],
                           self.from_core.at[seqs(c), slab(which), self.cols(b)],
                           self.cs.at[c, b, which], self.cr.at[c, b, which], 1)

    def far_copy(self, c, b):
        return self.remote(self.far_send.at[seqs(c), :, self.cols(b)], self.far_recv.at[seqs(c), :, self.cols(b)],
                           self.xs.at[c, b], self.xr.at[c, b], 2)

    def scatter_start(self, c, b):
        self.core_copy(c, b, 1).start()
        self.core_copy(c, b, 0).start()

    def scatter_middle(self, c, b):
        self.core_copy(c, b, 1).wait_recv()
        near = self.part[seqs(c), slab(2), self.cols(b)].astype(F32)
        self.far_send[seqs(c), :, self.cols(b)] = (near + self.from_core[seqs(c), slab(1), self.cols(b)].astype(F32)).astype(BF)
        self.far_copy(c, b).start()

    def scatter_finish(self, c):
        for b in range(RS_BLOCKS):
            self.core_copy(c, b, 0).wait_recv()
            self.far_copy(c, b).wait_recv()
            self.core_copy(c, b, 0).wait_send()
            self.core_copy(c, b, 1).wait_send()
            self.far_copy(c, b).wait_send()
        total = self.part[seqs(c), slab(0)].astype(F32) + self.from_core[seqs(c), slab(0)].astype(F32)
        return (total + self.far_recv[seqs(c)].astype(F32)).astype(BF).astype(F32)

    @staticmethod
    def scratch(d):
        dma = pltpu.SemaphoreType.DMA
        return [pltpu.VMEM((4, 128, d), BF), pltpu.VMEM((4, 64, d), BF), pltpu.VMEM((4, 32, d), BF), pltpu.VMEM((4, 32, d), BF),
                dma((2, 3)), dma((2, 3)), dma((2, RS_BLOCKS, 2)), dma((2, RS_BLOCKS, 2)), dma((2, RS_BLOCKS)), dma((2, RS_BLOCKS))]


def partial_sum(ex, c, block_of, bn=512):
    width = ex.part.shape[-1] // RS_BLOCKS
    for b in range(RS_BLOCKS):
        for j in range(width // bn):
            cols = pl.ds(b * width + j * bn, bn)
            ex.part[seqs(c), :, cols] = block_of(cols).astype(BF).reshape(2, 128, bn)
        ex.scatter_start(c, b)


def lane_low():
    return lax.broadcasted_iota(jnp.int32, (128, 128), 1) < 64


def two_heads(val, low):
    zero = jnp.zeros_like(val)
    return jnp.concatenate([jnp.where(low, val, zero), jnp.where(low, zero, val)], axis=0)


def forward_kernel(x_in, mask, vec, bup, wqkv_h, wout_h, wup_h, wdown_h,
                   y_out, x_s, hid_s, a_s, qkv_s, ctx_s, p_s, m_s, u_s, act_s,
                   wq, wo, wu, wd, xbuf, hbuf, ag_a, ag_m, qkv, ctx, prob, u, act,
                   wsem, ssem, part, from_core, far_send, far_recv, *sems):
    n_layers = wqkv_h.shape[0]
    ex = Exchange(part, from_core, far_send, far_recv, sems)

    def weight_copies(l, kind):
        pairs = ((wqkv_h, wq, 0), (wout_h, wo, 1)) if kind == 0 else ((wup_h, wu, 2), (wdown_h, wd, 3))
        return [pltpu.make_async_copy(src.at[l], dst, wsem.at[i]) for src, dst, i in pairs]

    def save_copies(l, c, kind):
        if kind == 0:
            pairs = ((xbuf, x_s, 0), (ag_a, a_s, 1), (qkv, qkv_s, 2), (ctx, ctx_s, 3), (prob, p_s, 4))
        else:
            pairs = ((hbuf, hid_s, 5), (ag_m, m_s, 6), (u, u_s, 7), (act, act_s, 8))
        return [pltpu.make_async_copy(src.at[seqs(c)], dst.at[l, seqs(c)], ssem.at[c, i]) for src, dst, i in pairs]

    def norm_and_send(src, l, c, row, buf):
        xhat, _ = normed(src[seqs(c)].reshape(64, -1))
        val = xhat * vec[row, pl.ds(l, 1), :] + vec[row + 1, pl.ds(l, 1), :]
        buf[seqs(c), slab(0)] = val.astype(BF).reshape(2, 32, -1)
        ex.gather_start(buf, c)

    def attention(c):
        a = rows_of(ag_a, c)
        for j in range(3):
            cols = pl.ds(512 * j, 512)
            qkv[seqs(c), :, cols] = dot_nt(a, wq[cols, :]).astype(BF).reshape(2, 128, 512)
        low = lane_low()
        for s in range(2):
            seq = 2 * c + s
            visible = mask[seq] > 0
            visible = jnp.concatenate([visible, visible], axis=0)
            for pair in range(4):
                q, k, v = (qkv[seq, :, pl.ds(512 * t + 128 * pair, 128)] for t in range(3))
                scores = dot_nt(two_heads(q, low), k) * 0.125
                scores = jnp.where(visible, scores, -1e30)
                e = jnp.exp(scores - jnp.max(scores, axis=-1, keepdims=True))
                p = e / jnp.sum(e, axis=-1, keepdims=True)
                prob[seq, pair] = p
                pb = p.astype(BF)
                both = jnp.concatenate([pb[:128], pb[128:]], axis=1)
                ctx[seq, :, pl.ds(128 * pair, 128)] = dot_nn(both, two_heads(v, low)).astype(BF)

    def mlp(l, c):
        m = rows_of(ag_m, c)

        @pl.loop(0, 4)
        def _(j):
            cols = pl.ds(pl.multiple_of(512 * j, 512), 512)
            pre = dot_nn(m, wu[:, cols]) + bup[pl.ds(l, 1), cols]
            u[seqs(c), :, cols] = pre.reshape(2, 128, 512)
            t = jnp.tanh(GELU_C * (pre + 0.044715 * (pre * pre * pre)))
            act[seqs(c), :, cols] = (0.5 * pre * (1.0 + t)).astype(BF).reshape(2, 128, 512)

    for kind in range(2):
        for copy in weight_copies(0, kind):
            copy.start()
    xbuf[...] = x_in[...]
    ex.barrier()
    for c in range(NUM_CHUNKS):
        norm_and_send(xbuf, 0, c, 0, ag_a)

    @pl.loop(0, n_layers)
    def _(l):
        for copy in weight_copies(l, 0):
            copy.wait()
        for c in range(NUM_CHUNKS):
            ex.gather_finish(ag_a, c)
            attention(c)
            for copy in save_copies(l, c, 0):
                copy.start()
            lhs = rows_of(ctx, c)
            partial_sum(ex, c, lambda cols: dot_nn(lhs, wo[:, cols]))
            for b in range(RS_BLOCKS):
                ex.scatter_middle(c, b)

        @pl.when(l + 1 < n_layers)
        def _():
            for copy in weight_copies(l + 1, 0):
                copy.start()

        for c in range(NUM_CHUNKS):
            hbuf[seqs(c)] = xbuf[seqs(c)] + ex.scatter_finish(c) + vec[4, pl.ds(l, 1), :][None]
            norm_and_send(hbuf, l, c, 2, ag_m)
        for copy in weight_copies(l, 1):
            copy.wait()
        for c in range(NUM_CHUNKS):
            ex.gather_finish(ag_m, c)
            mlp(l, c)
            for copy in save_copies(l, c, 1):
                copy.start()
            for copy in save_copies(l, c, 0):
                copy.wait()
            lhs = rows_of(act, c)
            partial_sum(ex, c, lambda cols: dot_nn(lhs, wd[:, cols]))
            for b in range(RS_BLOCKS):
                ex.scatter_middle(c, b)

        @pl.when(l + 1 < n_layers)
        def _():
            for copy in weight_copies(l + 1, 1):
                copy.start()

        for c in range(NUM_CHUNKS):
            xbuf[seqs(c)] = hbuf[seqs(c)] + ex.scatter_finish(c) + vec[5, pl.ds(l, 1), :][None]

            @pl.when(l + 1 < n_layers)
            def _():
                norm_and_send(xbuf, l + 1, c, 0, ag_a)

        for c in range(NUM_CHUNKS):
            for copy in save_copies(l, c, 1):
                copy.wait()

    y_out[...] = xbuf[...]


def backward_kernel(dy_in, vec, wqkv_h, wout_h, wup_h, wdown_h, x_s, hid_s, qkv_s, p_s, u_s,
                    d_x, dmlp_s, dpre_s, dattn_s, dqkv_s, g_bup, g_vec,
                    wq, wo, wu, wd, dcur, dhid, xbuf, hbuf, ag_a, ag_m, qkv, prob, u, dpre, dctx, dqkv, vacc, vfar,
                    wsem, rsem, ssem, vsem, part, from_core, far_send, far_recv, *sems):
    n_layers = wqkv_h.shape[0]
    ex = Exchange(part, from_core, far_send, far_recv, sems)

    def loads(l, kind):
        if kind == 0:
            whole = ((wqkv_h, wq, 0), (wout_h, wo, 1))
            saved = ((x_s, xbuf, 0), (qkv_s, qkv, 1), (p_s, prob, 2))
        else:
            whole = ((wdown_h, wd, 3), (wup_h, wu, 2))
            saved = ((u_s, u, 4), (hid_s, hbuf, 3))
        return ([pltpu.make_async_copy(src.at[l], dst, wsem.at[i]) for src, dst, i in whole]
                + [pltpu.make_async_copy(src.at[l], dst, rsem.at[i]) for src, dst, i in saved])

    def save_copies(l, c, kind):
        pairs = ((ag_a, dattn_s, 0), (dqkv, dqkv_s, 1)) if kind == 0 else ((ag_m, dmlp_s, 2), (dpre, dpre_s, 3))
        return [pltpu.make_async_copy(src.at[seqs(c)], dst.at[l, seqs(c)], ssem.at[c, i]) for src, dst, i in pairs]

    def send(src, c, buf):
        buf[seqs(c), slab(0)] = src[seqs(c)].astype(BF)
        ex.gather_start(buf, c)

    def add_row(i, l, c, val):
        row = (i, pl.ds(l, 1))
        total = jnp.sum(val, axis=0, keepdims=True)
        vacc[row] = total if c == 0 else vacc[row] + total

    def norm_bwd(z_ref, d_z, l, c, row):
        xhat, rstd = normed(z_ref[seqs(c)].reshape(64, -1))
        add_row(row, l, c, d_z * xhat)
        add_row(row + 1, l, c, d_z)
        g = d_z * vec[row, pl.ds(l, 1), :]
        g_mean = jnp.mean(g, axis=-1, keepdims=True)
        gx_mean = jnp.mean(g * xhat, axis=-1, keepdims=True)
        return rstd * (g - g_mean - xhat * gx_mean)

    def mlp_bwd(l, c):
        d_mlp = rows_of(ag_m, c)

        @pl.loop(0, 4)
        def _(j):
            cols = pl.ds(pl.multiple_of(512 * j, 512), 512)
            d_act = dot_nt(d_mlp, wd[cols, :]).astype(BF).astype(F32)
            pre = u[seqs(c), :, cols].reshape(256, 512)
            sq = pre * pre
            t = jnp.tanh(GELU_C * (pre + 0.044715 * (sq * pre)))
            slope = 0.5 * (1.0 + t) + 0.5 * pre * (1.0 - t * t) * (GELU_C * (1.0 + 0.134145 * sq))
            d_pre = d_act * slope
            total = jnp.sum(d_pre, axis=0, keepdims=True)
            g_bup[pl.ds(l, 1), cols] = total if c == 0 else g_bup[pl.ds(l, 1), cols] + total
            dpre[seqs(c), :, cols] = d_pre.astype(BF).reshape(2, 128, 512)

    def attention_bwd(c):
        dctx[seqs(c)] = dot_nt(rows_of(ag_a, c), wo[...]).astype(BF).reshape(2, 128, 512)
        low = lane_low()
        for s in range(2):
            seq = 2 * c + s
            for pair in range(4):
                q, k, v = (qkv[seq, :, pl.ds(512 * t + 128 * pair, 128)] for t in range(3))
                d_c = two_heads(dctx[seq, :, pl.ds(128 * pair, 128)], low)
                p = prob[seq, pair]
                d_p = dot_nt(d_c, v).astype(BF).astype(F32)
                d_s = p * (d_p - jnp.sum(d_p * p, axis=-1, keepdims=True))
                d_s = (d_s * 0.125).astype(BF)
                both = jnp.concatenate([d_s[:128], d_s[128:]], axis=1)
                d_q = dot_nn(both, two_heads(k, low))
                d_k = dot_tn(d_s, two_heads(q, low))
                d_v = dot_tn(p.astype(BF), d_c)
                for t, val in enumerate((d_q, d_k, d_v)):
                    dqkv[seq, :, pl.ds(512 * t + 128 * pair, 128)] = val.astype(BF)

    for kind in (1, 0):
        for copy in loads(n_layers - 1, kind):
            copy.start()
    dcur[...] = dy_in[...].astype(F32)
    ex.barrier()
    for c in range(NUM_CHUNKS):
        send(dcur, c, ag_m)

    @pl.loop(0, n_layers)
    def _(i):
        l = n_layers - 1 - i
        for copy in loads(l, 1):
            copy.wait()
        for c in range(NUM_CHUNKS):
            ex.gather_finish(ag_m, c)
            mlp_bwd(l, c)
            for copy in save_copies(l, c, 1):
                copy.start()
            lhs = rows_of(dpre, c)
            partial_sum(ex, c, lambda cols: dot_nt(lhs, wu[cols, :]))
            for b in range(RS_BLOCKS):
                ex.scatter_middle(c, b)
        for c in range(NUM_CHUNKS):
            d_cur = dcur[seqs(c)].reshape(64, -1)
            d_hid = d_cur + norm_bwd(hbuf, ex.scatter_finish(c).reshape(64, -1), l, c, 2)
            dhid[seqs(c)] = d_hid.reshape(2, 32, -1)
            send(dhid, c, ag_a)
            add_row(5, l, c, d_cur)
            add_row(4, l, c, d_hid)

        @pl.when(l > 0)
        def _():
            for copy in loads(l - 1, 1):
                copy.start()

        for copy in loads(l, 0):
            copy.wait()
        for c in range(NUM_CHUNKS):
            ex.gather_finish(ag_a, c)
            attention_bwd(c)
            for copy in save_copies(l, c, 0):
                copy.start()
            for copy in save_copies(l, c, 1):
                copy.wait()
            lhs = rows_of(dqkv, c)
            partial_sum(ex, c, lambda cols: dot_nn(lhs, wq[:, cols]))
            for b in range(RS_BLOCKS):
                ex.scatter_middle(c, b)
        for c in range(NUM_CHUNKS):
            d_ln = norm_bwd(xbuf, ex.scatter_finish(c).reshape(64, -1), l, c, 0)
            dcur[seqs(c)] = dhid[seqs(c)] + d_ln.reshape(2, 32, -1)

            @pl.when(l > 0)
            def _():
                send(dcur, c, ag_m)

        @pl.when(l > 0)
        def _():
            for copy in loads(l - 1, 0):
                copy.start()

        for c in range(NUM_CHUNKS):
            for copy in save_copies(l, c, 0):
                copy.wait()

    d_x[...] = dcur[...]
    for step, flip in enumerate((1, 2)):
        copy = ex.remote(vacc if step == 0 else g_vec, vfar.at[step], vsem.at[step, 0], vsem.at[step, 1], flip)
        copy.start()
        copy.wait()
        g_vec[...] = (vacc if step == 0 else g_vec)[...] + vfar[step]


def any_spec():
    return pl.BlockSpec(memory_space=pl.ANY)


def vmem_spec():
    return pl.BlockSpec(memory_space=pltpu.VMEM)


def run_forward(x, mask, vec, bup, wqkv, wout, wup, wdown):
    n, d = wqkv.shape[0], x.shape[-1]
    shape = jax.ShapeDtypeStruct
    dma = pltpu.SemaphoreType.DMA
    outs = [shape((4, 32, d), F32), shape((n, 4, 32, d), F32), shape((n, 4, 32, d), F32), shape((n, 4, 128, d), BF),
            shape((n, 4, 128, 1536), BF), shape((n, 4, 128, 512), BF), shape((n, 4, 4, 256, 128), F32),
            shape((n, 4, 128, d), BF), shape((n, 4, 128, d), F32), shape((n, 4, 128, d), BF)]
    return pl.pallas_call(
        forward_kernel,
        in_specs=[vmem_spec()] * 4 + [any_spec()] * 4,
        out_specs=[vmem_spec()] + [any_spec()] * 9,
        out_shape=outs,
        scratch_shapes=[pltpu.VMEM((1536, d), BF), pltpu.VMEM((512, d), BF), pltpu.VMEM((d, d), BF), pltpu.VMEM((d, d), BF),
                        pltpu.VMEM((4, 32, d), F32), pltpu.VMEM((4, 32, d), F32), pltpu.VMEM((4, 128, d), BF), pltpu.VMEM((4, 128, d), BF),
                        pltpu.VMEM((4, 128, 1536), BF), pltpu.VMEM((4, 128, 512), BF), pltpu.VMEM((4, 4, 256, 128), F32),
                        pltpu.VMEM((4, 128, d), F32), pltpu.VMEM((4, 128, d), BF), dma((4,)), dma((2, 9)), *Exchange.scratch(d)],
        compiler_params=pltpu.CompilerParams(collective_id=0, has_side_effects=True, vmem_limit_bytes=VMEM_LIMIT),
        name='forward',
    )(x, mask, vec, bup, wqkv, wout, wup, wdown)


def run_backward(dy, vec, wqkv, wout, wup, wdown, x_s, hid_s, qkv_s, p_s, u_s):
    n, d = wqkv.shape[0], dy.shape[-1]
    shape = jax.ShapeDtypeStruct
    dma = pltpu.SemaphoreType.DMA
    outs = [shape((4, 32, d), F32), shape((n, 4, 128, d), BF), shape((n, 4, 128, d), BF), shape((n, 4, 128, d), BF),
            shape((n, 4, 128, 1536), BF), shape((n, d), F32), shape((6, n, d), F32)]
    return pl.pallas_call(
        backward_kernel,
        in_specs=[vmem_spec()] * 2 + [any_spec()] * 9,
        out_specs=[vmem_spec()] + [any_spec()] * 4 + [vmem_spec()] * 2,
        out_shape=outs,
        scratch_shapes=[pltpu.VMEM((1536, d), BF), pltpu.VMEM((512, d), BF), pltpu.VMEM((d, d), BF), pltpu.VMEM((d, d), BF)]
                       + [pltpu.VMEM((4, 32, d), F32)] * 4
                       + [pltpu.VMEM((4, 128, d), BF), pltpu.VMEM((4, 128, d), BF), pltpu.VMEM((4, 128, 1536), BF), pltpu.VMEM((4, 4, 256, 128), F32),
                          pltpu.VMEM((4, 128, d), F32), pltpu.VMEM((4, 128, d), BF), pltpu.VMEM((4, 128, 512), BF), pltpu.VMEM((4, 128, 1536), BF),
                          pltpu.VMEM((6, n, d), F32), pltpu.VMEM((2, 6, n, d), F32),
                          dma((4,)), dma((5,)), dma((2, 4)), dma((2, 2)), *Exchange.scratch(d)],
        compiler_params=pltpu.CompilerParams(collective_id=1, has_side_effects=True, vmem_limit_bytes=VMEM_LIMIT),
        name='backward',
    )(dy, vec, wqkv, wout, wup, wdown, x_s, hid_s, qkv_s, p_s, u_s)


def wgrad_kernel(a, b, out):
    out[0] = dot_tn(a[0], b[0]).astype(BF)


def weight_grad(a, b):
    n, rows, m = a.shape
    width = b.shape[2]
    tm = 256
    return pl.pallas_call(
        wgrad_kernel,
        grid=(n, m // tm),
        in_specs=[pl.BlockSpec((1, rows, tm), lambda l, i: (l, 0, i)), pl.BlockSpec((1, rows, width), lambda l, i: (l, 0, 0))],
        out_specs=pl.BlockSpec((1, tm, width), lambda l, i: (l, i, 0)),
        out_shape=jax.ShapeDtypeStruct((n, m, width), BF),
        compiler_params=pltpu.CompilerParams(vmem_limit_bytes=32 * 1024 * 1024),
        cost_estimate=pl.CostEstimate(flops=2 * n * rows * m * width, bytes_accessed=2 * n * (m * width + rows * (m + width)), transcendentals=0),
        name='weight_grad',
    )(a, b)


def group_body(x_loc, dy_loc, len_loc, wqkv_loc, wout_loc, wup_loc, bup_loc, wdown_loc, vec_loc):
    n, d = wqkv_loc.shape[0], x_loc.shape[-1]
    me = lax.axis_index(TENSOR_AXIS)
    row = jnp.arange(128, dtype=jnp.int32)
    pos = ((row // 32) ^ me) * 32 + row % 32
    visible = (pos[None, None, :] <= pos[None, :, None]) & (pos[None, None, :] < len_loc[:, None, None])
    mask = visible.astype(F32)
    vec = vec_loc.transpose(1, 0, 2)
    wqkv = wqkv_loc.transpose(0, 2, 3, 4, 1).reshape(n, 1536, d)
    wout = wout_loc.reshape(n, 512, d)
    y, x_s, hid_s, a_s, qkv_s, ctx_s, p_s, m_s, u_s, act_s = run_forward(x_loc, mask, vec, bup_loc, wqkv, wout, wup_loc, wdown_loc)
    d_x, dmlp_s, dpre_s, dattn_s, dqkv_s, g_bup, g_vec = run_backward(dy_loc, vec, wqkv, wout, wup_loc, wdown_loc, x_s, hid_s, qkv_s, p_s, u_s)

    def tokens(val):
        return val.reshape(n, 512, val.shape[-1])

    g_qkv = weight_grad(tokens(dqkv_s), tokens(a_s)).reshape(n, 3, 8, 64, d).transpose(0, 4, 1, 2, 3)
    g_out = weight_grad(tokens(ctx_s), tokens(dattn_s)).reshape(n, 8, 64, d)
    g_up = weight_grad(tokens(m_s), tokens(dpre_s))
    g_down = weight_grad(tokens(act_s), tokens(dmlp_s))
    return y, d_x, g_qkv, g_out, g_up, g_bup, g_down, g_vec.transpose(1, 0, 2)


def solution(mesh):
    act_spec = P(PARTS_AXIS, TENSOR_AXIS, None)
    in_specs = (act_spec, act_spec, P(PARTS_AXIS), P(None, None, None, TENSOR_AXIS, None), P(None, TENSOR_AXIS, None, None), P(None, None, TENSOR_AXIS), P(None, TENSOR_AXIS), P(None, TENSOR_AXIS, None), P())
    out_specs = (act_spec, act_spec, P(PARTS_AXIS, None, None, TENSOR_AXIS, None), P(PARTS_AXIS, TENSOR_AXIS, None, None), P(PARTS_AXIS, None, TENSOR_AXIS), P(PARTS_AXIS, TENSOR_AXIS), P(PARTS_AXIS, TENSOR_AXIS, None), P(PARTS_AXIS, None, None))
    return jax.shard_map(group_body, mesh=mesh, in_specs=in_specs, out_specs=out_specs, check_vma=False)
```

time: 1200 us -> 582 us (0.48)
  waiting for transfers between devices: 592 us -> 0 us
  Pallas kernels: 0 us -> 560 us
  matrix products: 418 us -> 0 us
  other arithmetic: 131 us -> 1.55 us
  between operations: 16.3 us -> 0.71 us
  local copies, waits for them, and re-layouts: 33.2 us -> 20.2 us
    pallas_call x0 -> x6, Pallas kernels: none -> 560 us  [the longest x1 249 us: run_backward(): pl.pallas_call(backward_kernel, in_specs=[vmem_spec()] * 2 + [any_spec()]...]
    dot_general x68 -> x0, matrix products: 405 us -> none  [the longest x4 44.4 us: layer_bwd(): jnp.einsum('bsd,fd->bsf', d_mlp, w_down, preferred_element_type=jnp.float32)]
    reduce_scatter x16 -> x0, waiting for transfers between devices: 319 us -> none  [the longest x4 101 us: layer_fwd(): lax.psum_scatter(attn_part, TENSOR_AXIS, scatter_dimension=1, tiled=True)]
    all_gather x16 -> x0, waiting for transfers between devices: 247 us -> none  [the longest x4 80.5 us: layer_fwd(): a_full = lax.all_gather(a_shard, TENSOR_AXIS, axis=1, tiled=True)]
    another operation x5 -> x0, other arithmetic: 59.5 us -> none  [group_body(): jnp.stack([grad_set[grad_pos] for grad_set in layer_grads])]
    reduce_sum x39 -> x0, other arithmetic: 55.4 us -> none  [the longest x16 31 us: layer_norm(): return centered * lax.rsqrt(row_var + 1e-05) * gain_vec + shift_vec]
    psum x1 -> x0, waiting for transfers between devices: 25.4 us -> none  [group_body(): g_vec = lax.psum(stacked[5], TENSOR_AXIS)]
    convert_element_type x15 -> x1, other arithmetic: 14.4 us -> 0.73 us  [group_body(): mask = visible.astype(F32)]
  transfers between devices with their start and end apart: 33 -> 0, of which waited for: 28 -> 0; matrix products, arithmetic and copies ran while one was open for 16% -> 0% of each run, Pallas kernels for 0% -> 0%
where the time goes in v1:
time: 582 us
  Pallas kernels  560 us (96%)
  local copies, waits for them, and re-layouts  20.2 us (3%)
    pallas_call x1, Pallas kernels, run_backward(): pl.pallas_call(backward_kernel, in_specs=[vmem_spec()] * 2 + [any_spec()]...  249 us
    pallas_call x1, Pallas kernels, run_forward(): pl.pallas_call(forward_kernel, in_specs=[vmem_spec()] * 4 + [any_spec()]...  224 us
    pallas_call x4, Pallas kernels, weight_grad(): pl.pallas_call(wgrad_kernel, grid=(n, m // tm), in_specs=[pl.BlockSpec((1...  86.5 us
    unnamed x30, local copies, waits for them, and re-layouts  20.2 us

profile of v1, /device:TPU:0, one launch (start us, length us, event | category | flops | bytes accessed | tf_op | source)
XLA Modules:
  0.0 582.1 jit_solution(5358424661971559953)
XLA Ops:
  0.6 0.1 broadcast_compare_fusion
  0.7 0.7 broadcast_compare_fusion.1
  1.5 0.7 and_convert_fusion.mask
  2.2 224.3 %forward.1 = (f32[4,32,2048]{2,1,0:T(8,128)}, f32[4,4,32,2048]{3,2,1,0:T(8,128)}, f32[4,4,32,2048]{3,2,1,0:T(8,128)}, bf16[4,4,128,2048]{3,2,1,0:T(8,128)(2,1)},...) custom-call(f32[4,32,2048]{2,1,0:T(8,128)} %x_in.1, ...), custom_call_target="tpu_custom_call" | custom-call | tf_op jit(solution)/shard_map/forward/pallas_call | solution.py:426
  226.5 248.9 %backward.1 = (f32[4,32,2048]{2,1,0:T(8,128)}, bf16[4,4,128,2048]{3,2,1,0:T(8,128)(2,1)}, bf16[4,4,128,2048]{3,2,1,0:T(8,128)(2,1)}, bf16[4,4,128,2048]{3,2,1,0:...) custom-call(bf16[4,32,2048]{2,1,0:T(8,128)(2,1)} %dy_in.1, ...), custom_call_target="tpu_custom_call" | custom-call | tf_op jit(solution)/shard_map/backward/pallas_call | solution.py:446
  475.4 0.0 copy-start.3
  475.4 3.4 copy-done.3
  478.8 0.0 copy-start.5
  478.8 3.4 copy-done.5
  482.2 0.0 slice-start
  482.2 28.7 %weight_grad.7 = bf16[4,2048,2048]{2,1,0:T(8,128)(2,1)} custom-call(bf16[4,512,2048]{2,1,0:T(8,128)(2,1)S(1)} %bitcast.24, bf16[4,512,2048]{2,1,0:T(8,128)(2,1)S(1)} %bitcast.26), custom_call_target="tpu_custom_call" | custom-call | flops 17179869184 | bytes 50331648 | tf_op jit(solution)/shard_map/weight_grad/pallas_call | solution.py:470
  510.8 3.4 copy-done.2
  514.2 0.0 copy-start.4
  514.2 3.4 copy-done.4
  517.6 0.0 slice-start.1
  517.6 28.7 %weight_grad.6 = bf16[4,2048,2048]{2,1,0:T(8,128)(2,1)} custom-call(bf16[4,512,2048]{2,1,0:T(8,128)(2,1)S(1)} %bitcast.23, bf16[4,512,2048]{2,1,0:T(8,128)(2,1)S(1)} %bitcast.25), custom_call_target="tpu_custom_call" | custom-call | flops 17179869184 | bytes 50331648 | tf_op jit(solution)/shard_map/weight_grad/pallas_call | solution.py:470
  546.3 0.0 slice-done
  546.3 0.0 slice-done.1
  546.3 0.0 copy-done
  546.3 0.0 copy-start.6
  546.3 7.7 %weight_grad.5 = bf16[4,512,2048]{2,1,0:T(8,128)(2,1)} custom-call(bf16[4,512,512]{2,1,0:T(8,128)(2,1)S(1)} %bitcast.21, bf16[4,512,2048]{2,1,0:T(8,128)(2,1)S(1)} %bitcast.20), custom_call_target="tpu_custom_call" | custom-call | flops 4294967296 | bytes 18874368 | tf_op jit(solution)/shard_map/weight_grad/pallas_call | solution.py:470
  554.0 0.0 copy-done.6
  554.0 3.4 copy-done.1
  557.4 21.5 %weight_grad.4 = bf16[4,1536,2048]{2,1,0:T(8,128)(2,1)} custom-call(bf16[4,512,1536]{2,1,0:T(8,128)(2,1)S(1)} %bitcast.27, bf16[4,512,2048]{2,1,0:T(8,128)(2,1)S(1)} %bitcast.22), custom_call_target="tpu_custom_call" | custom-call | flops 12884901888 | bytes 39845888 | tf_op jit(solution)/shard_map/weight_grad/pallas_call | solution.py:470
  578.9 0.0 copy-done.7
  578.9 1.0 copy.21
  579.8 0.0 copy-done.8
  579.8 1.0 copy.22
  580.8 0.0 copy-done.10
  580.8 0.6 copy.23
  581.4 0.0 copy-done.9
  581.4 0.7 copy.24
  (9 shorter events, 0.0 us)
Async XLA Ops:
  475.4 3.4 copy-start.3
  478.8 3.4 copy-start.5
  482.2 64.1 %slice-start = ((s8[8388608]{0:T(1024)(128)(4,1)}), s8[4194304]{0:T(1024)(128)(4,1)S(1)}, s32[]{:S(2)}) async-start(s8[8388608]{0:T(1024)(128)(4,1)} %bitcast.18), calls=%async_computation | async-start | bytes 8388608
  510.8 3.4 copy-start.2
  514.2 3.4 copy-start.4
  517.6 28.7 %slice-start.1 = ((s8[8388608]{0:T(1024)(128)(4,1)}), s8[4194304]{0:T(1024)(128)(4,1)S(1)}, s32[]{:S(2)}) async-start(s8[8388608]{0:T(1024)(128)(4,1)} %bitcast.18), calls=%async_computation.1 | async-start | bytes 8388608
  517.6 28.7 %copy-start = (bf16[4,4,128,512]{3,2,1,0:T(8,128)(2,1)S(1)}, bf16[4,4,128,512]{3,2,1,0:T(8,128)(2,1)}, u32[]{:S(2)}) copy-start(bf16[4,4,128,512]{3,2,1,0:T(8,128)(2,1)} %get-tuple-element.34) | copy-start | bytes 6291460
  546.3 7.7 %copy-start.6 = (bf16[4,4,128,1536]{3,2,1,0:T(8,128)(2,1)S(1)}, bf16[4,4,128,1536]{3,2,1,0:T(8,128)(2,1)}, u32[]{:S(2)}) copy-start(bf16[4,4,128,1536]{3,2,1,0:T(8,128)(2,1)} %get-tuple-element.32) | copy-start | bytes 18874372
  554.0 3.4 copy-start.1
  557.4 21.5 %copy-start.7 = (f32[4,32,2048]{2,1,0:T(8,128)S(1)}, f32[4,32,2048]{2,1,0:T(8,128)}, u32[]{:S(2)}) copy-start(f32[4,32,2048]{2,1,0:T(8,128)} %get-tuple-element.50) | copy-start | bytes 3145732
  557.4 22.5 %copy-start.8 = (f32[4,32,2048]{2,1,0:T(8,128)S(1)}, f32[4,32,2048]{2,1,0:T(8,128)}, u32[]{:S(2)}) copy-start(f32[4,32,2048]{2,1,0:T(8,128)} %get-tuple-element.51) | copy-start | bytes 3145732
  557.4 23.4 %copy-start.10 = (f32[4,2048]{1,0:T(4,128)S(1)}, f32[4,2048]{1,0:T(4,128)}, u32[]{:S(2)}) copy-start(f32[4,2048]{1,0:T(4,128)} %get-tuple-element.55) | copy-start | bytes 98308
  557.4 24.0 %copy-start.9 = (f32[6,4,2048]{2,1,0:T(4,128)S(1)}, f32[6,4,2048]{2,1,0:T(4,128)}, u32[]{:S(2)}) copy-start(f32[6,4,2048]{2,1,0:T(4,128)} %get-tuple-element.41) | copy-start | bytes 589828

commit v2 on v1

v2 whole, which is shorter than its diff:
```python
import functools
import jax
import jax.numpy as jnp
from jax import lax
from jax.experimental import pallas as pl
from jax.experimental.pallas import tpu as pltpu
from jax.sharding import PartitionSpec as P

TENSOR_AXIS = 'tp'
PARTS_AXIS = 'dp'
BF = jnp.bfloat16
F32 = jnp.float32
MESH = pl.DeviceIdType.MESH
VMEM_LIMIT = 67043328
NUM_CHUNKS = 2
RS_BLOCKS = 2
GELU_C = 0.7978845608028654


def dot_nn(a, b):
    return lax.dot_general(a, b, (((1,), (0,)), ((), ())), preferred_element_type=F32)


def dot_nt(a, b):
    return lax.dot_general(a, b, (((1,), (1,)), ((), ())), preferred_element_type=F32)


def dot_tn(a, b):
    return lax.dot_general(a, b, (((0,), (0,)), ((), ())), preferred_element_type=F32)


def seqs(c):
    return pl.ds(2 * c, 2)


def rows_of(ref, c):
    val = ref[seqs(c)]
    return val.reshape(256, val.shape[-1])


def normed(z):
    mean = jnp.mean(z, axis=-1, keepdims=True)
    centered = z - mean
    var = jnp.mean(centered * centered, axis=-1, keepdims=True)
    rstd = lax.rsqrt(var + 1e-5)
    return centered * rstd, rstd


class Exchange:
    def __init__(self, part, from_core, far_send, far_recv, sems):
        self.me = lax.axis_index(TENSOR_AXIS)
        self.part, self.from_core = part, from_core
        self.far_send, self.far_recv = far_send, far_recv
        self.gs, self.gr, self.cs, self.cr, self.xs, self.xr = sems

    def remote(self, src, dst, send, recv, flip):
        return pltpu.make_async_remote_copy(
            src_ref=src, dst_ref=dst, send_sem=send, recv_sem=recv,
            device_id={TENSOR_AXIS: lax.bitwise_xor(self.me, flip)}, device_id_type=MESH)

    def barrier(self):
        sem = pltpu.get_barrier_semaphore()
        for flip in (1, 2):
            pl.semaphore_signal(sem, inc=1, device_id={TENSOR_AXIS: lax.bitwise_xor(self.me, flip)}, device_id_type=MESH)
        pl.semaphore_wait(sem, 2)

    def gather(self, buf, c):
        return self.remote(buf.at[seqs(c), pl.ds(0, 64)], buf.at[seqs(c), pl.ds(64, 64)], self.gs.at[c], self.gr.at[c], 1)

    def cols(self, b):
        width = self.part.shape[-1] // RS_BLOCKS
        return pl.ds(b * width, width)

    def core_copy(self, c, b):
        return self.remote(self.part.at[seqs(c), pl.ds(64, 64), self.cols(b)], self.from_core.at[seqs(c), :, self.cols(b)],
                           self.cs.at[c, b], self.cr.at[c, b], 1)

    def far_copy(self, kind, c, b, full):
        rows = pl.ds(0, 64) if full else pl.ds(32, 32)
        return self.remote(self.far_send.at[seqs(c), rows, self.cols(b)], self.far_recv.at[kind, seqs(c), rows, self.cols(b)],
                           self.xs.at[kind, c, b], self.xr.at[kind, c, b], 2)

    def middle(self, kind, c, full):
        for b in range(RS_BLOCKS):
            self.core_copy(c, b).wait_recv()
            near = self.part[seqs(c), pl.ds(0, 64), self.cols(b)].astype(F32)
            self.far_send[seqs(c), :, self.cols(b)] = (near + self.from_core[seqs(c), :, self.cols(b)].astype(F32)).astype(BF)
            if full is True:
                self.far_copy(kind, c, b, True).start()
            else:
                @pl.when(full)
                def _():
                    self.far_copy(kind, c, b, True).start()

                @pl.when(jnp.logical_not(full))
                def _():
                    self.far_copy(kind, c, b, False).start()

    def finish(self, kind, c, full):
        for b in range(RS_BLOCKS):
            self.far_copy(kind, c, b, full).wait_recv()
            self.far_copy(kind, c, b, full).wait_send()
            self.core_copy(c, b).wait_send()
        own = self.far_send[seqs(c), pl.ds(0, 32)].astype(F32) + self.far_recv[kind, seqs(c), pl.ds(32, 32)].astype(F32)
        own = own.astype(BF).astype(F32)
        if not full:
            return own
        twin = self.far_send[seqs(c), pl.ds(32, 32)].astype(F32) + self.far_recv[kind, seqs(c), pl.ds(0, 32)].astype(F32)
        return jnp.concatenate([own, twin.astype(BF).astype(F32)], axis=1)

    @staticmethod
    def scratch(d):
        dma = pltpu.SemaphoreType.DMA
        return [pltpu.VMEM((4, 128, d), BF), pltpu.VMEM((4, 64, d), BF), pltpu.VMEM((4, 64, d), BF), pltpu.VMEM((2, 4, 64, d), BF),
                dma((2,)), dma((2,)), dma((2, RS_BLOCKS)), dma((2, RS_BLOCKS)), dma((2, 2, RS_BLOCKS)), dma((2, 2, RS_BLOCKS))]


def partial_sum(ex, c, block_of, bn=512):
    width = ex.part.shape[-1] // RS_BLOCKS
    for b in range(RS_BLOCKS):
        @pl.loop(0, width // bn)
        def _(j):
            cols = pl.ds(pl.multiple_of(b * width + j * bn, bn), bn)
            ex.part[seqs(c), :, cols] = block_of(cols).astype(BF).reshape(2, 128, bn)

        ex.core_copy(c, b).start()


def lane_low():
    return lax.broadcasted_iota(jnp.int32, (128, 128), 1) < 64


def two_heads(val, low):
    zero = jnp.zeros_like(val)
    return jnp.concatenate([jnp.where(low, val, zero), jnp.where(low, zero, val)], axis=0)


def forward_kernel(x_in, mask, vec, bup, wqkv_h, wout_h, wup_h, wdown_h,
                   y_out, x_s, hid_s, a_s, qkv_s, ctx_s, p_s, m_s, u_s, act_s,
                   wq, wo, wu, wd, xbuf, hbuf, ag_a, ag_m, qkv, ctx, prob, u, act,
                   wsem, ssem, isem, part, from_core, far_send, far_recv, *sems):
    n_layers = wqkv_h.shape[0]
    ex = Exchange(part, from_core, far_send, far_recv, sems)

    def weight_copies(l, kind):
        pairs = ((wqkv_h, wq, 0), (wout_h, wo, 1)) if kind == 0 else ((wup_h, wu, 2), (wdown_h, wd, 3))
        return [pltpu.make_async_copy(src.at[l], dst, wsem.at[i]) for src, dst, i in pairs]

    def save_copies(l, c, kind):
        if kind == 0:
            pairs = ((xbuf, x_s, 0), (ag_a, a_s, 1), (qkv, qkv_s, 2), (ctx, ctx_s, 3), (prob, p_s, 4))
        else:
            pairs = ((hbuf, hid_s, 5), (ag_m, m_s, 6), (u, u_s, 7), (act, act_s, 8))
        return [pltpu.make_async_copy(src.at[seqs(c)], dst.at[l, seqs(c)], ssem.at[c, i]) for src, dst, i in pairs]

    def norm_and_gather(src, l, c, row, buf):
        xhat, _ = normed(src[seqs(c)].reshape(128, -1))
        val = xhat * vec[row, pl.ds(l, 1), :] + vec[row + 1, pl.ds(l, 1), :]
        buf[seqs(c), pl.ds(0, 64)] = val.astype(BF).reshape(2, 64, -1)
        ex.gather(buf, c).start()
        ex.gather(buf, c).wait()

    def first_copy(c):
        return ex.remote(x_in.at[seqs(c)], xbuf.at[seqs(c), pl.ds(32, 32)], isem.at[0, c], isem.at[1, c], 2)

    def attention(c):
        a = rows_of(ag_a, c)
        for j in range(3):
            cols = pl.ds(512 * j, 512)
            qkv[seqs(c), :, cols] = dot_nt(a, wq[cols, :]).astype(BF).reshape(2, 128, 512)
        low = lane_low()

        @pl.loop(0, 2)
        def _(s):
            seq = 2 * c + s
            visible = mask[seq] > 0
            visible = jnp.concatenate([visible, visible], axis=0)
            for pair in range(4):
                q, k, v = (qkv[seq, :, pl.ds(512 * t + 128 * pair, 128)] for t in range(3))
                scores = dot_nt(two_heads(q, low), k) * 0.125
                scores = jnp.where(visible, scores, -1e30)
                e = jnp.exp(scores - jnp.max(scores, axis=-1, keepdims=True))
                p = e / jnp.sum(e, axis=-1, keepdims=True)
                prob[seq, pair] = p
                pb = p.astype(BF)
                both = jnp.concatenate([pb[:128], pb[128:]], axis=1)
                ctx[seq, :, pl.ds(128 * pair, 128)] = dot_nn(both, two_heads(v, low)).astype(BF)

    def mlp(l, c):
        m = rows_of(ag_m, c)

        @pl.loop(0, 4)
        def _(j):
            cols = pl.ds(pl.multiple_of(512 * j, 512), 512)
            pre = dot_nn(m, wu[:, cols]) + bup[pl.ds(l, 1), cols]
            u[seqs(c), :, cols] = pre.reshape(2, 128, 512)
            t = jnp.tanh(GELU_C * (pre + 0.044715 * (pre * pre * pre)))
            act[seqs(c), :, cols] = (0.5 * pre * (1.0 + t)).astype(BF).reshape(2, 128, 512)

    for kind in range(2):
        for copy in weight_copies(0, kind):
            copy.start()
    ex.barrier()
    for c in range(NUM_CHUNKS):
        first_copy(c).start()
    xbuf[:, pl.ds(0, 32)] = x_in[...]

    @pl.loop(0, n_layers)
    def _(l):
        for c in range(NUM_CHUNKS):
            @pl.when(l == 0)
            def _():
                first_copy(c).wait()

            @pl.when(l > 0)
            def _():
                xbuf[seqs(c)] = hbuf[seqs(c)] + ex.finish(1, c, True) + vec[5, pl.ds(l - 1, 1), :][None]

            norm_and_gather(xbuf, l, c, 0, ag_a)
            if c == 0:
                for copy in weight_copies(l, 0):
                    copy.wait()
            attention(c)
            for copy in save_copies(l, c, 0):
                copy.start()
            lhs = rows_of(ctx, c)
            partial_sum(ex, c, lambda cols: dot_nn(lhs, wo[:, cols]))
            ex.middle(0, c, True)

        @pl.when(l + 1 < n_layers)
        def _():
            for copy in weight_copies(l + 1, 0):
                copy.start()

        for c in range(NUM_CHUNKS):
            hbuf[seqs(c)] = xbuf[seqs(c)] + ex.finish(0, c, True) + vec[4, pl.ds(l, 1), :][None]
            norm_and_gather(hbuf, l, c, 2, ag_m)
            if c == 0:
                for copy in weight_copies(l, 1):
                    copy.wait()
            mlp(l, c)
            for copy in save_copies(l, c, 1):
                copy.start()
            for copy in save_copies(l, c, 0):
                copy.wait()
            lhs = rows_of(act, c)
            partial_sum(ex, c, lambda cols: dot_nn(lhs, wd[:, cols]))
            ex.middle(1, c, l + 1 < n_layers)

        @pl.when(l + 1 < n_layers)
        def _():
            for copy in weight_copies(l + 1, 1):
                copy.start()

        for c in range(NUM_CHUNKS):
            for copy in save_copies(l, c, 1):
                copy.wait()

    for c in range(NUM_CHUNKS):
        y_out[seqs(c)] = hbuf[seqs(c), pl.ds(0, 32)] + ex.finish(1, c, False) + vec[5, pl.ds(n_layers - 1, 1), :][None]


def backward_kernel(dy_in, vec, wqkv_h, wout_h, wup_h, wdown_h, x_s, hid_s, qkv_s, p_s, u_s,
                    d_x, dmlp_s, dpre_s, dattn_s, dqkv_s, g_bup, g_vec,
                    wq, wo, wu, wd, dcur, dhid, zbuf, ag_a, ag_m, qkv, prob, u, dpre, dctx, dqkv, vacc, vfar, vlast,
                    wsem, rsem, zsem, ssem, vsem, isem, part, from_core, far_send, far_recv, *sems):
    n_layers = wqkv_h.shape[0]
    ex = Exchange(part, from_core, far_send, far_recv, sems)

    def loads(l, kind):
        if kind == 0:
            whole = ((wqkv_h, wq, 0), (wout_h, wo, 1))
            saved = ((qkv_s, qkv, 1), (p_s, prob, 2))
        else:
            whole = ((wdown_h, wd, 3), (wup_h, wu, 2))
            saved = ((u_s, u, 0),)
        return ([pltpu.make_async_copy(src.at[l], dst, wsem.at[i]) for src, dst, i in whole]
                + [pltpu.make_async_copy(src.at[l], dst, rsem.at[i]) for src, dst, i in saved])

    def z_load(l, c, kind):
        return pltpu.make_async_copy((x_s, hid_s)[kind].at[l, seqs(c)], zbuf.at[seqs(c)], zsem.at[c])

    def save_copies(l, c, kind):
        pairs = ((ag_a, dattn_s, 0), (dqkv, dqkv_s, 1)) if kind == 0 else ((ag_m, dmlp_s, 2), (dpre, dpre_s, 3))
        return [pltpu.make_async_copy(src.at[seqs(c)], dst.at[l, seqs(c)], ssem.at[c, i]) for src, dst, i in pairs]

    def send(src, c, buf):
        buf[seqs(c), pl.ds(0, 64)] = src[seqs(c)].astype(BF)
        ex.gather(buf, c).start()
        ex.gather(buf, c).wait()

    def first_copy(c):
        return ex.remote(dy_in.at[seqs(c)], far_recv.at[0, seqs(c), pl.ds(0, 32)], isem.at[0, c], isem.at[1, c], 2)

    def dx_copy(c):
        return pltpu.make_async_copy(dcur.at[seqs(c), pl.ds(0, 32)], d_x.at[seqs(c)], isem.at[0, c])

    def row_sum(val):
        sums = [jnp.sum(val[:, 32 * i:32 * i + 32].reshape(64, -1), axis=0, keepdims=True) for i in range(val.shape[1] // 32)]
        return sums[0] if len(sums) == 1 else sums[0] + sums[1]

    def add_row(i, l, c, val):
        row = (i, pl.ds(l, 1))
        total = row_sum(val)
        vacc[row] = total if c == 0 else vacc[row] + total

    def norm_bwd(z, d_z, gain):
        shape = z.shape
        z, d_z = z.reshape(-1, shape[-1]), d_z.reshape(-1, shape[-1])
        xhat, rstd = normed(z)
        g = d_z * gain
        g_mean = jnp.mean(g, axis=-1, keepdims=True)
        gx_mean = jnp.mean(g * xhat, axis=-1, keepdims=True)
        return (rstd * (g - g_mean - xhat * gx_mean)).reshape(shape), (d_z * xhat).reshape(shape)

    def mlp_bwd(l, c):
        d_mlp = rows_of(ag_m, c)

        @pl.loop(0, 4)
        def _(j):
            cols = pl.ds(pl.multiple_of(512 * j, 512), 512)
            d_act = dot_nt(d_mlp, wd[cols, :]).astype(BF).astype(F32)
            pre = u[seqs(c), :, cols].reshape(256, 512)
            sq = pre * pre
            t = jnp.tanh(GELU_C * (pre + 0.044715 * (sq * pre)))
            slope = 0.5 * (1.0 + t) + 0.5 * pre * (1.0 - t * t) * (GELU_C * (1.0 + 0.134145 * sq))
            d_pre = d_act * slope
            total = jnp.sum(d_pre, axis=0, keepdims=True)
            g_bup[pl.ds(l, 1), cols] = total if c == 0 else g_bup[pl.ds(l, 1), cols] + total
            dpre[seqs(c), :, cols] = d_pre.astype(BF).reshape(2, 128, 512)

    def attention_bwd(c):
        dctx[seqs(c)] = dot_nt(rows_of(ag_a, c), wo[...]).astype(BF).reshape(2, 128, 512)
        low = lane_low()

        @pl.loop(0, 2)
        def _(s):
            seq = 2 * c + s
            for pair in range(4):
                q, k, v = (qkv[seq, :, pl.ds(512 * t + 128 * pair, 128)] for t in range(3))
                d_c = two_heads(dctx[seq, :, pl.ds(128 * pair, 128)], low)
                p = prob[seq, pair]
                d_p = dot_nt(d_c, v).astype(BF).astype(F32)
                d_s = p * (d_p - jnp.sum(d_p * p, axis=-1, keepdims=True))
                d_s = (d_s * 0.125).astype(BF)
                both = jnp.concatenate([d_s[:128], d_s[128:]], axis=1)
                d_q = dot_nn(both, two_heads(k, low))
                d_k = dot_tn(d_s, two_heads(q, low))
                d_v = dot_tn(p.astype(BF), d_c)
                for t, val in enumerate((d_q, d_k, d_v)):
                    dqkv[seq, :, pl.ds(512 * t + 128 * pair, 128)] = val.astype(BF)

    last = n_layers - 1
    for kind in (1, 0):
        for copy in loads(last, kind):
            copy.start()
    for c in range(NUM_CHUNKS):
        z_load(last, c, 1).start()
    ex.barrier()
    for c in range(NUM_CHUNKS):
        first_copy(c).start()
    dcur[:, pl.ds(0, 32)] = dy_in[...].astype(F32)

    @pl.loop(0, n_layers)
    def _(i):
        l = last - i

        for c in range(NUM_CHUNKS):
            @pl.when(i == 0)
            def _():
                first_copy(c).wait()
                dcur[seqs(c), pl.ds(32, 32)] = far_recv[0, seqs(c), pl.ds(0, 32)].astype(F32)

            @pl.when(i > 0)
            def _():
                d_in = ex.finish(0, c, True)
                z_load(l + 1, c, 0).wait()
                d_ln, d_gain = norm_bwd(zbuf[seqs(c)], d_in, vec[0, pl.ds(l + 1, 1), :])
                z_load(l, c, 1).start()
                dcur[seqs(c)] = dhid[seqs(c)] + d_ln
                add_row(0, l + 1, c, d_gain)
                add_row(1, l + 1, c, d_in)

            send(dcur, c, ag_m)
            add_row(5, l, c, dcur[seqs(c)])
            if c == 0:
                for copy in loads(l, 1):
                    copy.wait()
            mlp_bwd(l, c)
            for copy in save_copies(l, c, 1):
                copy.start()

            @pl.when(i > 0)
            def _():
                for copy in save_copies(l + 1, c, 0):
                    copy.wait()

            lhs = rows_of(dpre, c)
            partial_sum(ex, c, lambda cols: dot_nt(lhs, wu[cols, :]))
            ex.middle(1, c, True)

        for c in range(NUM_CHUNKS):
            d_mid = ex.finish(1, c, True)
            z_load(l, c, 1).wait()
            d_ln, d_gain = norm_bwd(zbuf[seqs(c)], d_mid, vec[2, pl.ds(l, 1), :])
            z_load(l, c, 0).start()
            dhid[seqs(c)] = dcur[seqs(c)] + d_ln
            send(dhid, c, ag_a)
            add_row(2, l, c, d_gain)
            add_row(3, l, c, d_mid)
            add_row(4, l, c, dhid[seqs(c)])
            if c == 0:
                for copy in loads(l, 0):
                    copy.wait()
            else:
                @pl.when(l > 0)
                def _():
                    for copy in loads(l - 1, 1):
                        copy.start()

            attention_bwd(c)
            for copy in save_copies(l, c, 0):
                copy.start()
            for copy in save_copies(l, c, 1):
                copy.wait()
            lhs = rows_of(dqkv, c)
            partial_sum(ex, c, lambda cols: dot_nn(lhs, wq[:, cols]))
            ex.middle(0, c, l > 0)

        @pl.when(l > 0)
        def _():
            for copy in loads(l - 1, 0):
                copy.start()

    for c in range(NUM_CHUNKS):
        z_load(0, c, 0).wait()
        for copy in save_copies(0, c, 0):
            copy.wait()
        d_in = ex.finish(0, c, False)
        d_ln, d_gain = norm_bwd(zbuf[seqs(c), pl.ds(0, 32)], d_in, vec[0, pl.ds(0, 1), :])
        dcur[seqs(c), pl.ds(0, 32)] = dhid[seqs(c), pl.ds(0, 32)] + d_ln
        dx_copy(c).start()
        for row, val in enumerate((d_gain, d_in)):
            total = row_sum(val)
            at = (0, pl.ds(row, 1))
            vlast[at] = total if c == 0 else vlast[at] + total
    copy = ex.remote(vlast.at[0], vlast.at[1], vsem.at[0, 0], vsem.at[0, 1], 2)
    copy.start()
    copy.wait()
    for row in range(2):
        vacc[row, pl.ds(0, 1)] = vlast[0, pl.ds(row, 1)] + vlast[1, pl.ds(row, 1)]
    copy = ex.remote(vacc, vfar, vsem.at[1, 0], vsem.at[1, 1], 1)
    copy.start()
    copy.wait()
    g_vec[...] = vacc[...] + vfar[...]
    for c in range(NUM_CHUNKS):
        dx_copy(c).wait()


def any_spec():
    return pl.BlockSpec(memory_space=pl.ANY)


def vmem_spec():
    return pl.BlockSpec(memory_space=pltpu.VMEM)


def run_forward(x, mask, vec, bup, wqkv, wout, wup, wdown):
    n, d = wqkv.shape[0], x.shape[-1]
    shape = jax.ShapeDtypeStruct
    dma = pltpu.SemaphoreType.DMA
    outs = [shape((4, 32, d), F32), shape((n, 4, 64, d), F32), shape((n, 4, 64, d), F32), shape((n, 4, 128, d), BF),
            shape((n, 4, 128, 1536), BF), shape((n, 4, 128, 512), BF), shape((n, 4, 4, 256, 128), F32),
            shape((n, 4, 128, d), BF), shape((n, 4, 128, d), F32), shape((n, 4, 128, d), BF)]
    return pl.pallas_call(
        forward_kernel,
        in_specs=[vmem_spec()] * 4 + [any_spec()] * 4,
        out_specs=[vmem_spec()] + [any_spec()] * 9,
        out_shape=outs,
        scratch_shapes=[pltpu.VMEM((1536, d), BF), pltpu.VMEM((512, d), BF), pltpu.VMEM((d, d), BF), pltpu.VMEM((d, d), BF),
                        pltpu.VMEM((4, 64, d), F32), pltpu.VMEM((4, 64, d), F32), pltpu.VMEM((4, 128, d), BF), pltpu.VMEM((4, 128, d), BF),
                        pltpu.VMEM((4, 128, 1536), BF), pltpu.VMEM((4, 128, 512), BF), pltpu.VMEM((4, 4, 256, 128), F32),
                        pltpu.VMEM((4, 128, d), F32), pltpu.VMEM((4, 128, d), BF), dma((4,)), dma((2, 9)), dma((2, 2)), *Exchange.scratch(d)],
        compiler_params=pltpu.CompilerParams(collective_id=0, has_side_effects=True, vmem_limit_bytes=VMEM_LIMIT),
        name='forward',
    )(x, mask, vec, bup, wqkv, wout, wup, wdown)


def run_backward(dy, vec, wqkv, wout, wup, wdown, x_s, hid_s, qkv_s, p_s, u_s):
    n, d = wqkv.shape[0], dy.shape[-1]
    shape = jax.ShapeDtypeStruct
    dma = pltpu.SemaphoreType.DMA
    outs = [shape((4, 32, d), F32), shape((n, 4, 128, d), BF), shape((n, 4, 128, d), BF), shape((n, 4, 128, d), BF),
            shape((n, 4, 128, 1536), BF), shape((n, d), F32), shape((6, n, d), F32)]
    return pl.pallas_call(
        backward_kernel,
        in_specs=[vmem_spec()] * 2 + [any_spec()] * 9,
        out_specs=[any_spec()] * 5 + [vmem_spec()] * 2,
        out_shape=outs,
        scratch_shapes=[pltpu.VMEM((1536, d), BF), pltpu.VMEM((512, d), BF), pltpu.VMEM((d, d), BF), pltpu.VMEM((d, d), BF)]
                       + [pltpu.VMEM((4, 64, d), F32)] * 3
                       + [pltpu.VMEM((4, 128, d), BF), pltpu.VMEM((4, 128, d), BF), pltpu.VMEM((4, 128, 1536), BF), pltpu.VMEM((4, 4, 256, 128), F32),
                          pltpu.VMEM((4, 128, d), F32), pltpu.VMEM((4, 128, d), BF), pltpu.VMEM((4, 128, 512), BF), pltpu.VMEM((4, 128, 1536), BF),
                          pltpu.VMEM((6, n, d), F32), pltpu.VMEM((6, n, d), F32), pltpu.VMEM((2, 2, d), F32),
                          dma((4,)), dma((3,)), dma((2,)), dma((2, 4)), dma((2, 2)), dma((2, 2)), *Exchange.scratch(d)],
        compiler_params=pltpu.CompilerParams(collective_id=1, has_side_effects=True, vmem_limit_bytes=VMEM_LIMIT),
        name='backward',
    )(dy, vec, wqkv, wout, wup, wdown, x_s, hid_s, qkv_s, p_s, u_s)


def wgrad_kernel(a, b, out):
    out[0] = dot_tn(a[0], b[0]).astype(BF)


def weight_grad(a, b):
    n, rows, m = a.shape
    width = b.shape[2]
    tm = {2048: 1024, 1536: 768, 512: 512}[m]
    return pl.pallas_call(
        wgrad_kernel,
        grid=(n, m // tm),
        in_specs=[pl.BlockSpec((1, rows, tm), lambda l, i: (l, 0, i)), pl.BlockSpec((1, rows, width), lambda l, i: (l, 0, 0))],
        out_specs=pl.BlockSpec((1, tm, width), lambda l, i: (l, i, 0)),
        out_shape=jax.ShapeDtypeStruct((n, m, width), BF),
        compiler_params=pltpu.CompilerParams(vmem_limit_bytes=VMEM_LIMIT),
        cost_estimate=pl.CostEstimate(flops=2 * n * rows * m * width, bytes_accessed=2 * n * (m * width + rows * (m + width)), transcendentals=0),
        name='weight_grad',
    )(a, b)


def group_body(x_loc, dy_loc, len_loc, wqkv_loc, wout_loc, wup_loc, bup_loc, wdown_loc, vec_loc):
    n, d = wqkv_loc.shape[0], x_loc.shape[-1]
    me = lax.axis_index(TENSOR_AXIS)
    row = jnp.arange(128, dtype=jnp.int32)
    block = (row // 32) // 2 + 2 * ((row // 32) % 2)
    pos = (block ^ me) * 32 + row % 32
    visible = (pos[None, None, :] <= pos[None, :, None]) & (pos[None, None, :] < len_loc[:, None, None])
    mask = visible.astype(F32)
    vec = vec_loc.transpose(1, 0, 2)
    wqkv = wqkv_loc.transpose(0, 2, 3, 4, 1).reshape(n, 1536, d)
    wout = wout_loc.reshape(n, 512, d)
    y, x_s, hid_s, a_s, qkv_s, ctx_s, p_s, m_s, u_s, act_s = run_forward(x_loc, mask, vec, bup_loc, wqkv, wout, wup_loc, wdown_loc)
    d_x, dmlp_s, dpre_s, dattn_s, dqkv_s, g_bup, g_vec = run_backward(dy_loc, vec, wqkv, wout, wup_loc, wdown_loc, x_s, hid_s, qkv_s, p_s, u_s)

    def tokens(val):
        return val.reshape(n, 512, val.shape[-1])

    g_qkv = weight_grad(tokens(dqkv_s), tokens(a_s)).reshape(n, 3, 8, 64, d).transpose(0, 4, 1, 2, 3)
    g_out = weight_grad(tokens(ctx_s), tokens(dattn_s)).reshape(n, 8, 64, d)
    g_up = weight_grad(tokens(m_s), tokens(dpre_s))
    g_down = weight_grad(tokens(act_s), tokens(dmlp_s))
    return y, d_x, g_qkv, g_out, g_up, g_bup, g_down, g_vec.transpose(1, 0, 2)


def solution(mesh):
    act_spec = P(PARTS_AXIS, TENSOR_AXIS, None)
    in_specs = (act_spec, act_spec, P(PARTS_AXIS), P(None, None, None, TENSOR_AXIS, None), P(None, TENSOR_AXIS, None, None), P(None, None, TENSOR_AXIS), P(None, TENSOR_AXIS), P(None, TENSOR_AXIS, None), P())
    out_specs = (act_spec, act_spec, P(PARTS_AXIS, None, None, TENSOR_AXIS, None), P(PARTS_AXIS, TENSOR_AXIS, None, None), P(PARTS_AXIS, None, TENSOR_AXIS), P(PARTS_AXIS, TENSOR_AXIS), P(PARTS_AXIS, TENSOR_AXIS, None), P(PARTS_AXIS, None, None))
    return jax.shard_map(group_body, mesh=mesh, in_specs=in_specs, out_specs=out_specs, check_vma=False)
```

time: 582 us -> 504 us (0.87)
  Pallas kernels: 560 us -> 494 us
  local copies, waits for them, and re-layouts: 20.2 us -> 7.58 us
    pallas_call x1, Pallas kernels: 249 us -> 204 us  [run_backward(): pl.pallas_call(backward_kernel, in_specs=[vmem_spec()] * 2 + [any_spec()]...]
    pallas_call x1, Pallas kernels: 224 us -> 204 us  [run_forward(): pl.pallas_call(forward_kernel, in_specs=[vmem_spec()] * 4 + [any_spec()]...]
    unnamed x30 -> x4, local copies, waits for them, and re-layouts: 20.2 us -> 7.58 us
where the time goes in v2:
time: 504 us; the launch traced here: 503 us
  Pallas kernels  494 us (98%)
  local copies, waits for them, and re-layouts  7.58 us (2%)
    pallas_call x1, Pallas kernels, run_forward(): pl.pallas_call(forward_kernel, in_specs=[vmem_spec()] * 4 + [any_spec()]...  204 us
    pallas_call x1, Pallas kernels, run_backward(): pl.pallas_call(backward_kernel, in_specs=[vmem_spec()] * 2 + [any_spec()]...  204 us
    pallas_call x4, Pallas kernels, weight_grad(): pl.pallas_call(wgrad_kernel, grid=(n, m // tm), in_specs=[pl.BlockSpec((1...  86 us

profile of v2, /device:TPU:0, one launch (start us, length us, event | category | flops | bytes accessed | tf_op | source)
XLA Modules:
  0.0 503.5 jit_solution(16712230271679356428)
XLA Ops:
  0.7 0.1 broadcast_compare_fusion
  0.7 0.7 broadcast_compare_fusion.1
  1.5 0.7 and_convert_fusion.mask
  2.2 204.0 %forward.1 = (f32[4,32,2048]{2,1,0:T(8,128)}, f32[4,4,64,2048]{3,2,1,0:T(8,128)}, f32[4,4,64,2048]{3,2,1,0:T(8,128)}, bf16[4,4,128,2048]{3,2,1,0:T(8,128)(2,1)},...) custom-call(f32[4,32,2048]{2,1,0:T(8,128)} %x_in.1, ...), custom_call_target="tpu_custom_call" | custom-call | tf_op jit(solution)/shard_map/forward/pallas_call | solution.py:475
  206.3 203.7 %backward.1 = (f32[4,32,2048]{2,1,0:T(8,128)}, bf16[4,4,128,2048]{3,2,1,0:T(8,128)(2,1)}, bf16[4,4,128,2048]{3,2,1,0:T(8,128)(2,1)}, bf16[4,4,128,2048]{3,2,1,0:...) custom-call(bf16[4,32,2048]{2,1,0:T(8,128)(2,1)} %dy_in.1, ...), custom_call_target="tpu_custom_call" | custom-call | tf_op jit(solution)/shard_map/backward/pallas_call | solution.py:495
  409.9 26.6 %weight_grad.7 = bf16[4,2048,2048]{2,1,0:T(8,128)(2,1)} custom-call(bf16[4,512,2048]{2,1,0:T(8,128)(2,1)} %bitcast.30, bf16[4,512,2048]{2,1,0:T(8,128)(2,1)} %bitcast.32), custom_call_target="tpu_custom_call" | custom-call | flops 17179869184 | bytes 50331648 | tf_op jit(solution)/shard_map/weight_grad/pallas_call | solution.py:519
  436.5 26.6 %weight_grad.6 = bf16[4,2048,2048]{2,1,0:T(8,128)(2,1)} custom-call(bf16[4,512,2048]{2,1,0:T(8,128)(2,1)} %bitcast.29, bf16[4,512,2048]{2,1,0:T(8,128)(2,1)} %bitcast.31), custom_call_target="tpu_custom_call" | custom-call | flops 17179869184 | bytes 50331648 | tf_op jit(solution)/shard_map/weight_grad/pallas_call | solution.py:519
  463.1 10.1 %weight_grad.5 = bf16[4,512,2048]{2,1,0:T(8,128)(2,1)} custom-call(bf16[4,512,512]{2,1,0:T(8,128)(2,1)} %bitcast.24, bf16[4,512,2048]{2,1,0:T(8,128)(2,1)} %bitcast.23), custom_call_target="tpu_custom_call" | custom-call | flops 4294967296 | bytes 18874368 | tf_op jit(solution)/shard_map/weight_grad/pallas_call | solution.py:519
  473.2 22.7 %weight_grad.4 = bf16[4,1536,2048]{2,1,0:T(8,128)(2,1)} custom-call(bf16[4,512,1536]{2,1,0:T(8,128)(2,1)} %bitcast.33, bf16[4,512,2048]{2,1,0:T(8,128)(2,1)} %bitcast.28), custom_call_target="tpu_custom_call" | custom-call | flops 12884901888 | bytes 39845888 | tf_op jit(solution)/shard_map/weight_grad/pallas_call | solution.py:519
  495.9 2.3 copy.21
  498.2 2.3 copy.22
  500.5 1.4 copy.23
  501.9 1.6 copy.24
  (1 shorter events, 0.0 us)

commit v3 on v2

--- a/solution.py
+++ b/solution.py
@@ -13,7 +13,7 @@
 MESH = pl.DeviceIdType.MESH
 VMEM_LIMIT = 67043328
 NUM_CHUNKS = 2
-RS_BLOCKS = 2
+RS_BLOCKS = 4
 GELU_C = 0.7978845608028654
 
 
@@ -64,12 +64,16 @@
             pl.semaphore_signal(sem, inc=1, device_id={TENSOR_AXIS: lax.bitwise_xor(self.me, flip)}, device_id_type=MESH)
         pl.semaphore_wait(sem, 2)
 
-    def gather(self, buf, c):
-        return self.remote(buf.at[seqs(c), pl.ds(0, 64)], buf.at[seqs(c), pl.ds(64, 64)], self.gs.at[c], self.gr.at[c], 1)
+    def gather(self, buf, seq):
+        return self.remote(buf.at[seq, pl.ds(0, 64)], buf.at[seq, pl.ds(64, 64)], self.gs.at[seq], self.gr.at[seq], 1)
+
+    def gather_wait(self, buf, c):
+        for s in range(2):
+            self.gather(buf, 2 * c + s).wait()
 
     def cols(self, b):
         width = self.part.shape[-1] // RS_BLOCKS
-        return pl.ds(b * width, width)
+        return pl.ds(pl.multiple_of(b * width, width), width)
 
     def core_copy(self, c, b):
         return self.remote(self.part.at[seqs(c), pl.ds(64, 64), self.cols(b)], self.from_core.at[seqs(c), :, self.cols(b)],
@@ -80,21 +84,20 @@
         return self.remote(self.far_send.at[seqs(c), rows, self.cols(b)], self.far_recv.at[kind, seqs(c), rows, self.cols(b)],
                            self.xs.at[kind, c, b], self.xr.at[kind, c, b], 2)
 
-    def middle(self, kind, c, full):
-        for b in range(RS_BLOCKS):
-            self.core_copy(c, b).wait_recv()
-            near = self.part[seqs(c), pl.ds(0, 64), self.cols(b)].astype(F32)
-            self.far_send[seqs(c), :, self.cols(b)] = (near + self.from_core[seqs(c), :, self.cols(b)].astype(F32)).astype(BF)
-            if full is True:
+    def middle(self, kind, c, b, full):
+        self.core_copy(c, b).wait_recv()
+        near = self.part[seqs(c), pl.ds(0, 64), self.cols(b)].astype(F32)
+        self.far_send[seqs(c), :, self.cols(b)] = (near + self.from_core[seqs(c), :, self.cols(b)].astype(F32)).astype(BF)
+        if isinstance(full, bool):
+            self.far_copy(kind, c, b, full).start()
+        else:
+            @pl.when(full)
+            def _():
                 self.far_copy(kind, c, b, True).start()
-            else:
-                @pl.when(full)
-                def _():
-                    self.far_copy(kind, c, b, True).start()
-
-                @pl.when(jnp.logical_not(full))
-                def _():
-                    self.far_copy(kind, c, b, False).start()
+
+            @pl.when(jnp.logical_not(full))
+            def _():
+                self.far_copy(kind, c, b, False).start()
 
     def finish(self, kind, c, full):
         for b in range(RS_BLOCKS):
@@ -112,18 +115,22 @@
     def scratch(d):
         dma = pltpu.SemaphoreType.DMA
         return [pltpu.VMEM((4, 128, d), BF), pltpu.VMEM((4, 64, d), BF), pltpu.VMEM((4, 64, d), BF), pltpu.VMEM((2, 4, 64, d), BF),
-                dma((2,)), dma((2,)), dma((2, RS_BLOCKS)), dma((2, RS_BLOCKS)), dma((2, 2, RS_BLOCKS)), dma((2, 2, RS_BLOCKS))]
-
-
-def partial_sum(ex, c, block_of, bn=512):
-    width = ex.part.shape[-1] // RS_BLOCKS
-    for b in range(RS_BLOCKS):
-        @pl.loop(0, width // bn)
-        def _(j):
-            cols = pl.ds(pl.multiple_of(b * width + j * bn, bn), bn)
-            ex.part[seqs(c), :, cols] = block_of(cols).astype(BF).reshape(2, 128, bn)
-
+                dma((4,)), dma((4,)), dma((2, RS_BLOCKS)), dma((2, RS_BLOCKS)), dma((2, 2, RS_BLOCKS)), dma((2, 2, RS_BLOCKS))]
+
+
+LAST = RS_BLOCKS - 1
+
+
+def partial_sum(ex, kind, c, full, block_of):
+    @pl.loop(0, RS_BLOCKS)
+    def _(b):
+        cols = ex.cols(b)
+        ex.part[seqs(c), :, cols] = block_of(cols).astype(BF).reshape(2, 128, -1)
         ex.core_copy(c, b).start()
+
+        @pl.when(b > 0)
+        def _():
+            ex.middle(kind, c, b - 1, full)
 
 
 def lane_low():
@@ -135,33 +142,43 @@
     return jnp.concatenate([jnp.where(low, val, zero), jnp.where(low, zero, val)], axis=0)
 
 
-def forward_kernel(x_in, mask, vec, bup, wqkv_h, wout_h, wup_h, wdown_h,
-                   y_out, x_s, hid_s, a_s, qkv_s, ctx_s, p_s, m_s, u_s, act_s,
-                   wq, wo, wu, wd, xbuf, hbuf, ag_a, ag_m, qkv, ctx, prob, u, act,
+def forward_kernel(x_in, lens, vec, bup, wqkv_h, wout_h, wup_h, wdown_h,
+                   y_out, x_s, hid_s, a_s, qkv_s, p_s, slope_s, lhs_s,
+                   wq, wo, wu, wd, xbuf, hbuf, ag_a, ag_m, qkv, ctx, prob, slope, act,
                    wsem, ssem, isem, part, from_core, far_send, far_recv, *sems):
     n_layers = wqkv_h.shape[0]
     ex = Exchange(part, from_core, far_send, far_recv, sems)
 
+    d = x_in.shape[-1]
+
+    def lhs_cols(start, width):
+        return lhs_s.at[:, :, :, pl.ds(start, width)]
+
     def weight_copies(l, kind):
         pairs = ((wqkv_h, wq, 0), (wout_h, wo, 1)) if kind == 0 else ((wup_h, wu, 2), (wdown_h, wd, 3))
         return [pltpu.make_async_copy(src.at[l], dst, wsem.at[i]) for src, dst, i in pairs]
 
     def save_copies(l, c, kind):
         if kind == 0:
-            pairs = ((xbuf, x_s, 0), (ag_a, a_s, 1), (qkv, qkv_s, 2), (ctx, ctx_s, 3), (prob, p_s, 4))
+            pairs = ((xbuf, x_s, 0), (ag_a, a_s, 1), (qkv, qkv_s, 2), (ctx, lhs_cols(2 * d, 512), 3), (prob, p_s, 4))
         else:
-            pairs = ((hbuf, hid_s, 5), (ag_m, m_s, 6), (u, u_s, 7), (act, act_s, 8))
+            pairs = ((hbuf, hid_s, 5), (ag_m, lhs_cols(0, d), 6), (slope, slope_s, 7), (act, lhs_cols(d, d), 8))
         return [pltpu.make_async_copy(src.at[seqs(c)], dst.at[l, seqs(c)], ssem.at[c, i]) for src, dst, i in pairs]
 
     def norm_and_gather(src, l, c, row, buf):
-        xhat, _ = normed(src[seqs(c)].reshape(128, -1))
-        val = xhat * vec[row, pl.ds(l, 1), :] + vec[row + 1, pl.ds(l, 1), :]
-        buf[seqs(c), pl.ds(0, 64)] = val.astype(BF).reshape(2, 64, -1)
-        ex.gather(buf, c).start()
-        ex.gather(buf, c).wait()
+        for seq in (2 * c, 2 * c + 1):
+            xhat, _ = normed(src[seq])
+            val = xhat * vec[row, pl.ds(l, 1), :] + vec[row + 1, pl.ds(l, 1), :]
+            buf[seq, pl.ds(0, 64)] = val.astype(BF)
+            ex.gather(buf, seq).start()
 
     def first_copy(c):
         return ex.remote(x_in.at[seqs(c)], xbuf.at[seqs(c), pl.ds(32, 32)], isem.at[0, c], isem.at[1, c], 2)
+
+    def position(axis):
+        i = lax.broadcasted_iota(jnp.int32, (256, 128), axis) & 127
+        block = ((i >> 6) & 1) | ((i >> 4) & 2)
+        return ((block ^ ex.me) << 5) | (i & 31)
 
     def attention(c):
         a = rows_of(ag_a, c)
@@ -173,8 +190,8 @@
         @pl.loop(0, 2)
         def _(s):
             seq = 2 * c + s
-            visible = mask[seq] > 0
-            visible = jnp.concatenate([visible, visible], axis=0)
+            key_pos, query_pos = position(1), position(0)
+            visible = (key_pos <= query_pos) & (key_pos < lens[seq])
             for pair in range(4):
                 q, k, v = (qkv[seq, :, pl.ds(512 * t + 128 * pair, 128)] for t in range(3))
                 scores = dot_nt(two_heads(q, low), k) * 0.125
@@ -193,8 +210,10 @@
         def _(j):
             cols = pl.ds(pl.multiple_of(512 * j, 512), 512)
             pre = dot_nn(m, wu[:, cols]) + bup[pl.ds(l, 1), cols]
-            u[seqs(c), :, cols] = pre.reshape(2, 128, 512)
-            t = jnp.tanh(GELU_C * (pre + 0.044715 * (pre * pre * pre)))
+            sq = pre * pre
+            t = jnp.tanh(GELU_C * (pre + 0.044715 * (sq * pre)))
+            grad = 0.5 * (1.0 + t) + 0.5 * pre * (1.0 - t * t) * (GELU_C * (1.0 + 0.134145 * sq))
+            slope[seqs(c), :, cols] = grad.reshape(2, 128, 512)
             act[seqs(c), :, cols] = (0.5 * pre * (1.0 + t)).astype(BF).reshape(2, 128, 512)
 
     for kind in range(2):
@@ -218,14 +237,20 @@
 
             norm_and_gather(xbuf, l, c, 0, ag_a)
             if c == 0:
+                @pl.when(l > 0)
+                def _():
+                    ex.middle(1, 1, LAST, True)
+
                 for copy in weight_copies(l, 0):
                     copy.wait()
+            else:
+                ex.middle(0, 0, LAST, True)
+            ex.gather_wait(ag_a, c)
             attention(c)
             for copy in save_copies(l, c, 0):
                 copy.start()
             lhs = rows_of(ctx, c)
-            partial_sum(ex, c, lambda cols: dot_nn(lhs, wo[:, cols]))
-            ex.middle(0, c, True)
+            partial_sum(ex, 0, c, True, lambda cols: dot_nn(lhs, wo[:, cols]))
 
         @pl.when(l + 1 < n_layers)
         def _():
@@ -236,16 +261,19 @@
             hbuf[seqs(c)] = xbuf[seqs(c)] + ex.finish(0, c, True) + vec[4, pl.ds(l, 1), :][None]
             norm_and_gather(hbuf, l, c, 2, ag_m)
             if c == 0:
+                ex.middle(0, 1, LAST, True)
                 for copy in weight_copies(l, 1):
                     copy.wait()
+            else:
+                ex.middle(1, 0, LAST, l + 1 < n_layers)
+            ex.gather_wait(ag_m, c)
             mlp(l, c)
             for copy in save_copies(l, c, 1):
                 copy.start()
             for copy in save_copies(l, c, 0):
                 copy.wait()
             lhs = rows_of(act, c)
-            partial_sum(ex, c, lambda cols: dot_nn(lhs, wd[:, cols]))
-            ex.middle(1, c, l + 1 < n_layers)
+            partial_sum(ex, 1, c, l + 1 < n_layers, lambda cols: dot_nn(lhs, wd[:, cols]))
 
         @pl.when(l + 1 < n_layers)
         def _():
@@ -256,13 +284,14 @@
             for copy in save_copies(l, c, 1):
                 copy.wait()
 
+    ex.middle(1, 1, LAST, False)
     for c in range(NUM_CHUNKS):
         y_out[seqs(c)] = hbuf[seqs(c), pl.ds(0, 32)] + ex.finish(1, c, False) + vec[5, pl.ds(n_layers - 1, 1), :][None]
 
 
-def backward_kernel(dy_in, vec, wqkv_h, wout_h, wup_h, wdown_h, x_s, hid_s, qkv_s, p_s, u_s,
-                    d_x, dmlp_s, dpre_s, dattn_s, dqkv_s, g_bup, g_vec,
-                    wq, wo, wu, wd, dcur, dhid, zbuf, ag_a, ag_m, qkv, prob, u, dpre, dctx, dqkv, vacc, vfar, vlast,
+def backward_kernel(dy_in, vec, wqkv_h, wout_h, wup_h, wdown_h, x_s, hid_s, qkv_s, p_s, slope_s,
+                    d_x, dqkv_s, rhs_s, g_bup, g_vec,
+                    wq, wo, wu, wd, dcur, dhid, zbuf, ag_a, ag_m, qkv, prob, slope, dpre, dctx, dqkv, vacc, vfar, vlast,
                     wsem, rsem, zsem, ssem, vsem, isem, part, from_core, far_send, far_recv, *sems):
     n_layers = wqkv_h.shape[0]
     ex = Exchange(part, from_core, far_send, far_recv, sems)
@@ -273,7 +302,7 @@
             saved = ((qkv_s, qkv, 1), (p_s, prob, 2))
         else:
             whole = ((wdown_h, wd, 3), (wup_h, wu, 2))
-            saved = ((u_s, u, 0),)
+            saved = ((slope_s, slope, 0),)
         return ([pltpu.make_async_copy(src.at[l], dst, wsem.at[i]) for src, dst, i in whole]
                 + [pltpu.make_async_copy(src.at[l], dst, rsem.at[i]) for src, dst, i in saved])
 
@@ -281,13 +310,13 @@
         return pltpu.make_async_copy((x_s, hid_s)[kind].at[l, seqs(c)], zbuf.at[seqs(c)], zsem.at[c])
 
     def save_copies(l, c, kind):
-        pairs = ((ag_a, dattn_s, 0), (dqkv, dqkv_s, 1)) if kind == 0 else ((ag_m, dmlp_s, 2), (dpre, dpre_s, 3))
+        pairs = ((ag_a, rhs_s.at[2], 0), (dqkv, dqkv_s, 1)) if kind == 0 else ((ag_m, rhs_s.at[1], 2), (dpre, rhs_s.at[0], 3))
         return [pltpu.make_async_copy(src.at[seqs(c)], dst.at[l, seqs(c)], ssem.at[c, i]) for src, dst, i in pairs]
 
     def send(src, c, buf):
-        buf[seqs(c), pl.ds(0, 64)] = src[seqs(c)].astype(BF)
-        ex.gather(buf, c).start()
-        ex.gather(buf, c).wait()
+        for seq in (2 * c, 2 * c + 1):
+            buf[seq, pl.ds(0, 64)] = src[seq].astype(BF)
+            ex.gather(buf, seq).start()
 
     def first_copy(c):
         return ex.remote(dy_in.at[seqs(c)], far_recv.at[0, seqs(c), pl.ds(0, 32)], isem.at[0, c], isem.at[1, c], 2)
@@ -320,11 +349,7 @@
         def _(j):
             cols = pl.ds(pl.multiple_of(512 * j, 512), 512)
             d_act = dot_nt(d_mlp, wd[cols, :]).astype(BF).astype(F32)
-            pre = u[seqs(c), :, cols].reshape(256, 512)
-            sq = pre * pre
-            t = jnp.tanh(GELU_C * (pre + 0.044715 * (sq * pre)))
-            slope = 0.5 * (1.0 + t) + 0.5 * pre * (1.0 - t * t) * (GELU_C * (1.0 + 0.134145 * sq))
-            d_pre = d_act * slope
+            d_pre = d_act * slope[seqs(c), :, cols].reshape(256, 512)
             total = jnp.sum(d_pre, axis=0, keepdims=True)
             g_bup[pl.ds(l, 1), cols] = total if c == 0 else g_bup[pl.ds(l, 1), cols] + total
             dpre[seqs(c), :, cols] = d_pre.astype(BF).reshape(2, 128, 512)
@@ -378,14 +403,23 @@
                 d_ln, d_gain = norm_bwd(zbuf[seqs(c)], d_in, vec[0, pl.ds(l + 1, 1), :])
                 z_load(l, c, 1).start()
                 dcur[seqs(c)] = dhid[seqs(c)] + d_ln
+                send(dcur, c, ag_m)
+                if c == 0:
+                    ex.middle(0, 1, LAST, True)
                 add_row(0, l + 1, c, d_gain)
                 add_row(1, l + 1, c, d_in)
 
-            send(dcur, c, ag_m)
+            @pl.when(i == 0)
+            def _():
+                send(dcur, c, ag_m)
+
+            if c == 1:
+                ex.middle(1, 0, LAST, True)
             add_row(5, l, c, dcur[seqs(c)])
             if c == 0:
                 for copy in loads(l, 1):
                     copy.wait()
+            ex.gather_wait(ag_m, c)
             mlp_bwd(l, c)
             for copy in save_copies(l, c, 1):
                 copy.start()
@@ -396,8 +430,7 @@
                     copy.wait()
 
             lhs = rows_of(dpre, c)
-            partial_sum(ex, c, lambda cols: dot_nt(lhs, wu[cols, :]))
-            ex.middle(1, c, True)
+            partial_sum(ex, 1, c, True, lambda cols: dot_nt(lhs, wu[cols, :]))
 
         for c in range(NUM_CHUNKS):
             d_mid = ex.finish(1, c, True)
@@ -406,6 +439,10 @@
             z_load(l, c, 0).start()
             dhid[seqs(c)] = dcur[seqs(c)] + d_ln
             send(dhid, c, ag_a)
+            if c == 0:
+                ex.middle(1, 1, LAST, True)
+            else:
+                ex.middle(0, 0, LAST, l > 0)
             add_row(2, l, c, d_gain)
             add_row(3, l, c, d_mid)
             add_row(4, l, c, dhid[seqs(c)])
@@ -418,20 +455,21 @@
                     for copy in loads(l - 1, 1):
                         copy.start()
 
+            ex.gather_wait(ag_a, c)
             attention_bwd(c)
             for copy in save_copies(l, c, 0):
                 copy.start()
             for copy in save_copies(l, c, 1):
                 copy.wait()
             lhs = rows_of(dqkv, c)
-            partial_sum(ex, c, lambda cols: dot_nn(lhs, wq[:, cols]))
-            ex.middle(0, c, l > 0)
+            partial_sum(ex, 0, c, l > 0, lambda cols: dot_nn(lhs, wq[:, cols]))
 
         @pl.when(l > 0)
         def _():
             for copy in loads(l - 1, 0):
                 copy.start()
 
+    ex.middle(0, 1, LAST, False)
     for c in range(NUM_CHUNKS):
         z_load(0, c, 0).wait()
         for copy in save_copies(0, c, 0):
@@ -465,17 +503,16 @@
     return pl.BlockSpec(memory_space=pltpu.VMEM)
 
 
-def run_forward(x, mask, vec, bup, wqkv, wout, wup, wdown):
+def run_forward(x, lens, vec, bup, wqkv, wout, wup, wdown):
     n, d = wqkv.shape[0], x.shape[-1]
     shape = jax.ShapeDtypeStruct
     dma = pltpu.SemaphoreType.DMA
     outs = [shape((4, 32, d), F32), shape((n, 4, 64, d), F32), shape((n, 4, 64, d), F32), shape((n, 4, 128, d), BF),
-            shape((n, 4, 128, 1536), BF), shape((n, 4, 128, 512), BF), shape((n, 4, 4, 256, 128), F32),
-            shape((n, 4, 128, d), BF), shape((n, 4, 128, d), F32), shape((n, 4, 128, d), BF)]
+            shape((n, 4, 128, 1536), BF), shape((n, 4, 4, 256, 128), F32), shape((n, 4, 128, d), F32), shape((n, 4, 128, 2 * d + 512), BF)]
     return pl.pallas_call(
         forward_kernel,
-        in_specs=[vmem_spec()] * 4 + [any_spec()] * 4,
-        out_specs=[vmem_spec()] + [any_spec()] * 9,
+        in_specs=[vmem_spec(), pl.BlockSpec(memory_space=pltpu.SMEM), vmem_spec(), vmem_spec()] + [any_spec()] * 4,
+        out_specs=[vmem_spec()] + [any_spec()] * 7,
         out_shape=outs,
         scratch_shapes=[pltpu.VMEM((1536, d), BF), pltpu.VMEM((512, d), BF), pltpu.VMEM((d, d), BF), pltpu.VMEM((d, d), BF),
                         pltpu.VMEM((4, 64, d), F32), pltpu.VMEM((4, 64, d), F32), pltpu.VMEM((4, 128, d), BF), pltpu.VMEM((4, 128, d), BF),
@@ -483,19 +520,18 @@
                         pltpu.VMEM((4, 128, d), F32), pltpu.VMEM((4, 128, d), BF), dma((4,)), dma((2, 9)), dma((2, 2)), *Exchange.scratch(d)],
         compiler_params=pltpu.CompilerParams(collective_id=0, has_side_effects=True, vmem_limit_bytes=VMEM_LIMIT),
         name='forward',
-    )(x, mask, vec, bup, wqkv, wout, wup, wdown)
-
-
-def run_backward(dy, vec, wqkv, wout, wup, wdown, x_s, hid_s, qkv_s, p_s, u_s):
+    )(x, lens, vec, bup, wqkv, wout, wup, wdown)
+
+
+def run_backward(dy, vec, wqkv, wout, wup, wdown, x_s, hid_s, qkv_s, p_s, slope_s):
     n, d = wqkv.shape[0], dy.shape[-1]
     shape = jax.ShapeDtypeStruct
     dma = pltpu.SemaphoreType.DMA
-    outs = [shape((4, 32, d), F32), shape((n, 4, 128, d), BF), shape((n, 4, 128, d), BF), shape((n, 4, 128, d), BF),
-            shape((n, 4, 128, 1536), BF), shape((n, d), F32), shape((6, n, d), F32)]
+    outs = [shape((4, 32, d), F32), shape((n, 4, 128, 1536), BF), shape((3, n, 4, 128, d), BF), shape((n, d), F32), shape((6, n, d), F32)]
     return pl.pallas_call(
         backward_kernel,
         in_specs=[vmem_spec()] * 2 + [any_spec()] * 9,
-        out_specs=[any_spec()] * 5 + [vmem_spec()] * 2,
+        out_specs=[any_spec()] * 3 + [vmem_spec()] * 2,
         out_shape=outs,
         scratch_shapes=[pltpu.VMEM((1536, d), BF), pltpu.VMEM((512, d), BF), pltpu.VMEM((d, d), BF), pltpu.VMEM((d, d), BF)]
                        + [pltpu.VMEM((4, 64, d), F32)] * 3
@@ -505,50 +541,101 @@
                           dma((4,)), dma((3,)), dma((2,)), dma((2, 4)), dma((2, 2)), dma((2, 2)), *Exchange.scratch(d)],
         compiler_params=pltpu.CompilerParams(collective_id=1, has_side_effects=True, vmem_limit_bytes=VMEM_LIMIT),
         name='backward',
-    )(dy, vec, wqkv, wout, wup, wdown, x_s, hid_s, qkv_s, p_s, u_s)
-
-
-def wgrad_kernel(a, b, out):
-    out[0] = dot_tn(a[0], b[0]).astype(BF)
-
-
-def weight_grad(a, b):
-    n, rows, m = a.shape
-    width = b.shape[2]
-    tm = {2048: 1024, 1536: 768, 512: 512}[m]
+    )(dy, vec, wqkv, wout, wup, wdown, x_s, hid_s, qkv_s, p_s, slope_s)
+
+
+def wgrad_kernel(lhs_f, lhs_b, rhs_f, rhs_b, g_up, g_down, g_qkv, g_out, lbuf, rbuf, obuf, lsem, rsem, osem):
+    n, rows, d = rhs_f.shape
+    kinds = ((lhs_f, 0, 1024, d // 1024, rhs_b.at[0], g_up), (lhs_f, d, 1024, d // 1024, rhs_b.at[1], g_down),
+             (lhs_b, 0, 768, lhs_b.shape[2] // 768, rhs_f, g_qkv), (lhs_f, 2 * d, 512, (lhs_f.shape[2] - 2 * d) // 512, rhs_b.at[2], g_out))
+
+    def lhs_copy(kind, s):
+        src, first, tile, per, _, _ = kinds[kind]
+        cols = pl.ds(pl.multiple_of(first + lax.rem(s, per) * tile, 128), tile)
+        slot = lax.rem(s, 2)
+        return pltpu.make_async_copy(src.at[s // per, :, cols], lbuf.at[slot, :, pl.ds(0, tile)], lsem.at[slot])
+
+    def rhs_copy(kind, l):
+        slot = lax.rem(l, 2)
+        return pltpu.make_async_copy(kinds[kind][4].at[l], rbuf.at[slot], rsem.at[slot])
+
+    def out_copy(kind, s):
+        tile, per, out = kinds[kind][2], kinds[kind][3], kinds[kind][5]
+        slot = lax.rem(s, 2)
+        at = pl.ds(pl.multiple_of(lax.rem(s, per) * tile, 128), tile)
+        return pltpu.make_async_copy(obuf.at[slot, pl.ds(0, tile)], out.at[s // per, at], osem.at[slot])
+
+    lhs_copy(0, 0).start()
+    rhs_copy(0, 0).start()
+    for kind, (_, _, tile, per, _, _) in enumerate(kinds):
+        steps = n * per
+
+        @pl.loop(0, steps)
+        def _(s):
+            @pl.when(s + 1 < steps)
+            def _():
+                lhs_copy(kind, s + 1).start()
+
+            @pl.when((lax.rem(s, per) == 0) & (s // per + 1 < n))
+            def _():
+                rhs_copy(kind, s // per + 1).start()
+
+            if kind + 1 < len(kinds):
+                @pl.when(s + 1 == steps)
+                def _():
+                    lhs_copy(kind + 1, 0).start()
+                    rhs_copy(kind + 1, 0).start()
+
+            lhs_copy(kind, s).wait()
+
+            @pl.when(lax.rem(s, per) == 0)
+            def _():
+                rhs_copy(kind, s // per).wait()
+
+            @pl.when(s >= 2)
+            def _():
+                out_copy(kind, s - 2).wait()
+
+            if kind > 0:
+                @pl.when(s < 2)
+                def _():
+                    out_copy(kind - 1, n * kinds[kind - 1][3] - 2 + s).wait()
+
+            slot = lax.rem(s, 2)
+            obuf[slot, pl.ds(0, tile)] = dot_tn(lbuf[slot, :, pl.ds(0, tile)], rbuf[lax.rem(s // per, 2)]).astype(BF)
+            out_copy(kind, s).start()
+
+    last = n * kinds[-1][3]
+    for s in (last - 2, last - 1):
+        out_copy(len(kinds) - 1, s).wait()
+
+
+def weight_grads(lhs_f, lhs_b, rhs_f, rhs_b):
+    n, rows, d = rhs_f.shape
+    widths = (d, d, lhs_b.shape[2], lhs_f.shape[2] - 2 * d)
+    dma = pltpu.SemaphoreType.DMA
     return pl.pallas_call(
         wgrad_kernel,
-        grid=(n, m // tm),
-        in_specs=[pl.BlockSpec((1, rows, tm), lambda l, i: (l, 0, i)), pl.BlockSpec((1, rows, width), lambda l, i: (l, 0, 0))],
-        out_specs=pl.BlockSpec((1, tm, width), lambda l, i: (l, i, 0)),
-        out_shape=jax.ShapeDtypeStruct((n, m, width), BF),
-        compiler_params=pltpu.CompilerParams(vmem_limit_bytes=VMEM_LIMIT),
-        cost_estimate=pl.CostEstimate(flops=2 * n * rows * m * width, bytes_accessed=2 * n * (m * width + rows * (m + width)), transcendentals=0),
-        name='weight_grad',
-    )(a, b)
+        in_specs=[any_spec()] * 4,
+        out_specs=[any_spec()] * 4,
+        out_shape=[jax.ShapeDtypeStruct((n, w, d), BF) for w in widths],
+        scratch_shapes=[pltpu.VMEM((2, rows, 1024), BF), pltpu.VMEM((2, rows, d), BF), pltpu.VMEM((2, 1024, d), BF), dma((2,)), dma((2,)), dma((2,))],
+        compiler_params=pltpu.CompilerParams(vmem_limit_bytes=52 * 1024 * 1024),
+        cost_estimate=pl.CostEstimate(flops=2 * n * rows * d * sum(widths), bytes_accessed=2 * n * d * sum(widths), transcendentals=0),
+        name='weight_grads',
+    )(lhs_f, lhs_b, rhs_f, rhs_b)
 
 
 def group_body(x_loc, dy_loc, len_loc, wqkv_loc, wout_loc, wup_loc, bup_loc, wdown_loc, vec_loc):
     n, d = wqkv_loc.shape[0], x_loc.shape[-1]
-    me = lax.axis_index(TENSOR_AXIS)
-    row = jnp.arange(128, dtype=jnp.int32)
-    block = (row // 32) // 2 + 2 * ((row // 32) % 2)
-    pos = (block ^ me) * 32 + row % 32
-    visible = (pos[None, None, :] <= pos[None, :, None]) & (pos[None, None, :] < len_loc[:, None, None])
-    mask = visible.astype(F32)
     vec = vec_loc.transpose(1, 0, 2)
     wqkv = wqkv_loc.transpose(0, 2, 3, 4, 1).reshape(n, 1536, d)
     wout = wout_loc.reshape(n, 512, d)
-    y, x_s, hid_s, a_s, qkv_s, ctx_s, p_s, m_s, u_s, act_s = run_forward(x_loc, mask, vec, bup_loc, wqkv, wout, wup_loc, wdown_loc)
-    d_x, dmlp_s, dpre_s, dattn_s, dqkv_s, g_bup, g_vec = run_backward(dy_loc, vec, wqkv, wout, wup_loc, wdown_loc, x_s, hid_s, qkv_s, p_s, u_s)
-
-    def tokens(val):
-        return val.reshape(n, 512, val.shape[-1])
-
-    g_qkv = weight_grad(tokens(dqkv_s), tokens(a_s)).reshape(n, 3, 8, 64, d).transpose(0, 4, 1, 2, 3)
-    g_out = weight_grad(tokens(ctx_s), tokens(dattn_s)).reshape(n, 8, 64, d)
-    g_up = weight_grad(tokens(m_s), tokens(dpre_s))
-    g_down = weight_grad(tokens(act_s), tokens(dmlp_s))
+    y, x_s, hid_s, a_s, qkv_s, p_s, slope_s, lhs_s = run_forward(x_loc, len_loc, vec, bup_loc, wqkv, wout, wup_loc, wdown_loc)
+    d_x, dqkv_s, rhs_s, g_bup, g_vec = run_backward(dy_loc, vec, wqkv, wout, wup_loc, wdown_loc, x_s, hid_s, qkv_s, p_s, slope_s)
+    g_up, g_down, g_qkv, g_out = weight_grads(lhs_s.reshape(n, 512, -1), dqkv_s.reshape(n, 512, -1), a_s.reshape(n, 512, d), rhs_s.reshape(3, n, 512, d))
+    g_qkv = g_qkv.reshape(n, 3, 8, 64, d).transpose(0, 4, 1, 2, 3)
+    g_out = g_out.reshape(n, 8, 64, d)
     return y, d_x, g_qkv, g_out, g_up, g_bup, g_down, g_vec.transpose(1, 0, 2)
 
 

time: 504 us -> 473 us (0.938)
  Pallas kernels: 494 us -> 469 us
    pallas_call x5 -> x2, Pallas kernels: 290 us -> 272 us  [the longest x1 204 us: run_forward(): pl.pallas_call(forward_kernel, in_specs=[vmem_spec(), pl.BlockSpec(memory...]
    pallas_call x1, Pallas kernels: 204 us -> 197 us  [run_backward(): pl.pallas_call(backward_kernel, in_specs=[vmem_spec()] * 2 + [any_spec()]...]
where the time goes in v3:
time: 473 us
  Pallas kernels  469 us (99%)
    pallas_call x1, Pallas kernels, run_forward(): pl.pallas_call(forward_kernel, in_specs=[vmem_spec(), pl.BlockSpec(memory...  204 us
    pallas_call x1, Pallas kernels, run_backward(): pl.pallas_call(backward_kernel, in_specs=[vmem_spec()] * 2 + [any_spec()]...  197 us
    pallas_call x1, Pallas kernels, weight_grads(): pl.pallas_call(wgrad_kernel, in_specs=[any_spec()] * 4, out_specs=[any_sp...  67.5 us

profile of v3, /device:TPU:0, one launch (start us, length us, event | category | flops | bytes accessed | tf_op | source)
XLA Modules:
  0.0 473.0 jit_solution(10388039094501203580)
XLA Ops:
  0.6 204.2 %forward.1 = (f32[4,32,2048]{2,1,0:T(8,128)}, f32[4,4,64,2048]{3,2,1,0:T(8,128)}, f32[4,4,64,2048]{3,2,1,0:T(8,128)}, bf16[4,4,128,2048]{3,2,1,0:T(8,128)(2,1)},...) custom-call(f32[4,32,2048]{2,1,0:T(8,128)} %x_in.1, ...), custom_call_target="tpu_custom_call" | custom-call | tf_op jit(solution)/shard_map/forward/pallas_call | solution.py:512
  204.8 197.4 %backward.1 = (f32[4,32,2048]{2,1,0:T(8,128)}, bf16[4,4,128,1536]{3,2,1,0:T(8,128)(2,1)}, bf16[3,4,4,128,2048]{4,3,2,1,0:T(8,128)(2,1)}, f32[4,2048]{1,0:T(4,128)}, f32[6,4,2048]{2,1,0:T(4,128)}) custom-call(bf16[4,32,2048]{2,1,0:T(8,128)(2,1)} %dy_in.1, f32[6,4,2048]{2,1,0:T(4,128)} %bitcast.19, bf16[4,1536,2048]{2,1,0:T(8,128)(2,1)} %bitcast.15, ...), custom_call_target="tpu_custom_call" | custom-call | tf_op jit(solution)/shard_map/backward/pallas_call | solution.py:531
  402.2 0.0 copy-start
  402.2 0.0 copy-start.1
  402.2 0.0 copy-start.3
  402.3 0.0 copy-start.2
  402.3 67.5 %weight_grads.1 = (bf16[4,2048,2048]{2,1,0:T(8,128)(2,1)}, bf16[4,2048,2048]{2,1,0:T(8,128)(2,1)}, bf16[4,1536,2048]{2,1,0:T(8,128)(2,1)}, bf16[4,512,2048]{2,1,0:T(8,128)(2,1)}) custom-call(bf16[4,512,4608]{2,1,0:T(8,128)(2,1)} %bitcast.22, bf16[4,512,1536]{2,1,0:T(8,128)(2,1)} %bitcast.24, bf16[4,512,2048]{2,1,0:T(8,128)(2,1)} %bitcast.23, ...), custom_call_target="tpu_custom_call" | custom-call | flops 51539607552 | bytes 100663296 | tf_op jit(solution)/shard_map/weight_grads/pallas_call | solution.py:617
  469.8 0.0 copy-done
  469.8 1.0 copy.21
  470.8 0.0 copy-done.1
  470.8 1.0 copy.22
  471.7 0.0 copy-done.3
  471.7 0.6 copy.23
  472.3 0.0 copy-done.2
  472.3 0.7 copy.24
Async XLA Ops:
  402.2 67.5 %copy-start = (f32[4,32,2048]{2,1,0:T(8,128)S(1)}, f32[4,32,2048]{2,1,0:T(8,128)}, u32[]{:S(2)}) copy-start(f32[4,32,2048]{2,1,0:T(8,128)} %get-tuple-element.50) | copy-start | bytes 3145732
  402.2 68.5 %copy-start.1 = (f32[4,32,2048]{2,1,0:T(8,128)S(1)}, f32[4,32,2048]{2,1,0:T(8,128)}, u32[]{:S(2)}) copy-start(f32[4,32,2048]{2,1,0:T(8,128)} %get-tuple-element.51) | copy-start | bytes 3145732
  402.2 69.5 %copy-start.3 = (f32[4,2048]{1,0:T(4,128)S(1)}, f32[4,2048]{1,0:T(4,128)}, u32[]{:S(2)}) copy-start(f32[4,2048]{1,0:T(4,128)} %get-tuple-element.55) | copy-start | bytes 98308
  402.3 70.1 %copy-start.2 = (f32[6,4,2048]{2,1,0:T(4,128)S(1)}, f32[6,4,2048]{2,1,0:T(4,128)}, u32[]{:S(2)}) copy-start(f32[6,4,2048]{2,1,0:T(4,128)} %get-tuple-element.41) | copy-start | bytes 589828

commit v4 on v3

v4 whole, which is shorter than its diff:
```python
import functools
import jax
import jax.numpy as jnp
from jax import lax
from jax.experimental import pallas as pl
from jax.experimental.pallas import tpu as pltpu
from jax.sharding import PartitionSpec as P

TENSOR_AXIS = 'tp'
PARTS_AXIS = 'dp'
BF = jnp.bfloat16
F32 = jnp.float32
MESH = pl.DeviceIdType.MESH
VMEM_LIMIT = 67043328
SEQ = 128
HALF = 64
SHARD = 32
ROWS = 256
HEADS = 512
QKV = 3 * HEADS
TILE = 1024
BATCH = 4
TOKENS = BATCH * SEQ
NUM_CHUNKS = 2
RS_BLOCKS = 4
GELU_C = 0.7978845608028654


def dot_nn(a, b):
    return lax.dot_general(a, b, (((1,), (0,)), ((), ())), preferred_element_type=F32)


def dot_nt(a, b):
    return lax.dot_general(a, b, (((1,), (1,)), ((), ())), preferred_element_type=F32)


def dot_tn(a, b):
    return lax.dot_general(a, b, (((0,), (0,)), ((), ())), preferred_element_type=F32)


def seqs(c):
    return pl.ds(2 * c, 2)


def rows_of(ref, c):
    val = ref[seqs(c)]
    return val.reshape(ROWS, val.shape[-1])


def normed(z):
    mean = jnp.mean(z, axis=-1, keepdims=True)
    centered = z - mean
    var = jnp.mean(centered * centered, axis=-1, keepdims=True)
    rstd = lax.rsqrt(var + 1e-5)
    return centered * rstd, rstd


class Exchange:
    def __init__(self, part, from_core, far_send, far_recv, sems):
        self.me = lax.axis_index(TENSOR_AXIS)
        self.part, self.from_core = part, from_core
        self.far_send, self.far_recv = far_send, far_recv
        self.gs, self.gr, self.cs, self.cr, self.xs, self.xr = sems

    def remote(self, src, dst, send, recv, flip):
        return pltpu.make_async_remote_copy(
            src_ref=src, dst_ref=dst, send_sem=send, recv_sem=recv,
            device_id={TENSOR_AXIS: lax.bitwise_xor(self.me, flip)}, device_id_type=MESH)

    def barrier(self):
        sem = pltpu.get_barrier_semaphore()
        for flip in (1, 2):
            pl.semaphore_signal(sem, inc=1, device_id={TENSOR_AXIS: lax.bitwise_xor(self.me, flip)}, device_id_type=MESH)
        pl.semaphore_wait(sem, 2)

    def gather(self, buf, seq):
        return self.remote(buf.at[seq, pl.ds(0, HALF)], buf.at[seq, pl.ds(HALF, HALF)], self.gs.at[seq], self.gr.at[seq], 1)

    def gather_wait(self, buf, c):
        for s in range(2):
            self.gather(buf, 2 * c + s).wait()

    def cols(self, b):
        width = self.part.shape[-1] // RS_BLOCKS
        return pl.ds(pl.multiple_of(b * width, width), width)

    def core_copy(self, c, b):
        return self.remote(self.part.at[seqs(c), pl.ds(HALF, HALF), self.cols(b)], self.from_core.at[seqs(c), :, self.cols(b)],
                           self.cs.at[c, b], self.cr.at[c, b], 1)

    def far_copy(self, kind, c, b, full):
        rows = pl.ds(0, HALF) if full else pl.ds(SHARD, SHARD)
        return self.remote(self.far_send.at[seqs(c), rows, self.cols(b)], self.far_recv.at[kind, seqs(c), rows, self.cols(b)],
                           self.xs.at[kind, c, b], self.xr.at[kind, c, b], 2)

    def middle(self, kind, c, b, full=True):
        self.core_copy(c, b).wait_recv()
        near = self.part[seqs(c), pl.ds(0, HALF), self.cols(b)].astype(F32)
        self.far_send[seqs(c), :, self.cols(b)] = (near + self.from_core[seqs(c), :, self.cols(b)].astype(F32)).astype(BF)
        if isinstance(full, bool):
            self.far_copy(kind, c, b, full).start()
        else:
            @pl.when(full)
            def _():
                self.far_copy(kind, c, b, True).start()

            @pl.when(jnp.logical_not(full))
            def _():
                self.far_copy(kind, c, b, False).start()

    def finish(self, kind, c, full=True):
        for b in range(RS_BLOCKS):
            self.far_copy(kind, c, b, full).wait_recv()
            self.far_copy(kind, c, b, full).wait_send()
            self.core_copy(c, b).wait_send()
        own = self.far_send[seqs(c), pl.ds(0, SHARD)].astype(F32) + self.far_recv[kind, seqs(c), pl.ds(SHARD, SHARD)].astype(F32)
        own = own.astype(BF).astype(F32)
        if not full:
            return own
        twin = self.far_send[seqs(c), pl.ds(SHARD, SHARD)].astype(F32) + self.far_recv[kind, seqs(c), pl.ds(0, SHARD)].astype(F32)
        return jnp.concatenate([own, twin.astype(BF).astype(F32)], axis=1)

    @staticmethod
    def scratch(d):
        dma = pltpu.SemaphoreType.DMA
        return [pltpu.VMEM((BATCH, SEQ, d), BF), pltpu.VMEM((BATCH, HALF, d), BF), pltpu.VMEM((BATCH, HALF, d), BF), pltpu.VMEM((2, 4, HALF, d), BF),
                dma((4,)), dma((4,)), dma((2, RS_BLOCKS)), dma((2, RS_BLOCKS)), dma((2, 2, RS_BLOCKS)), dma((2, 2, RS_BLOCKS))]


LAST = RS_BLOCKS - 1


def partial_sum(ex, kind, c, block_of, full=True):
    @pl.loop(0, RS_BLOCKS)
    def _(b):
        cols = ex.cols(b)
        ex.part[seqs(c), :, cols] = block_of(cols).astype(BF).reshape(2, SEQ, -1)
        ex.core_copy(c, b).start()

        @pl.when(b > 0)
        def _():
            ex.middle(kind, c, b - 1, full)


def lane_low():
    return lax.broadcasted_iota(jnp.int32, (SEQ, SEQ), 1) < HALF


def two_heads(val, low):
    zero = jnp.zeros_like(val)
    return jnp.concatenate([jnp.where(low, val, zero), jnp.where(low, zero, val)], axis=0)


def stack_kernel(x_in, dy_in, lens, vec, bup, wqkv_h, wout_h, wup_h, wdown_h,
                 y_out, d_x, x_s, hid_s, a_s, qkv_s, p_s, slope_s, lhs_s, dqkv_s, rhs_s, g_bup, g_vec,
                 wq, wo, wu, wd, xbuf, hbuf, dcur, ag_a, ag_m, qkv, ctx, prob, slope, act, dqkv, dyfar, vacc, vfar, vlast,
                 wsem, ssem, isem, rsem, zsem, vsem, part, from_core, far_send, far_recv, *sems):
    n_layers = wqkv_h.shape[0]
    last = n_layers - 1
    ex = Exchange(part, from_core, far_send, far_recv, sems)

    d = x_in.shape[-1]

    def lhs_cols(start, width):
        return lhs_s.at[:, :, :, pl.ds(start, width)]

    def weight_copies(l, kind):
        pairs = ((wqkv_h, wq, 0), (wout_h, wo, 1)) if kind == 0 else ((wup_h, wu, 2), (wdown_h, wd, 3))
        return [pltpu.make_async_copy(src.at[l], dst, wsem.at[i]) for src, dst, i in pairs]

    def fwd_saves(l, c, kind):
        if kind == 0:
            pairs = ((xbuf, x_s, 0), (ag_a, a_s, 1), (qkv, qkv_s, 2), (ctx, lhs_cols(2 * d, HEADS), 3), (prob, p_s, 4))
        else:
            pairs = ((hbuf, hid_s, 5), (ag_m, lhs_cols(0, d), 6), (slope, slope_s, 7), (act, lhs_cols(d, d), 8))
        return [pltpu.make_async_copy(src.at[seqs(c)], dst.at[l, seqs(c)], ssem.at[c, i]) for src, dst, i in pairs]

    def norm_and_gather(src, l, c, row, buf):
        for seq in (2 * c, 2 * c + 1):
            xhat, _ = normed(src[seq])
            val = xhat * vec[row, pl.ds(l, 1), :] + vec[row + 1, pl.ds(l, 1), :]
            buf[seq, pl.ds(0, HALF)] = val.astype(BF)
            ex.gather(buf, seq).start()

    def dy_copy(c):
        return ex.remote(dy_in.at[seqs(c)], dyfar.at[seqs(c)], isem.at[2, c], isem.at[3, c], 2)

    def first_copy(c):
        return ex.remote(xbuf.at[seqs(c), pl.ds(0, SHARD)], xbuf.at[seqs(c), pl.ds(SHARD, SHARD)], isem.at[0, c], isem.at[1, c], 2)

    def position(axis):
        i = lax.broadcasted_iota(jnp.int32, (ROWS, SEQ), axis) & 127
        block = ((i >> 6) & 1) | ((i >> 4) & 2)
        return ((block ^ ex.me) << 5) | (i & 31)

    def attention(c):
        a = rows_of(ag_a, c)
        for j in range(3):
            cols = pl.ds(HEADS * j, HEADS)
            qkv[seqs(c), :, cols] = dot_nt(a, wq[cols, :]).astype(BF).reshape(2, SEQ, HEADS)
        low = lane_low()

        @pl.loop(0, 2)
        def _(s):
            seq = 2 * c + s
            key_pos, query_pos = position(1), position(0)
            visible = (key_pos <= query_pos) & (key_pos < lens[seq])
            for pair in range(4):
                q, k, v = (qkv[seq, :, pl.ds(HEADS * t + SEQ * pair, SEQ)] for t in range(3))
                scores = dot_nt(two_heads(q, low), k) * 0.125
                scores = jnp.where(visible, scores, -1e30)
                e = jnp.exp(scores - jnp.max(scores, axis=-1, keepdims=True))
                p = e / jnp.sum(e, axis=-1, keepdims=True)
                prob[seq, pair] = p
                pb = p.astype(BF)
                both = jnp.concatenate([pb[:SEQ], pb[SEQ:]], axis=1)
                ctx[seq, :, pl.ds(SEQ * pair, SEQ)] = dot_nn(both, two_heads(v, low)).astype(BF)

    def mlp(l, c):
        m = rows_of(ag_m, c)

        @pl.loop(0, 4)
        def _(j):
            cols = pl.ds(pl.multiple_of(HEADS * j, HEADS), HEADS)
            pre = dot_nn(m, wu[:, cols]) + bup[pl.ds(l, 1), cols]
            sq = pre * pre
            t = jnp.tanh(GELU_C * (pre + 0.044715 * (sq * pre)))
            grad = 0.5 * (1.0 + t) + 0.5 * pre * (1.0 - t * t) * (GELU_C * (1.0 + 0.134145 * sq))
            slope[seqs(c), :, cols] = grad.reshape(2, SEQ, HEADS)
            act[seqs(c), :, cols] = (0.5 * pre * (1.0 + t)).astype(BF).reshape(2, SEQ, HEADS)

    def loads(l, kind):
        if kind == 0:
            whole = ((wqkv_h, wq, 0), (wout_h, wo, 1))
            saved = ((qkv_s, qkv, 1), (p_s, prob, 2))
        else:
            whole = ((wdown_h, wd, 3), (wup_h, wu, 2))
            saved = ((slope_s, slope, 0),)
        return ([pltpu.make_async_copy(src.at[l], dst, wsem.at[i]) for src, dst, i in whole]
                + [pltpu.make_async_copy(src.at[l], dst, rsem.at[i]) for src, dst, i in saved])

    def z_load(l, c, kind):
        return pltpu.make_async_copy((x_s, hid_s)[kind].at[l, seqs(c)], xbuf.at[seqs(c)], zsem.at[c])

    def bwd_saves(l, c, kind):
        pairs = ((ag_a, rhs_s.at[2], 0), (dqkv, dqkv_s, 1)) if kind == 0 else ((ag_m, rhs_s.at[1], 2), (act, rhs_s.at[0], 3))
        return [pltpu.make_async_copy(src.at[seqs(c)], dst.at[l, seqs(c)], ssem.at[c, i]) for src, dst, i in pairs]

    def send(src, c, buf):
        for seq in (2 * c, 2 * c + 1):
            buf[seq, pl.ds(0, HALF)] = src[seq].astype(BF)
            ex.gather(buf, seq).start()

    def y_copy(c):
        return pltpu.make_async_copy(hbuf.at[seqs(c), pl.ds(0, SHARD)], y_out.at[seqs(c)], isem.at[1, c])

    def dx_copy(c):
        return pltpu.make_async_copy(dcur.at[seqs(c), pl.ds(0, SHARD)], d_x.at[seqs(c)], isem.at[0, c])

    def row_sum(val):
        sums = [jnp.sum(val[:, SHARD * i:SHARD * i + SHARD].reshape(HALF, -1), axis=0, keepdims=True) for i in range(val.shape[1] // SHARD)]
        return sums[0] if len(sums) == 1 else sums[0] + sums[1]

    def add_row(i, l, c, val):
        row = (i, pl.ds(l, 1))
        total = row_sum(val)
        vacc[row] = total if c == 0 else vacc[row] + total

    def norm_bwd(z, d_z, gain):
        shape = z.shape
        z, d_z = z.reshape(-1, shape[-1]), d_z.reshape(-1, shape[-1])
        xhat, rstd = normed(z)
        g = d_z * gain
        g_mean = jnp.mean(g, axis=-1, keepdims=True)
        gx_mean = jnp.mean(g * xhat, axis=-1, keepdims=True)
        return (rstd * (g - g_mean - xhat * gx_mean)).reshape(shape), (d_z * xhat).reshape(shape)

    def mlp_bwd(l, c):
        d_mlp = rows_of(ag_m, c)

        @pl.loop(0, 4)
        def _(j):
            cols = pl.ds(pl.multiple_of(HEADS * j, HEADS), HEADS)
            d_act = dot_nt(d_mlp, wd[cols, :]).astype(BF).astype(F32)
            d_pre = d_act * slope[seqs(c), :, cols].reshape(ROWS, HEADS)
            total = jnp.sum(d_pre, axis=0, keepdims=True)
            g_bup[pl.ds(l, 1), cols] = total if c == 0 else g_bup[pl.ds(l, 1), cols] + total
            act[seqs(c), :, cols] = d_pre.astype(BF).reshape(2, SEQ, HEADS)

    def attention_bwd(c):
        ctx[seqs(c)] = dot_nt(rows_of(ag_a, c), wo[...]).astype(BF).reshape(2, SEQ, HEADS)
        low = lane_low()

        @pl.loop(0, 2)
        def _(s):
            seq = 2 * c + s
            for pair in range(4):
                q, k, v = (qkv[seq, :, pl.ds(HEADS * t + SEQ * pair, SEQ)] for t in range(3))
                d_c = two_heads(ctx[seq, :, pl.ds(SEQ * pair, SEQ)], low)
                p = prob[seq, pair]
                d_p = dot_nt(d_c, v).astype(BF).astype(F32)
                d_s = p * (d_p - jnp.sum(d_p * p, axis=-1, keepdims=True))
                d_s = (d_s * 0.125).astype(BF)
                both = jnp.concatenate([d_s[:SEQ], d_s[SEQ:]], axis=1)
                d_q = dot_nn(both, two_heads(k, low))
                d_k = dot_tn(d_s, two_heads(q, low))
                d_v = dot_tn(p.astype(BF), d_c)
                for t, val in enumerate((d_q, d_k, d_v)):
                    dqkv[seq, :, pl.ds(HEADS * t + SEQ * pair, SEQ)] = val.astype(BF)

    x_copies = [pltpu.make_async_copy(x_in.at[seqs(c)], xbuf.at[seqs(c), pl.ds(0, SHARD)], isem.at[2, c]) for c in range(NUM_CHUNKS)]
    for copy in x_copies:
        copy.start()
    for kind in range(2):
        for copy in weight_copies(0, kind):
            copy.start()
    ex.barrier()
    for c in range(NUM_CHUNKS):
        x_copies[c].wait()
        first_copy(c).start()

    @pl.loop(0, n_layers)
    def _(l):
        for c in range(NUM_CHUNKS):
            @pl.when(l == 0)
            def _():
                first_copy(c).wait()

            @pl.when(l > 0)
            def _():
                xbuf[seqs(c)] = hbuf[seqs(c)] + ex.finish(1, c) + vec[5, pl.ds(l - 1, 1), :][None]

            norm_and_gather(xbuf, l, c, 0, ag_a)
            if c == 0:
                @pl.when(l > 0)
                def _():
                    ex.middle(1, 1, LAST)

                for copy in weight_copies(l, 0):
                    copy.wait()
            else:
                ex.middle(0, 0, LAST)
            ex.gather_wait(ag_a, c)
            attention(c)
            for copy in fwd_saves(l, c, 0):
                copy.start()
            lhs = rows_of(ctx, c)
            partial_sum(ex, 0, c, lambda cols: dot_nn(lhs, wo[:, cols]))

        @pl.when(l + 1 < n_layers)
        def _():
            for copy in weight_copies(l + 1, 0):
                copy.start()

        for c in range(NUM_CHUNKS):
            hbuf[seqs(c)] = xbuf[seqs(c)] + ex.finish(0, c) + vec[4, pl.ds(l, 1), :][None]
            norm_and_gather(hbuf, l, c, 2, ag_m)
            if c == 0:
                ex.middle(0, 1, LAST)

                @pl.when(l == last)
                def _():
                    for other in range(NUM_CHUNKS):
                        dy_copy(other).start()

                for copy in weight_copies(l, 1):
                    copy.wait()
            else:
                ex.middle(1, 0, LAST, l + 1 < n_layers)
            ex.gather_wait(ag_m, c)
            mlp(l, c)
            for copy in fwd_saves(l, c, 1):
                copy.start()
            for copy in fwd_saves(l, c, 0):
                copy.wait()
            lhs = rows_of(act, c)
            if c == 1:
                for copy in fwd_saves(l, 0, 1):
                    copy.wait()
            partial_sum(ex, 1, c, lambda cols: dot_nn(lhs, wd[:, cols]), l + 1 < n_layers)

        @pl.when(l + 1 < n_layers)
        def _():
            for copy in weight_copies(l + 1, 1):
                copy.start()

        for copy in fwd_saves(l, 1, 1):
            copy.wait()

    ex.middle(1, 1, LAST, False)
    for c in range(NUM_CHUNKS):
        z_load(last, c, 1).start()
    dcur[:, pl.ds(0, SHARD)] = dy_in[...].astype(F32)

    @pl.loop(0, n_layers)
    def _(i):
        l = last - i

        for c in range(NUM_CHUNKS):
            @pl.when(i == 0)
            def _():
                dy_copy(c).wait()
                dcur[seqs(c), pl.ds(SHARD, SHARD)] = dyfar[seqs(c)].astype(F32)
                send(dcur, c, ag_m)

            @pl.when(i > 0)
            def _():
                d_in = ex.finish(1, c)
                z_load(l + 1, c, 0).wait()
                d_ln, d_gain = norm_bwd(xbuf[seqs(c)], d_in, vec[0, pl.ds(l + 1, 1), :])
                z_load(l, c, 1).start()
                dcur[seqs(c)] = hbuf[seqs(c)] + d_ln
                send(dcur, c, ag_m)
                if c == 0:
                    ex.middle(1, 1, LAST)
                add_row(0, l + 1, c, d_gain)
                add_row(1, l + 1, c, d_in)

            if c == 1:
                ex.middle(0, 0, LAST)
            add_row(5, l, c, dcur[seqs(c)])
            if c == 0:
                @pl.when(i > 0)
                def _():
                    for copy in loads(l, 1):
                        copy.wait()

            ex.gather_wait(ag_m, c)
            mlp_bwd(l, c)
            for copy in bwd_saves(l, c, 1):
                copy.start()

            @pl.when(i > 0)
            def _():
                for copy in bwd_saves(l + 1, c, 0):
                    copy.wait()

            @pl.when(i == 0)
            def _():
                own = pl.ds(0, SHARD)
                hbuf[seqs(c), own] = hbuf[seqs(c), own] + ex.finish(1, c, False) + vec[5, pl.ds(last, 1), :][None]
                y_copy(c).start()

            lhs = rows_of(act, c)
            partial_sum(ex, 0, c, lambda cols: dot_nt(lhs, wu[cols, :]))

        for c in range(NUM_CHUNKS):
            d_mid = ex.finish(0, c)
            z_load(l, c, 1).wait()
            d_ln, d_gain = norm_bwd(xbuf[seqs(c)], d_mid, vec[2, pl.ds(l, 1), :])
            z_load(l, c, 0).start()

            @pl.when(i == 0)
            def _():
                y_copy(c).wait()

            hbuf[seqs(c)] = dcur[seqs(c)] + d_ln
            send(hbuf, c, ag_a)
            if c == 0:
                ex.middle(0, 1, LAST)
            else:
                ex.middle(1, 0, LAST, l > 0)
            add_row(2, l, c, d_gain)
            add_row(3, l, c, d_mid)
            add_row(4, l, c, hbuf[seqs(c)])
            if c == 0:
                @pl.when(i > 0)
                def _():
                    for copy in loads(l, 0):
                        copy.wait()
            else:
                @pl.when(l > 0)
                def _():
                    for copy in loads(l - 1, 1):
                        copy.start()

            ex.gather_wait(ag_a, c)
            attention_bwd(c)
            for copy in bwd_saves(l, c, 0):
                copy.start()
            for copy in bwd_saves(l, c, 1):
                copy.wait()
            lhs = rows_of(dqkv, c)
            partial_sum(ex, 1, c, lambda cols: dot_nn(lhs, wq[:, cols]), l > 0)

        @pl.when(l > 0)
        def _():
            for copy in loads(l - 1, 0):
                copy.start()

    ex.middle(1, 1, LAST, False)
    for c in range(NUM_CHUNKS):
        z_load(0, c, 0).wait()
        for copy in bwd_saves(0, c, 0):
            copy.wait()
        d_in = ex.finish(1, c, False)
        d_ln, d_gain = norm_bwd(xbuf[seqs(c), pl.ds(0, SHARD)], d_in, vec[0, pl.ds(0, 1), :])
        dcur[seqs(c), pl.ds(0, SHARD)] = hbuf[seqs(c), pl.ds(0, SHARD)] + d_ln
        dx_copy(c).start()
        for row, val in enumerate((d_gain, d_in)):
            total = row_sum(val)
            at = (0, pl.ds(row, 1))
            vlast[at] = total if c == 0 else vlast[at] + total
    copy = ex.remote(vlast.at[0], vlast.at[1], vsem.at[0, 0], vsem.at[0, 1], 2)
    copy.start()
    copy.wait()
    for row in range(2):
        vacc[row, pl.ds(0, 1)] = vlast[0, pl.ds(row, 1)] + vlast[1, pl.ds(row, 1)]
    copy = ex.remote(vacc, vfar, vsem.at[1, 0], vsem.at[1, 1], 1)
    copy.start()
    copy.wait()
    g_vec[...] = vacc[...] + vfar[...]
    for c in range(NUM_CHUNKS):
        dx_copy(c).wait()


def any_spec():
    return pl.BlockSpec(memory_space=pl.ANY)


def vmem_spec():
    return pl.BlockSpec(memory_space=pltpu.VMEM)


def run_stack(x, dy, lens, vec, bup, wqkv, wout, wup, wdown):
    n, d = wqkv.shape[0], x.shape[-1]
    shape = jax.ShapeDtypeStruct
    vmem = pltpu.VMEM
    dma = pltpu.SemaphoreType.DMA
    own, held, tokens = (BATCH, SHARD, d), (BATCH, HALF, d), (BATCH, SEQ, d)
    qkv, prob = (BATCH, SEQ, QKV), (BATCH, BATCH, ROWS, SEQ)
    outs = ([shape(own, F32)] * 2 + [shape((n, *held), F32)] * 2
            + [shape((n, *tokens), BF), shape((n, *qkv), BF), shape((n, *prob), F32), shape((n, *tokens), F32), shape((n, BATCH, SEQ, 2 * d + HEADS), BF),
               shape((n, *qkv), BF), shape((3, n, *tokens), BF), shape((n, d), F32), shape((6, n, d), F32)])
    scratch = ([vmem((QKV, d), BF), vmem((HEADS, d), BF), vmem((d, d), BF), vmem((d, d), BF)] + [vmem(held, F32)] * 3 + [vmem(tokens, BF)] * 2
               + [vmem(qkv, BF), vmem((BATCH, SEQ, HEADS), BF), vmem(prob, F32), vmem(tokens, F32), vmem(tokens, BF), vmem(qkv, BF), vmem(own, BF)]
               + [vmem((6, n, d), F32)] * 2 + [vmem((2, 2, d), F32)]
               + [dma((4,)), dma((2, 9)), dma((4, 2)), dma((3,)), dma((2,)), dma((2, 2))] + Exchange.scratch(d))
    return pl.pallas_call(
        stack_kernel,
        in_specs=[any_spec(), vmem_spec(), pl.BlockSpec(memory_space=pltpu.SMEM)] + [vmem_spec()] * 2 + [any_spec()] * 4,
        out_specs=[any_spec()] * 11 + [vmem_spec()] * 2,
        out_shape=outs,
        scratch_shapes=scratch,
        compiler_params=pltpu.CompilerParams(collective_id=0, has_side_effects=True, vmem_limit_bytes=VMEM_LIMIT),
        name='stack',
    )(x, dy, lens, vec, bup, wqkv, wout, wup, wdown)


def wgrad_kernel(lhs_f, lhs_b, rhs_f, rhs_b, g_up, g_down, g_qkv, g_out, lbuf, rbuf, obuf, lsem, rsem, osem):
    n, rows, d = rhs_f.shape
    kinds = ((lhs_f, 0, TILE, d // TILE, rhs_b.at[0], g_up), (lhs_f, d, TILE, d // TILE, rhs_b.at[1], g_down),
             (lhs_b, 0, 768, lhs_b.shape[2] // 768, rhs_f, g_qkv), (lhs_f, 2 * d, HEADS, (lhs_f.shape[2] - 2 * d) // HEADS, rhs_b.at[2], g_out))

    def lhs_copy(kind, s):
        src, first, tile, per, _, _ = kinds[kind]
        cols = pl.ds(pl.multiple_of(first + lax.rem(s, per) * tile, SEQ), tile)
        slot = lax.rem(s, 2)
        return pltpu.make_async_copy(src.at[s // per, :, cols], lbuf.at[slot, :, pl.ds(0, tile)], lsem.at[slot])

    def rhs_copy(kind, l):
        slot = lax.rem(l, 2)
        return pltpu.make_async_copy(kinds[kind][4].at[l], rbuf.at[slot], rsem.at[slot])

    def out_copy(kind, s):
        tile, per, out = kinds[kind][2], kinds[kind][3], kinds[kind][5]
        slot = lax.rem(s, 2)
        at = pl.ds(pl.multiple_of(lax.rem(s, per) * tile, SEQ), tile)
        return pltpu.make_async_copy(obuf.at[slot, pl.ds(0, tile)], out.at[s // per, at], osem.at[slot])

    lhs_copy(0, 0).start()
    rhs_copy(0, 0).start()
    for kind, (_, _, tile, per, _, _) in enumerate(kinds):
        steps = n * per

        @pl.loop(0, steps)
        def _(s):
            @pl.when(s + 1 < steps)
            def _():
                lhs_copy(kind, s + 1).start()

            @pl.when((lax.rem(s, per) == 0) & (s // per + 1 < n))
            def _():
                rhs_copy(kind, s // per + 1).start()

            if kind + 1 < len(kinds):
                @pl.when(s + 1 == steps)
                def _():
                    lhs_copy(kind + 1, 0).start()
                    rhs_copy(kind + 1, 0).start()

            lhs_copy(kind, s).wait()

            @pl.when(lax.rem(s, per) == 0)
            def _():
                rhs_copy(kind, s // per).wait()

            @pl.when(s >= 2)
            def _():
                out_copy(kind, s - 2).wait()

            if kind > 0:
                @pl.when(s < 2)
                def _():
                    out_copy(kind - 1, n * kinds[kind - 1][3] - 2 + s).wait()

            slot = lax.rem(s, 2)
            obuf[slot, pl.ds(0, tile)] = dot_tn(lbuf[slot, :, pl.ds(0, tile)], rbuf[lax.rem(s // per, 2)]).astype(BF)
            out_copy(kind, s).start()

    last = n * kinds[-1][3]
    for s in (last - 2, last - 1):
        out_copy(len(kinds) - 1, s).wait()


def weight_grads(lhs_f, lhs_b, rhs_f, rhs_b):
    n, rows, d = rhs_f.shape
    widths = (d, d, lhs_b.shape[2], lhs_f.shape[2] - 2 * d)
    dma = pltpu.SemaphoreType.DMA
    return pl.pallas_call(
        wgrad_kernel,
        in_specs=[any_spec()] * 4,
        out_specs=[any_spec()] * 4,
        out_shape=[jax.ShapeDtypeStruct((n, w, d), BF) for w in widths],
        scratch_shapes=[pltpu.VMEM((2, rows, TILE), BF), pltpu.VMEM((2, rows, d), BF), pltpu.VMEM((2, TILE, d), BF), dma((2,)), dma((2,)), dma((2,))],
        compiler_params=pltpu.CompilerParams(vmem_limit_bytes=52 * 1024 * 1024),
        cost_estimate=pl.CostEstimate(flops=2 * n * rows * d * sum(widths), bytes_accessed=2 * n * d * sum(widths), transcendentals=0),
        name='weight_grads',
    )(lhs_f, lhs_b, rhs_f, rhs_b)


def group_body(x_loc, dy_loc, len_loc, wqkv_loc, wout_loc, wup_loc, bup_loc, wdown_loc, vec_loc):
    n, d = wqkv_loc.shape[0], x_loc.shape[-1]
    vec = vec_loc.transpose(1, 0, 2)
    wqkv = wqkv_loc.transpose(0, 2, 3, 4, 1).reshape(n, QKV, d)
    wout = wout_loc.reshape(n, HEADS, d)
    outs = run_stack(x_loc, dy_loc, len_loc, vec, bup_loc, wqkv, wout, wup_loc, wdown_loc)
    y, d_x, _, _, a_s, _, _, _, lhs_s, dqkv_s, rhs_s, g_bup, g_vec = outs
    g_up, g_down, g_qkv, g_out = weight_grads(lhs_s.reshape(n, TOKENS, -1), dqkv_s.reshape(n, TOKENS, -1), a_s.reshape(n, TOKENS, d), rhs_s.reshape(3, n, TOKENS, d))
    g_qkv = g_qkv.reshape(n, 3, 8, HALF, d).transpose(0, 4, 1, 2, 3)
    g_out = g_out.reshape(n, 8, HALF, d)
    return y, d_x, g_qkv, g_out, g_up, g_bup, g_down, g_vec.transpose(1, 0, 2)


def solution(mesh):
    act_spec = P(PARTS_AXIS, TENSOR_AXIS, None)
    in_specs = (act_spec, act_spec, P(PARTS_AXIS), P(None, None, None, TENSOR_AXIS, None), P(None, TENSOR_AXIS, None, None), P(None, None, TENSOR_AXIS), P(None, TENSOR_AXIS), P(None, TENSOR_AXIS, None), P())
    out_specs = (act_spec, act_spec, P(PARTS_AXIS, None, None, TENSOR_AXIS, None), P(PARTS_AXIS, TENSOR_AXIS, None, None), P(PARTS_AXIS, None, TENSOR_AXIS), P(PARTS_AXIS, TENSOR_AXIS), P(PARTS_AXIS, TENSOR_AXIS, None), P(PARTS_AXIS, None, None))
    return jax.shard_map(group_body, mesh=mesh, in_specs=in_specs, out_specs=out_specs, check_vma=False)
```

time: 473 us -> 463 us (0.979)
  Pallas kernels: 469 us -> 458 us
    pallas_call x2 -> x1, Pallas kernels: 402 us -> 391 us  [run_stack(): pl.pallas_call(stack_kernel, in_specs=[any_spec(), vmem_spec(), pl.BlockS...]
where the time goes in v4:
time: 463 us; the launch traced here: 462 us
  Pallas kernels  458 us (99%)
    pallas_call x1, Pallas kernels, run_stack(): pl.pallas_call(stack_kernel, in_specs=[any_spec(), vmem_spec(), pl.BlockS...  391 us
    pallas_call x1, Pallas kernels, weight_grads(): pl.pallas_call(wgrad_kernel, in_specs=[any_spec()] * 4, out_specs=[any_sp...  67.5 us

profile of v4, /device:TPU:0, one launch (start us, length us, event | category | flops | bytes accessed | tf_op | source)
XLA Modules:
  0.0 462.1 jit_solution(17571355929293130171)
XLA Ops:
  0.6 390.7 %stack.1 = (f32[4,32,2048]{2,1,0:T(8,128)}, f32[4,32,2048]{2,1,0:T(8,128)}, f32[4,4,64,2048]{3,2,1,0:T(8,128)}, f32[4,4,64,2048]{3,2,1,0:T(8,128)}, bf16[4,4,128...) custom-call(f32[4,32,2048]{2,1,0:T(8,128)} %x_in.1, ...), custom_call_target="tpu_custom_call" | custom-call | tf_op jit(solution)/shard_map/stack/pallas_call | solution.py:539
  391.3 0.0 copy-start.1
  391.3 0.0 copy-start
  391.3 0.0 copy-start.3
  391.3 0.0 copy-start.2
  391.3 67.5 %weight_grads.1 = (bf16[4,2048,2048]{2,1,0:T(8,128)(2,1)}, bf16[4,2048,2048]{2,1,0:T(8,128)(2,1)}, bf16[4,1536,2048]{2,1,0:T(8,128)(2,1)}, bf16[4,512,2048]{2,1,0:T(8,128)(2,1)}) custom-call(bf16[4,512,4608]{2,1,0:T(8,128)(2,1)} %bitcast.19, bf16[4,512,1536]{2,1,0:T(8,128)(2,1)} %bitcast.21, bf16[4,512,2048]{2,1,0:T(8,128)(2,1)} %bitcast.20, ...), custom_call_target="tpu_custom_call" | custom-call | flops 51539607552 | bytes 100663296 | tf_op jit(solution)/shard_map/weight_grads/pallas_call | solution.py:620
  458.9 0.0 copy-done.1
  458.9 1.0 copy.21
  459.9 0.0 copy-done
  459.9 1.0 copy.22
  460.8 0.0 copy-done.3
  460.8 0.6 copy.23
  461.4 0.0 copy-done.2
  461.4 0.7 copy.24
Async XLA Ops:
  391.3 67.6 %copy-start.1 = (f32[4,32,2048]{2,1,0:T(8,128)S(1)}, f32[4,32,2048]{2,1,0:T(8,128)}, u32[]{:S(2)}) copy-start(f32[4,32,2048]{2,1,0:T(8,128)} %get-tuple-element.40) | copy-start | bytes 3145732
  391.3 68.5 %copy-start = (f32[4,32,2048]{2,1,0:T(8,128)S(1)}, f32[4,32,2048]{2,1,0:T(8,128)}, u32[]{:S(2)}) copy-start(f32[4,32,2048]{2,1,0:T(8,128)} %get-tuple-element.41) | copy-start | bytes 3145732
  391.3 69.5 %copy-start.3 = (f32[4,2048]{1,0:T(4,128)S(1)}, f32[4,2048]{1,0:T(4,128)}, u32[]{:S(2)}) copy-start(f32[4,2048]{1,0:T(4,128)} %get-tuple-element.45) | copy-start | bytes 98308
  391.3 70.1 %copy-start.2 = (f32[6,4,2048]{2,1,0:T(4,128)S(1)}, f32[6,4,2048]{2,1,0:T(4,128)}, u32[]{:S(2)}) copy-start(f32[6,4,2048]{2,1,0:T(4,128)} %get-tuple-element.31) | copy-start | bytes 589828

commit v5 on v4

--- a/solution.py
+++ b/solution.py
@@ -547,15 +547,18 @@
     )(x, dy, lens, vec, bup, wqkv, wout, wup, wdown)
 
 
-def wgrad_kernel(lhs_f, lhs_b, rhs_f, rhs_b, g_up, g_down, g_qkv, g_out, lbuf, rbuf, obuf, lsem, rsem, osem):
+def wgrad_kernel(lhs_f, lhs_b, rhs_f, rhs_b, y_in, dx_in, bup_in, vec_in, g_up, g_down, g_qkv, g_out, y_out, dx_out, bup_out, vec_out,
+                 lbuf, rbuf, obuf, lsem, rsem, osem, small_sem, *small_buf):
+    small_in, small_out = (y_in, dx_in, bup_in, vec_in), (y_out, dx_out, bup_out, vec_out)
     n, rows, d = rhs_f.shape
     kinds = ((lhs_f, 0, TILE, d // TILE, rhs_b.at[0], g_up), (lhs_f, d, TILE, d // TILE, rhs_b.at[1], g_down),
-             (lhs_b, 0, 768, lhs_b.shape[2] // 768, rhs_f, g_qkv), (lhs_f, 2 * d, HEADS, (lhs_f.shape[2] - 2 * d) // HEADS, rhs_b.at[2], g_out))
+             (lhs_b, 0, QKV // 2, 2, rhs_f, g_qkv), (lhs_f, 2 * d, HEADS, 1, rhs_b.at[2], g_out))
+    base = [n * sum(k[3] for k in kinds[:i]) for i in range(len(kinds))]
 
     def lhs_copy(kind, s):
         src, first, tile, per, _, _ = kinds[kind]
         cols = pl.ds(pl.multiple_of(first + lax.rem(s, per) * tile, SEQ), tile)
-        slot = lax.rem(s, 2)
+        slot = lax.rem(base[kind] + s, 3)
         return pltpu.make_async_copy(src.at[s // per, :, cols], lbuf.at[slot, :, pl.ds(0, tile)], lsem.at[slot])
 
     def rhs_copy(kind, l):
@@ -568,25 +571,34 @@
         at = pl.ds(pl.multiple_of(lax.rem(s, per) * tile, SEQ), tile)
         return pltpu.make_async_copy(obuf.at[slot, pl.ds(0, tile)], out.at[s // per, at], osem.at[slot])
 
+    loads = [pltpu.make_async_copy(src, buf, small_sem.at[i]) for i, (src, buf) in enumerate(zip(small_in, small_buf))]
+    stores = [pltpu.make_async_copy(buf, dst, small_sem.at[i]) for i, (dst, buf) in enumerate(zip(small_out, small_buf))]
+    rhs_copy(0, 0).start()
     lhs_copy(0, 0).start()
-    rhs_copy(0, 0).start()
+    lhs_copy(0, 1).start()
+    for copy in loads:
+        copy.start()
     for kind, (_, _, tile, per, _, _) in enumerate(kinds):
         steps = n * per
 
         @pl.loop(0, steps)
         def _(s):
-            @pl.when(s + 1 < steps)
-            def _():
-                lhs_copy(kind, s + 1).start()
+            @pl.when(s + 2 < steps)
+            def _():
+                lhs_copy(kind, s + 2).start()
 
             @pl.when((lax.rem(s, per) == 0) & (s // per + 1 < n))
             def _():
                 rhs_copy(kind, s // per + 1).start()
 
             if kind + 1 < len(kinds):
+                @pl.when(s + 2 == steps)
+                def _():
+                    lhs_copy(kind + 1, 0).start()
+
                 @pl.when(s + 1 == steps)
                 def _():
-                    lhs_copy(kind + 1, 0).start()
+                    lhs_copy(kind + 1, 1).start()
                     rhs_copy(kind + 1, 0).start()
 
             lhs_copy(kind, s).wait()
@@ -604,29 +616,37 @@
                 def _():
                     out_copy(kind - 1, n * kinds[kind - 1][3] - 2 + s).wait()
 
-            slot = lax.rem(s, 2)
-            obuf[slot, pl.ds(0, tile)] = dot_tn(lbuf[slot, :, pl.ds(0, tile)], rbuf[lax.rem(s // per, 2)]).astype(BF)
+            lhs = lbuf[lax.rem(base[kind] + s, 3), :, pl.ds(0, tile)]
+            obuf[lax.rem(s, 2), pl.ds(0, tile)] = dot_tn(lhs, rbuf[lax.rem(s // per, 2)]).astype(BF)
             out_copy(kind, s).start()
+
+        if kind == 0:
+            for load, store in zip(loads, stores):
+                load.wait()
+                store.start()
 
     last = n * kinds[-1][3]
     for s in (last - 2, last - 1):
         out_copy(len(kinds) - 1, s).wait()
-
-
-def weight_grads(lhs_f, lhs_b, rhs_f, rhs_b):
+    for copy in stores:
+        copy.wait()
+
+
+def weight_grads(lhs_f, lhs_b, rhs_f, rhs_b, *small):
     n, rows, d = rhs_f.shape
     widths = (d, d, lhs_b.shape[2], lhs_f.shape[2] - 2 * d)
     dma = pltpu.SemaphoreType.DMA
     return pl.pallas_call(
         wgrad_kernel,
-        in_specs=[any_spec()] * 4,
-        out_specs=[any_spec()] * 4,
-        out_shape=[jax.ShapeDtypeStruct((n, w, d), BF) for w in widths],
-        scratch_shapes=[pltpu.VMEM((2, rows, TILE), BF), pltpu.VMEM((2, rows, d), BF), pltpu.VMEM((2, TILE, d), BF), dma((2,)), dma((2,)), dma((2,))],
-        compiler_params=pltpu.CompilerParams(vmem_limit_bytes=52 * 1024 * 1024),
+        in_specs=[any_spec()] * 8,
+        out_specs=[any_spec()] * 8,
+        out_shape=[jax.ShapeDtypeStruct((n, w, d), BF) for w in widths] + [jax.ShapeDtypeStruct(v.shape, v.dtype) for v in small],
+        scratch_shapes=[pltpu.VMEM((3, rows, TILE), BF), pltpu.VMEM((2, rows, d), BF), pltpu.VMEM((2, TILE, d), BF),
+                        dma((3,)), dma((2,)), dma((2,)), dma((4,))] + [pltpu.VMEM(v.shape, v.dtype) for v in small],
+        compiler_params=pltpu.CompilerParams(vmem_limit_bytes=VMEM_LIMIT),
         cost_estimate=pl.CostEstimate(flops=2 * n * rows * d * sum(widths), bytes_accessed=2 * n * d * sum(widths), transcendentals=0),
         name='weight_grads',
-    )(lhs_f, lhs_b, rhs_f, rhs_b)
+    )(lhs_f, lhs_b, rhs_f, rhs_b, *small)
 
 
 def group_body(x_loc, dy_loc, len_loc, wqkv_loc, wout_loc, wup_loc, bup_loc, wdown_loc, vec_loc):
@@ -636,7 +656,8 @@
     wout = wout_loc.reshape(n, HEADS, d)
     outs = run_stack(x_loc, dy_loc, len_loc, vec, bup_loc, wqkv, wout, wup_loc, wdown_loc)
     y, d_x, _, _, a_s, _, _, _, lhs_s, dqkv_s, rhs_s, g_bup, g_vec = outs
-    g_up, g_down, g_qkv, g_out = weight_grads(lhs_s.reshape(n, TOKENS, -1), dqkv_s.reshape(n, TOKENS, -1), a_s.reshape(n, TOKENS, d), rhs_s.reshape(3, n, TOKENS, d))
+    operands = (lhs_s.reshape(n, TOKENS, -1), dqkv_s.reshape(n, TOKENS, -1), a_s.reshape(n, TOKENS, d), rhs_s.reshape(3, n, TOKENS, d))
+    g_up, g_down, g_qkv, g_out, y, d_x, g_bup, g_vec = weight_grads(*operands, y, d_x, g_bup, g_vec)
     g_qkv = g_qkv.reshape(n, 3, 8, HALF, d).transpose(0, 4, 1, 2, 3)
     g_out = g_out.reshape(n, 8, HALF, d)
     return y, d_x, g_qkv, g_out, g_up, g_bup, g_down, g_vec.transpose(1, 0, 2)

time: 463 us -> 459 us (level)
  no operation moved by 1% of the time
where the time goes in v5:
time: 459 us
  Pallas kernels  458 us (100%)
    pallas_call x1, Pallas kernels, run_stack(): pl.pallas_call(stack_kernel, in_specs=[any_spec(), vmem_spec(), pl.BlockS...  391 us
    pallas_call x1, Pallas kernels, weight_grads(): pl.pallas_call(wgrad_kernel, in_specs=[any_spec()] * 8, out_specs=[any_sp...  67.7 us

profile of v5, /device:TPU:0, one launch (start us, length us, event | category | flops | bytes accessed | tf_op | source)
XLA Modules:
  0.0 459.2 jit_solution(12806005059855163960)
XLA Ops:
  0.6 390.7 %stack.1 = (f32[4,32,2048]{2,1,0:T(8,128)}, f32[4,32,2048]{2,1,0:T(8,128)}, f32[4,4,64,2048]{3,2,1,0:T(8,128)}, f32[4,4,64,2048]{3,2,1,0:T(8,128)}, bf16[4,4,128...) custom-call(f32[4,32,2048]{2,1,0:T(8,128)} %x_in.1, ...), custom_call_target="tpu_custom_call" | custom-call | tf_op jit(solution)/shard_map/stack/pallas_call | solution.py:539
  391.3 67.7 %weight_grads.1 = (bf16[4,2048,2048]{2,1,0:T(8,128)(2,1)}, bf16[4,2048,2048]{2,1,0:T(8,128)(2,1)}, bf16[4,1536,2048]{2,1,0:T(8,128)(2,1)}, bf16[4,512,2048]{2,1,...) custom-call(bf16[4,512,4608]{2,1,0:T(8,128)(2,1)} %bitcast.18, ...), custom_call_target="tpu_custom_call" | custom-call | flops 51539607552 | bytes 100663296 | tf_op jit(solution)/shard_map/weight_grads/pallas_call | solution.py:639

commit v6 on v5

--- a/solution.py
+++ b/solution.py
@@ -21,6 +21,7 @@
 TILE = 1024
 BATCH = 4
 TOKENS = BATCH * SEQ
+OWN = pl.ds(0, SHARD)
 NUM_CHUNKS = 2
 RS_BLOCKS = 4
 GELU_C = 0.7978845608028654
@@ -40,6 +41,10 @@
 
 def seqs(c):
     return pl.ds(2 * c, 2)
+
+
+def pair_of(c):
+    return 2 * c, 2 * c + 1
 
 
 def rows_of(ref, c):
@@ -108,17 +113,18 @@
             def _():
                 self.far_copy(kind, c, b, False).start()
 
-    def finish(self, kind, c, full=True):
-        for b in range(RS_BLOCKS):
+    def arrive(self, kind, c, full=True):
+        @pl.loop(0, RS_BLOCKS)
+        def _(b):
             self.far_copy(kind, c, b, full).wait_recv()
             self.far_copy(kind, c, b, full).wait_send()
             self.core_copy(c, b).wait_send()
-        own = self.far_send[seqs(c), pl.ds(0, SHARD)].astype(F32) + self.far_recv[kind, seqs(c), pl.ds(SHARD, SHARD)].astype(F32)
-        own = own.astype(BF).astype(F32)
-        if not full:
-            return own
-        twin = self.far_send[seqs(c), pl.ds(SHARD, SHARD)].astype(F32) + self.far_recv[kind, seqs(c), pl.ds(0, SHARD)].astype(F32)
-        return jnp.concatenate([own, twin.astype(BF).astype(F32)], axis=1)
+
+    def total(self, kind, seq, full=True):
+        own, twin = OWN, pl.ds(SHARD, SHARD)
+        pairs = ((own, twin), (twin, own)) if full else ((own, twin),)
+        sums = [self.far_send[seq, here].astype(F32) + self.far_recv[kind, seq, there].astype(F32) for here, there in pairs]
+        return jnp.concatenate([v.astype(BF).astype(F32) for v in sums], axis=0)
 
     @staticmethod
     def scratch(d):
@@ -175,8 +181,10 @@
             pairs = ((hbuf, hid_s, 5), (ag_m, lhs_cols(0, d), 6), (slope, slope_s, 7), (act, lhs_cols(d, d), 8))
         return [pltpu.make_async_copy(src.at[seqs(c)], dst.at[l, seqs(c)], ssem.at[c, i]) for src, dst, i in pairs]
 
-    def norm_and_gather(src, l, c, row, buf):
-        for seq in (2 * c, 2 * c + 1):
+    def norm_and_gather(src, l, c, row, buf, update=None):
+        for seq in pair_of(c):
+            if update is not None:
+                update(seq)
             xhat, _ = normed(src[seq])
             val = xhat * vec[row, pl.ds(l, 1), :] + vec[row + 1, pl.ds(l, 1), :]
             buf[seq, pl.ds(0, HALF)] = val.astype(BF)
@@ -186,7 +194,7 @@
         return ex.remote(dy_in.at[seqs(c)], dyfar.at[seqs(c)], isem.at[2, c], isem.at[3, c], 2)
 
     def first_copy(c):
-        return ex.remote(xbuf.at[seqs(c), pl.ds(0, SHARD)], xbuf.at[seqs(c), pl.ds(SHARD, SHARD)], isem.at[0, c], isem.at[1, c], 2)
+        return ex.remote(xbuf.at[seqs(c), OWN], xbuf.at[seqs(c), pl.ds(SHARD, SHARD)], isem.at[0, c], isem.at[1, c], 2)
 
     def position(axis):
         i = lax.broadcasted_iota(jnp.int32, (ROWS, SEQ), axis) & 127
@@ -246,16 +254,25 @@
         pairs = ((ag_a, rhs_s.at[2], 0), (dqkv, dqkv_s, 1)) if kind == 0 else ((ag_m, rhs_s.at[1], 2), (act, rhs_s.at[0], 3))
         return [pltpu.make_async_copy(src.at[seqs(c)], dst.at[l, seqs(c)], ssem.at[c, i]) for src, dst, i in pairs]
 
-    def send(src, c, buf):
-        for seq in (2 * c, 2 * c + 1):
-            buf[seq, pl.ds(0, HALF)] = src[seq].astype(BF)
-            ex.gather(buf, seq).start()
+    def send(src, seq, buf):
+        buf[seq, pl.ds(0, HALF)] = src[seq].astype(BF)
+        ex.gather(buf, seq).start()
+
+    def norm_bwd_and_send(kind, c, gain, base, dst, buf):
+        terms = []
+        for seq in pair_of(c):
+            d_z = ex.total(kind, seq)
+            d_ln, d_gain = norm_bwd(xbuf[seq], d_z, gain)
+            dst[seq] = base[seq] + d_ln
+            send(dst, seq, buf)
+            terms.append((d_gain, d_z))
+        return [jnp.stack(pair) for pair in zip(*terms)]
 
     def y_copy(c):
-        return pltpu.make_async_copy(hbuf.at[seqs(c), pl.ds(0, SHARD)], y_out.at[seqs(c)], isem.at[1, c])
+        return pltpu.make_async_copy(hbuf.at[seqs(c), OWN], y_out.at[seqs(c)], isem.at[1, c])
 
     def dx_copy(c):
-        return pltpu.make_async_copy(dcur.at[seqs(c), pl.ds(0, SHARD)], d_x.at[seqs(c)], isem.at[0, c])
+        return pltpu.make_async_copy(dcur.at[seqs(c), OWN], d_x.at[seqs(c)], isem.at[0, c])
 
     def row_sum(val):
         sums = [jnp.sum(val[:, SHARD * i:SHARD * i + SHARD].reshape(HALF, -1), axis=0, keepdims=True) for i in range(val.shape[1] // SHARD)]
@@ -308,7 +325,7 @@
                 for t, val in enumerate((d_q, d_k, d_v)):
                     dqkv[seq, :, pl.ds(HEADS * t + SEQ * pair, SEQ)] = val.astype(BF)
 
-    x_copies = [pltpu.make_async_copy(x_in.at[seqs(c)], xbuf.at[seqs(c), pl.ds(0, SHARD)], isem.at[2, c]) for c in range(NUM_CHUNKS)]
+    x_copies = [pltpu.make_async_copy(x_in.at[seqs(c)], xbuf.at[seqs(c), OWN], isem.at[2, c]) for c in range(NUM_CHUNKS)]
     for copy in x_copies:
         copy.start()
     for kind in range(2):
@@ -325,12 +342,16 @@
             @pl.when(l == 0)
             def _():
                 first_copy(c).wait()
+                norm_and_gather(xbuf, l, c, 0, ag_a)
 
             @pl.when(l > 0)
             def _():
-                xbuf[seqs(c)] = hbuf[seqs(c)] + ex.finish(1, c) + vec[5, pl.ds(l - 1, 1), :][None]
-
-            norm_and_gather(xbuf, l, c, 0, ag_a)
+                def update(seq):
+                    xbuf[seq] = hbuf[seq] + ex.total(1, seq) + vec[5, pl.ds(l - 1, 1), :]
+
+                ex.arrive(1, c)
+                norm_and_gather(xbuf, l, c, 0, ag_a, update)
+
             if c == 0:
                 @pl.when(l > 0)
                 def _():
@@ -353,8 +374,11 @@
                 copy.start()
 
         for c in range(NUM_CHUNKS):
-            hbuf[seqs(c)] = xbuf[seqs(c)] + ex.finish(0, c) + vec[4, pl.ds(l, 1), :][None]
-            norm_and_gather(hbuf, l, c, 2, ag_m)
+            def update(seq):
+                hbuf[seq] = xbuf[seq] + ex.total(0, seq) + vec[4, pl.ds(l, 1), :]
+
+            ex.arrive(0, c)
+            norm_and_gather(hbuf, l, c, 2, ag_m, update)
             if c == 0:
                 ex.middle(0, 1, LAST)
 
@@ -390,7 +414,7 @@
     ex.middle(1, 1, LAST, False)
     for c in range(NUM_CHUNKS):
         z_load(last, c, 1).start()
-    dcur[:, pl.ds(0, SHARD)] = dy_in[...].astype(F32)
+    dcur[:, OWN] = dy_in[...].astype(F32)
 
     @pl.loop(0, n_layers)
     def _(i):
@@ -401,16 +425,15 @@
             def _():
                 dy_copy(c).wait()
                 dcur[seqs(c), pl.ds(SHARD, SHARD)] = dyfar[seqs(c)].astype(F32)
-                send(dcur, c, ag_m)
+                for seq in pair_of(c):
+                    send(dcur, seq, ag_m)
 
             @pl.when(i > 0)
             def _():
-                d_in = ex.finish(1, c)
+                ex.arrive(1, c)
                 z_load(l + 1, c, 0).wait()
-                d_ln, d_gain = norm_bwd(xbuf[seqs(c)], d_in, vec[0, pl.ds(l + 1, 1), :])
+                d_gain, d_in = norm_bwd_and_send(1, c, vec[0, pl.ds(l + 1, 1), :], hbuf, dcur, ag_m)
                 z_load(l, c, 1).start()
-                dcur[seqs(c)] = hbuf[seqs(c)] + d_ln
-                send(dcur, c, ag_m)
                 if c == 0:
                     ex.middle(1, 1, LAST)
                 add_row(0, l + 1, c, d_gain)
@@ -437,25 +460,24 @@
 
             @pl.when(i == 0)
             def _():
-                own = pl.ds(0, SHARD)
-                hbuf[seqs(c), own] = hbuf[seqs(c), own] + ex.finish(1, c, False) + vec[5, pl.ds(last, 1), :][None]
+                own = OWN
+                ex.arrive(1, c, False)
+                for seq in pair_of(c):
+                    hbuf[seq, own] = hbuf[seq, own] + ex.total(1, seq, False) + vec[5, pl.ds(last, 1), :]
                 y_copy(c).start()
 
             lhs = rows_of(act, c)
             partial_sum(ex, 0, c, lambda cols: dot_nt(lhs, wu[cols, :]))
 
         for c in range(NUM_CHUNKS):
-            d_mid = ex.finish(0, c)
+            @pl.when(i == 0)
+            def _():
+                y_copy(c).wait()
+
+            ex.arrive(0, c)
             z_load(l, c, 1).wait()
-            d_ln, d_gain = norm_bwd(xbuf[seqs(c)], d_mid, vec[2, pl.ds(l, 1), :])
+            d_gain, d_mid = norm_bwd_and_send(0, c, vec[2, pl.ds(l, 1), :], dcur, hbuf, ag_a)
             z_load(l, c, 0).start()
-
-            @pl.when(i == 0)
-            def _():
-                y_copy(c).wait()
-
-            hbuf[seqs(c)] = dcur[seqs(c)] + d_ln
-            send(hbuf, c, ag_a)
             if c == 0:
                 ex.middle(0, 1, LAST)
             else:
@@ -493,9 +515,10 @@
         z_load(0, c, 0).wait()
         for copy in bwd_saves(0, c, 0):
             copy.wait()
-        d_in = ex.finish(1, c, False)
-        d_ln, d_gain = norm_bwd(xbuf[seqs(c), pl.ds(0, SHARD)], d_in, vec[0, pl.ds(0, 1), :])
-        dcur[seqs(c), pl.ds(0, SHARD)] = hbuf[seqs(c), pl.ds(0, SHARD)] + d_ln
+        ex.arrive(1, c, False)
+        d_in = jnp.stack([ex.total(1, seq, False) for seq in pair_of(c)])
+        d_ln, d_gain = norm_bwd(xbuf[seqs(c), OWN], d_in, vec[0, pl.ds(0, 1), :])
+        dcur[seqs(c), OWN] = hbuf[seqs(c), OWN] + d_ln
         dx_copy(c).start()
         for row, val in enumerate((d_gain, d_in)):
             total = row_sum(val)

time: 459 us -> 459 us (level)
  no operation moved by 1% of the time
where the time goes in v6:
time: 459 us
  Pallas kernels  458 us (100%)
    pallas_call x1, Pallas kernels, run_stack(): pl.pallas_call(stack_kernel, in_specs=[any_spec(), vmem_spec(), pl.BlockS...  390 us
    pallas_call x1, Pallas kernels, weight_grads(): pl.pallas_call(wgrad_kernel, in_specs=[any_spec()] * 8, out_specs=[any_sp...  67.7 us

profile of v6, /device:TPU:0, one launch (start us, length us, event | category | flops | bytes accessed | tf_op | source)
XLA Modules:
  0.0 458.8 jit_solution(12151778467107918736)
XLA Ops:
  0.6 390.3 %stack.1 = (f32[4,32,2048]{2,1,0:T(8,128)}, f32[4,32,2048]{2,1,0:T(8,128)}, f32[4,4,64,2048]{3,2,1,0:T(8,128)}, f32[4,4,64,2048]{3,2,1,0:T(8,128)}, bf16[4,4,128...) custom-call(f32[4,32,2048]{2,1,0:T(8,128)} %x_in.1, ...), custom_call_target="tpu_custom_call" | custom-call | tf_op jit(solution)/shard_map/stack/pallas_call | solution.py:562
  390.9 67.7 %weight_grads.1 = (bf16[4,2048,2048]{2,1,0:T(8,128)(2,1)}, bf16[4,2048,2048]{2,1,0:T(8,128)(2,1)}, bf16[4,1536,2048]{2,1,0:T(8,128)(2,1)}, bf16[4,512,2048]{2,1,...) custom-call(bf16[4,512,4608]{2,1,0:T(8,128)(2,1)} %bitcast.18, ...), custom_call_target="tpu_custom_call" | custom-call | flops 51539607552 | bytes 100663296 | tf_op jit(solution)/shard_map/weight_grads/pallas_call | solution.py:662
